TPU v7x, 256 devices: a whole 4x4x8 slice. The times are simulated.
256 devices in a mesh: col: 64 (over y, z, core), lev: 4 (over x).
Axes of the slice: x: 4, y: 4, z: 8, core: 2. Of those that a mesh axis runs over, the one named last changes fastest.
Arguments:
- state_anom: bfloat16 [48, 64, 65536], P('lev', None, 'col'), may hold values from -6 to 6
- error_sum: float32 [48, 65536], P('lev', 'col'), may hold values from -3 to 3
- obs_anom: bfloat16 [64, 131072], P('lev', 'col'), may hold values from -6 to 6
- local_weight: float32 [32, 131072], P(None, 'col'), may hold values from 0.05 to 1
- neighbours: int32 [32, 131072], P(None, 'col'), may hold values from 0 to 3071, as said below
- innovation: float32 [131072], P(('col', 'lev')), may hold values from -6 to 6
- obs_type: int32 [131072], P(('col', 'lev')), may hold values from 0 to 31
- live: int32 [131072], P(('col', 'lev')), may hold values 0 or 1
Outputs:
- impact: float32 [131072], P(('col', 'lev'))
- type_impact: float32 [32], replicated
Inputs may be any that keep to these rules, and one draw needn't show every extreme that they name: Observation o lies in column tile o // 2048; the column (o // 2048 - 1) * 1024 + neighbours[n, o] lies in that tile or the tile on either side of it, inside the grid.
All inputs are finite; a program needn't handle non-finite values. No bound on the sum of `live` on one device may be relied on, other than what follows from the above.
Results may differ from a plain program's by a relative error of at most 0.0003.
Values may be sent and summed in bfloat16 or wider, within the bound.
No kernel may reach another device: no remote copies, remote signals or barrier semaphores. Data moves between devices by JAX's collectives and lax.ppermute only.
A program may use at most 64 MiB of HBM per device.

v0:
```python
import functools
import math

import jax
import jax.numpy as jnp
from jax import lax
from jax.sharding import Mesh
from jax.sharding import PartitionSpec as P

MEMBERS = 64
NTYPE = 32
COL = ("col_0", "col_1", "col_2")
COL_LEV = ("col_0", "col_1", "col_2", "lev")


def in_blocks(x, dim, length):
    dims = x.shape
    blocks = x.reshape(*dims[:dim], length, dims[dim] // length, *dims[dim + 1 :])
    return jnp.moveaxis(blocks, dim, 0)


def summed_on_arrival(x, axis, dim):
    length = lax.axis_size(axis)
    blocks = lax.all_to_all(in_blocks(x, dim, length), axis, 0, 0, tiled=True)
    return jnp.sum(blocks, axis=0)


def with_halo(cells, sides, width):
    for axis, dim in sides:
        count = lax.axis_size(axis)
        ends = count - 1
        head = lax.slice_in_dim(cells, 0, width, axis=dim)
        tail = lax.slice_in_dim(cells, cells.shape[dim] - width, cells.shape[dim], axis=dim)
        cells = jnp.concatenate(
            [
                lax.ppermute(tail, axis, [(i, (i + 1) % count) for i in range(ends)]),
                cells,
                lax.ppermute(head, axis, [((i + 1) % count, i) for i in range(ends)]),
            ],
            axis=dim,
        )
    return cells


def by_axis(x, axes):
    return functools.reduce(lax.psum, axes, x)


def block_pairs(extended, anom, weight, index):
    span = extended.shape[1]
    column_ids = lax.broadcasted_iota(jnp.int32, (span, index.shape[1]), 0)
    table = jnp.sum(
        jnp.where(index[:, None, :] == column_ids[None, :, :], weight[:, None, :], 0.0), axis=0
    )
    spread = jnp.dot(
        extended, table, precision=lax.Precision.HIGHEST, preferred_element_type=jnp.float32
    )
    return jnp.sum(anom.astype(jnp.float32) * spread, axis=0)


def shards(state_anom, error_sum, obs_anom, local_weight, neighbours, innovation, obs_type, live):
    columns = state_anom.shape[2]
    partial_sens = jnp.einsum(
        "lkc,lc->kc", state_anom.astype(jnp.float32), error_sum, precision=lax.Precision.HIGHEST
    )
    sens = summed_on_arrival(partial_sens, "lev", 0)
    extended = with_halo(sens, ((COL, 1),), columns)
    obs_slots = obs_anom.shape[1]
    step_rows = math.gcd(obs_slots, 512)
    count = obs_slots // step_rows
    groups = obs_anom.shape[0]
    anom_blocks = jnp.transpose(obs_anom.reshape(groups, count, step_rows), (1, 0, 2))
    weight_blocks = jnp.transpose(
        local_weight.reshape(local_weight.shape[0], count, step_rows), (1, 0, 2)
    )
    index_blocks = jnp.transpose(
        neighbours.reshape(neighbours.shape[0], count, step_rows), (1, 0, 2)
    )

    def one_block(items):
        return block_pairs(extended, items[0], items[1], items[2])

    partial_pair = lax.map(one_block, (anom_blocks, weight_blocks, index_blocks)).reshape(obs_slots)
    pair = summed_on_arrival(partial_pair, "lev", 0)
    impact = pair * innovation * live.astype(jnp.float32) / (MEMBERS - 1.0)
    onehot = (obs_type[None, :] == jnp.arange(NTYPE, dtype=jnp.int32)[:, None]).astype(jnp.float32)
    type_part = jnp.sum(onehot * impact[None, :], axis=1)
    type_impact = by_axis(type_part, COL_LEV)
    return (impact, type_impact)


def solution(mesh):
    split = Mesh(
        mesh.devices.reshape(4, 8, 2, mesh.shape["lev"]), ("col_0", "col_1", "col_2", "lev")
    )
    return jax.shard_map(
        shards,
        mesh=split,
        in_specs=(
            P("lev", None, COL),
            P("lev", COL),
            P("lev", COL),
            P(None, COL),
            P(None, COL),
            P(COL_LEV),
            P(COL_LEV),
            P(COL_LEV),
        ),
        out_specs=(P(COL_LEV), P()),
        check_vma=False,
    )
```

profile of v0, /device:TPU:1, one launch (start us, length us, event | category | flops | bytes accessed | tf_op | source)
XLA Modules:
  0.0 217.9 jit_solution(12510541475392437061)
XLA Ops:
  0.6 1.8 multiply_reduce_fusion
  2.4 10.2 %all_to_all.14 = f32[4,16,1024]{2,1,0:T(8,128)S(1)} all-to-all(f32[4,16,1024]{2,1,0:T(8,128)S(1)} %bitcast.45), channel_id=1, replica_groups=mesh['col_0'=4,'col_1'=8,'col_2'=2,'lev'=4] {'lev'}, dimensions={0} | all-to-all | bytes 524288 | tf_op jit(solution)/shard_map/all_to_all | solution.py:24
  12.6 5.5 %collective-permute-start = (f32[16,1024]{1,0:T(8,128)S(1)}, f32[16,1024]{1,0:T(8,128)S(1)}, u32[]{:S(2)}, u32[]{:S(2)}) collective-permute-start(f32[16,1024]{1,0:T(8,128)S(1)} %reduce_sum.45), channel_id=1, source_target_pairs={{0,4},{4,8},{8,12},{12,16},{16,20},{20,24},{24,28},{28,32},{32,36}... | collective-permute-start | bytes 196616 | tf_op jit(solution)/shard_map/ppermute | solution.py:36
  18.2 1.9 collective-permute-start.1
  20.1 1.1 reshape.27
  21.2 1.1 reshape.28
  22.4 0.9 reshape.26
  23.3 0.0 collective-permute-done
  23.3 0.5 collective-permute-done.1
  23.8 0.0 copy-start.2
  23.8 0.0 copy-start.3
  23.8 0.0 copy-start.1
  23.8 146.3 %while.10 = (s32[]{:T(128)}, f32[4,512]{1,0:T(4,128)S(1)}, bf16[4,16,512]{2,1,0:T(8,128)(2,1)S(1)}, s32[4,32,512]{2,0,1:T(4,128)S(1)}, f32[4,32,512]{2,0,1:T(4,1...) while((s32[]{:T(128)}, f32[4,512]{1,0:T(4,128)S(1)}, bf16[4,16,512]{2,1,0:T(8,128)(2,1)S(1)}, ...), condition=%wide.region_4.5_spmd, body=%wide.region_1.4_spmd.sunk | while | flops 451436032 | bytes 13457509 | solution.py:83
  23.8 0.1 constant_dynamic-slice_fusion.4
  23.9 0.1 constant_dynamic-slice_fusion.5
  24.0 30.9 %select_reduce_fusion.3 = f32[3072,512]{1,0:T(8,128)} fusion(f32[32,512]{1,0:T(8,128)S(1)} %bitcast.41, s32[32,512]{1,0:T(8,128)S(1)} %bitcast.42), kind=kLoop, calls=%fused_computation.clone.1 | loop fusion | flops 149422080 | bytes 6422528 | tf_op jit(solution)/shard_map/while/body/eval_jaxpr/reduce_sum | solution.py:52
  54.9 5.4 %fusion.9 = f32[512]{0:T(512)S(1)} fusion(f32[3072,512]{1,0:T(8,128)} %select_reduce_fusion.3, f32[16,3072]{1,0:T(8,128)S(1)} %get-tuple-element.123, bf16[4,16,512]{2,1,0:T(8,128)(2,1)S(1)} %get-tuple-element.120, s32[]{:T(128)} %get-tuple-element.110), kind=kOutput, calls=%fused_computation.4.clone.1 | convolution fusion | flops 302013952 | bytes 6506500 | tf_op jit(solution)/shard_map/while/body/eval_jaxpr/dot_general | solution.py:55
  60.3 0.1 dynamic_update_slice.5
  60.4 0.1 constant_dynamic-slice_fusion.4
  60.5 0.1 constant_dynamic-slice_fusion.5
  60.5 30.9 %select_reduce_fusion.3 = f32[3072,512]{1,0:T(8,128)} fusion(f32[32,512]{1,0:T(8,128)S(1)} %bitcast.41, s32[32,512]{1,0:T(8,128)S(1)} %bitcast.42), kind=kLoop, calls=%fused_computation.clone.1 | loop fusion | flops 149422080 | bytes 6422528 | tf_op jit(solution)/shard_map/while/body/eval_jaxpr/reduce_sum | solution.py:52
  91.5 5.4 %fusion.9 = f32[512]{0:T(512)S(1)} fusion(f32[3072,512]{1,0:T(8,128)} %select_reduce_fusion.3, f32[16,3072]{1,0:T(8,128)S(1)} %get-tuple-element.123, bf16[4,16,512]{2,1,0:T(8,128)(2,1)S(1)} %get-tuple-element.120, s32[]{:T(128)} %get-tuple-element.110), kind=kOutput, calls=%fused_computation.4.clone.1 | convolution fusion | flops 302013952 | bytes 6506500 | tf_op jit(solution)/shard_map/while/body/eval_jaxpr/dot_general | solution.py:55
  96.9 0.1 dynamic_update_slice.5
  97.0 0.1 constant_dynamic-slice_fusion.4
  97.0 0.1 constant_dynamic-slice_fusion.5
  97.1 30.9 %select_reduce_fusion.3 = f32[3072,512]{1,0:T(8,128)} fusion(f32[32,512]{1,0:T(8,128)S(1)} %bitcast.41, s32[32,512]{1,0:T(8,128)S(1)} %bitcast.42), kind=kLoop, calls=%fused_computation.clone.1 | loop fusion | flops 149422080 | bytes 6422528 | tf_op jit(solution)/shard_map/while/body/eval_jaxpr/reduce_sum | solution.py:52
  128.0 5.4 %fusion.9 = f32[512]{0:T(512)S(1)} fusion(f32[3072,512]{1,0:T(8,128)} %select_reduce_fusion.3, f32[16,3072]{1,0:T(8,128)S(1)} %get-tuple-element.123, bf16[4,16,512]{2,1,0:T(8,128)(2,1)S(1)} %get-tuple-element.120, s32[]{:T(128)} %get-tuple-element.110), kind=kOutput, calls=%fused_computation.4.clone.1 | convolution fusion | flops 302013952 | bytes 6506500 | tf_op jit(solution)/shard_map/while/body/eval_jaxpr/dot_general | solution.py:55
  133.5 0.1 dynamic_update_slice.5
  133.5 0.1 constant_dynamic-slice_fusion.4
  133.6 0.1 constant_dynamic-slice_fusion.5
  133.7 30.9 %select_reduce_fusion.3 = f32[3072,512]{1,0:T(8,128)} fusion(f32[32,512]{1,0:T(8,128)S(1)} %bitcast.41, s32[32,512]{1,0:T(8,128)S(1)} %bitcast.42), kind=kLoop, calls=%fused_computation.clone.1 | loop fusion | flops 149422080 | bytes 6422528 | tf_op jit(solution)/shard_map/while/body/eval_jaxpr/reduce_sum | solution.py:52
  164.6 5.4 %fusion.9 = f32[512]{0:T(512)S(1)} fusion(f32[3072,512]{1,0:T(8,128)} %select_reduce_fusion.3, f32[16,3072]{1,0:T(8,128)S(1)} %get-tuple-element.123, bf16[4,16,512]{2,1,0:T(8,128)(2,1)S(1)} %get-tuple-element.120, s32[]{:T(128)} %get-tuple-element.110), kind=kOutput, calls=%fused_computation.4.clone.1 | convolution fusion | flops 302013952 | bytes 6506500 | tf_op jit(solution)/shard_map/while/body/eval_jaxpr/dot_general | solution.py:55
  170.0 0.1 dynamic_update_slice.5
  170.1 6.5 %all_to_all.15 = f32[4,1,512]{2,1,0:T(1,128)S(1)} all-to-all(f32[4,1,512]{2,1,0:T(1,128)S(1)} %all_to_all.10), channel_id=1, replica_groups=mesh['col_0'=4,'col_1'=8,'col_2'=2,'lev'=4] {'lev'}, dimensions={0} | all-to-all | bytes 16384 | tf_op jit(solution)/shard_map/all_to_all | solution.py:24
  176.6 0.0 copy-done.2
  176.6 0.0 copy-done.3
  176.7 0.0 copy-done.1
  176.7 0.0 copy-start
  176.7 0.1 select_reduce_fusion.1
  176.8 8.7 %psum.28 = f32[32]{0:T(128)S(1)} all-reduce(f32[32]{0:T(128)S(1)} %select_reduce_fusion.1), channel_id=1, replica_groups=mesh['col_0'=4,'col_1'=8,'col_2'=2,'lev'=4] {'col_0'}, use_global_device_ids=true, to_apply=%region_7.8 | all-reduce | flops 32 | bytes 256 | tf_op jit(solution)/shard_map/psum | solution.py:46
  185.5 15.4 %psum.29 = f32[32]{0:T(128)S(1)} all-reduce(f32[32]{0:T(128)S(1)} %psum.28), channel_id=1, replica_groups=mesh['col_0'=4,'col_1'=8,'col_2'=2,'lev'=4] {'col_1'}, use_global_device_ids=true, to_apply=%region_8.9 | all-reduce | flops 32 | bytes 256 | tf_op jit(solution)/shard_map/psum | solution.py:46
  200.9 9.6 %psum.30 = f32[32]{0:T(128)S(1)} all-reduce(f32[32]{0:T(128)S(1)} %psum.29), channel_id=1, replica_groups=mesh['col_0'=4,'col_1'=8,'col_2'=2,'lev'=4] {'col_2'}, use_global_device_ids=true, to_apply=%region_9.10 | all-reduce | flops 32 | bytes 256 | tf_op jit(solution)/shard_map/psum | solution.py:46
  210.5 7.3 %psum.31 = f32[32]{0:T(128)} all-reduce(f32[32]{0:T(128)S(1)} %psum.30), channel_id=1, replica_groups=mesh['col_0'=4,'col_1'=8,'col_2'=2,'lev'=4] {'lev'}, use_global_device_ids=true, to_apply=%region_10.11 | all-reduce | flops 32 | bytes 256 | tf_op jit(solution)/shard_map/psum | solution.py:46
  217.9 0.0 copy-done
  (15 shorter events, 0.1 us)
Async XLA Ops:
  12.6 10.6 %collective-permute-start = (f32[16,1024]{1,0:T(8,128)S(1)}, f32[16,1024]{1,0:T(8,128)S(1)}, u32[]{:S(2)}, u32[]{:S(2)}) collective-permute-start(f32[16,1024]{1,0:T(8,128)S(1)} %reduce_sum.45), channel_id=1, source_target_pairs={{0,4},{4,8},{8,12},{12,16},{16,20},{20,24},{24,28},{28,32},{32,36}... | collective-permute-start | bytes 196616 | tf_op jit(solution)/shard_map/ppermute | solution.py:36
  18.2 5.6 %collective-permute-start.1 = (f32[16,1024]{1,0:T(8,128)S(1)}, f32[16,1024]{1,0:T(8,128)S(1)}, u32[]{:S(2)}, u32[]{:S(2)}) collective-permute-start(f32[16,1024]{1,0:T(8,128)S(1)} %reduce_sum.45), channel_id=1, source_target_pairs={{4,0},{8,4},{12,8},{16,12},{20,16},{24,20},{28,24},{32,28},{36,32}... | collective-permute-start | bytes 196616 | tf_op jit(solution)/shard_map/ppermute | solution.py:38
  23.8 152.9 %copy-start.2 = (s32[512]{0:T(512)S(1)}, s32[512]{0:T(512)}, u32[]{:S(2)}) copy-start(s32[512]{0:T(512)} %param.17) | copy-start | bytes 6148
  23.8 152.9 %copy-start.3 = (f32[512]{0:T(512)S(1)}, f32[512]{0:T(512)}, u32[]{:S(2)}) copy-start(f32[512]{0:T(512)} %param.15) | copy-start | bytes 6148
  23.8 152.9 %copy-start.1 = (s32[512]{0:T(512)S(1)}, s32[512]{0:T(512)}, u32[]{:S(2)}) copy-start(s32[512]{0:T(512)} %param.16) | copy-start | bytes 6148
  176.7 41.2 %copy-start = (f32[512]{0:T(512)}, f32[512]{0:T(512)S(1)}, u32[]{:S(2)}) copy-start(f32[512]{0:T(512)S(1)} %multiply_multiply_fusion) | copy-start | bytes 6148
where the time goes:
time: 219 us; the launch traced here: 218 us
  other arithmetic  126 us (58%)
  blocking collectives  57.8 us (26%)
  matrix products  21.7 us (10%)
  starting transfers between devices  7.43 us (3%)
  local copies, waits for them, and re-layouts  3.91 us (2%)
    reduce_sum x4, other arithmetic, block_pairs(): jnp.sum(jnp.where(index[:, None, :] == column_ids[None, :, :], weight[:,...  124 us
    psum x4, blocking collectives, by_axis(): return functools.reduce(lax.psum, axes, x)  41.1 us
    dot_general x4, matrix products, block_pairs(): jnp.dot(extended, table, precision=lax.Precision.HIGHEST, preferred_eleme...  21.7 us
    all_to_all x2, blocking collectives, summed_on_arrival(): blocks = lax.all_to_all(in_blocks(x, dim, length), axis, 0, 0, tiled=True)  16.7 us
    ppermute x1, starting transfers between devices, with_halo(): lax.ppermute(tail, axis, [(i, (i + 1) % count) for i in range(ends)])  5.51 us
  transfers between devices with their start and end apart: 2, of which 1 were waited for; matrix products, arithmetic and copies ran while one was open for 1% of the time, Pallas kernels for 0%

commit v1 on v0

v1 whole, which is shorter than its diff:
```python
import jax
import jax.numpy as jnp
from jax import lax
from jax.experimental import pallas as pl
from jax.experimental.pallas import tpu as pltpu
from jax.sharding import Mesh
from jax.sharding import PartitionSpec as P

MEMBERS = 64
NTYPE = 32
COL = ("col_0", "col_1", "col_2")
COL_LEV = ("col_0", "col_1", "col_2", "lev")
GROUPS = 4
TILE = 128
F32 = jnp.float32
BF16 = jnp.bfloat16
VMEM = pl.BlockSpec(memory_space=pltpu.VMEM)


def hi_lo(x):
    hi = x.astype(BF16)
    lo = (x - hi.astype(F32)).astype(BF16)
    return jnp.concatenate([hi, lo], axis=0)


def pack_kernel(state, error, anom, out):
    total = state[0].astype(F32) * error[0:1, :]
    for level in range(1, state.shape[0]):
        total += state[level].astype(F32) * error[level : level + 1, :]
    members, width = total.shape
    out[0, 0 : 2 * members, :] = hi_lo(total)
    rows = anom.shape[0]
    for chunk in range(anom.shape[1] // width):
        at = 2 * members + chunk * rows
        out[0, at : at + rows, :] = anom[:, chunk * width : (chunk + 1) * width]


def pack(state, error, anom):
    levels, members, columns = state.shape
    width = columns // GROUPS
    rows, slots = anom.shape
    height = 2 * members + rows * slots // width
    return pl.pallas_call(
        pack_kernel,
        grid=(GROUPS,),
        in_specs=[
            pl.BlockSpec((levels, members, width), lambda q: (0, 0, q)),
            pl.BlockSpec((levels, width), lambda q: (0, q)),
            pl.BlockSpec((rows, slots), lambda q: (0, 0)),
        ],
        out_specs=pl.BlockSpec((1, height, width), lambda q: (q, 0, 0)),
        out_shape=jax.ShapeDtypeStruct((GROUPS, height, width), BF16),
        name="pack",
    )(state, error, anom)


def total_kernel(parts, out):
    half = out.shape[0] // 2
    total = parts[0, 0:half, :].astype(F32) + parts[0, half:, :].astype(F32)
    for group in range(1, GROUPS):
        total += parts[group, 0:half, :].astype(F32) + parts[group, half:, :].astype(F32)
    out[...] = hi_lo(total)


def total_sens(parts):
    width = parts.shape[2]
    return pl.pallas_call(
        total_kernel,
        grid=(1,),
        in_specs=[pl.BlockSpec((GROUPS, 2 * MEMBERS, width), lambda i: (0, 0, 0))],
        out_specs=pl.BlockSpec((2 * MEMBERS, width), lambda i: (0, 0)),
        out_shape=jax.ShapeDtypeStruct((2 * MEMBERS, width), BF16),
        name="total",
    )(parts)


def pairs_kernel(group, left, mid, right, parts, index, weight, out):
    width = mid.shape[1]
    per = width // TILE
    chunks = out.shape[1] // width
    first = group[0] * per
    neigh = index.shape[0]

    @pl.loop(0, chunks)
    def _(chunk):
        row = pl.multiple_of(2 * MEMBERS + chunk * 16, 16)
        anom = jnp.concatenate([parts[g, pl.ds(row, 16), :] for g in range(GROUPS)], axis=0)
        anom = jnp.concatenate([anom, anom], axis=0)
        spread = [
            lax.dot_general(anom, side[...], (((0,), (0,)), ((), ())), preferred_element_type=F32)
            for side in (left, mid, right)
        ]
        for t in range(per):
            at = pl.multiple_of(chunk * width + t * TILE, TILE)
            idx = index[:, pl.ds(at, TILE)]
            idx = jnp.concatenate([idx] * (TILE // neigh), axis=0).T
            lane = idx & (TILE - 1)
            block = (idx >> 7) - first
            picked = jnp.zeros((TILE, TILE), F32)
            for side in range(3):
                for h in range(per):
                    source = spread[side][t * TILE : (t + 1) * TILE, h * TILE : (h + 1) * TILE]
                    got = jnp.take_along_axis(source, lane, axis=1, mode="promise_in_bounds")
                    picked = jnp.where(block == side * GROUPS * per + h, got, picked)
            picked = picked.T[0:neigh, :]
            pair = jnp.sum(picked * weight[:, pl.ds(at, TILE)], axis=0, keepdims=True)
            out[:, pl.ds(at, TILE)] = pair


def pairs(group, left, mid, right, parts, index, weight):
    slots = index.shape[1]
    return pl.pallas_call(
        pairs_kernel,
        in_specs=[pl.BlockSpec(memory_space=pltpu.SMEM)] + [VMEM] * 6,
        out_specs=VMEM,
        out_shape=jax.ShapeDtypeStruct((1, slots), F32),
        name="pairs",
    )(group, left, mid, right, parts, index, weight)


def shards(state_anom, error_sum, obs_anom, local_weight, neighbours, innovation, obs_type, live):
    send = pack(state_anom, error_sum, obs_anom)
    parts = lax.all_to_all(send, "lev", 0, 0, tiled=True)
    mid = total_sens(parts)
    ends = lax.axis_size(COL) - 1
    left = lax.ppermute(mid, COL, [(i, i + 1) for i in range(ends)])
    right = lax.ppermute(mid, COL, [(i + 1, i) for i in range(ends)])
    group = lax.axis_index("lev").reshape(1)
    share = pairs(group, left, mid, right, parts, neighbours, local_weight)
    got = lax.all_to_all(share.reshape(GROUPS, 1, -1), "lev", 0, 0, tiled=True)
    pair = jnp.sum(got, axis=(0, 1))
    impact = pair * innovation * live.astype(F32) / (MEMBERS - 1.0)
    onehot = (obs_type[None, :] == jnp.arange(NTYPE, dtype=jnp.int32)[:, None]).astype(F32)
    type_part = jnp.sum(onehot * impact[None, :], axis=1)
    count = lax.axis_size(COL_LEV)
    spread = jnp.broadcast_to(type_part[None, None, :], (count, 1, NTYPE))
    type_impact = jnp.sum(lax.all_to_all(spread, COL_LEV, 0, 0, tiled=True), axis=(0, 1))
    return (impact, type_impact)


def solution(mesh):
    split = Mesh(
        mesh.devices.reshape(4, 8, 2, mesh.shape["lev"]), ("col_0", "col_1", "col_2", "lev")
    )
    return jax.shard_map(
        shards,
        mesh=split,
        in_specs=(
            P("lev", None, COL),
            P("lev", COL),
            P("lev", COL),
            P(None, COL),
            P(None, COL),
            P(COL_LEV),
            P(COL_LEV),
            P(COL_LEV),
        ),
        out_specs=(P(COL_LEV), P()),
        check_vma=False,
    )
```

time: 219 us -> 74.7 us (0.34)
  other arithmetic: 126 us -> 0.94 us
  matrix products: 21.7 us -> 0 us
  Pallas kernels: 0 us -> 14 us
  blocking collectives: 57.8 us -> 45.1 us
  waiting for transfers between devices: 0.48 us -> 3.85 us
  local copies, waits for them, and re-layouts: 3.91 us -> 0.71 us
    reduce_sum x6 -> x2, other arithmetic: 124 us -> 0.82 us  [the longest x1 0.8 us: shards(): jnp.sum(lax.all_to_all(spread, COL_LEV, 0, 0, tiled=True), axis=(0, 1))]
    psum x4 -> x0, blocking collectives: 41.1 us -> none  [by_axis(): return functools.reduce(lax.psum, axes, x)]
    all_to_all x2 -> x3, blocking collectives: 16.7 us -> 45.1 us  [the longest x1 25.7 us: shards(): lax.all_to_all(spread, COL_LEV, 0, 0, tiled=True)]
    dot_general x4 -> x0, matrix products: 21.7 us -> none  [block_pairs(): jnp.dot(extended, table, precision=lax.Precision.HIGHEST, preferred_eleme...]
    pallas_call x0 -> x3, Pallas kernels: none -> 14 us  [the longest x1 8.87 us: pairs(): pl.pallas_call(pairs_kernel, in_specs=[pl.BlockSpec(memory_space=pltpu.SM...]
    ppermute x2, waiting for transfers between devices: 0.48 us -> 3.85 us  [the longest x1 3.84 us: shards(): right = lax.ppermute(mid, COL, [(i + 1, i) for i in range(ends)])]
    reshape x3 -> x0, local copies, waits for them, and re-layouts: 3.12 us -> none  [the longest x1 1.13 us: shards(): neighbours.reshape(neighbours.shape[0], count, step_rows)]
  transfers between devices with their start and end apart: 2 -> 2, of which waited for: 1 -> 1; matrix products, arithmetic and copies ran while one was open for 1% -> 0% of each run, Pallas kernels for 0% -> 0%
where the time goes in v1:
time: 74.7 us; the launch traced here: 74.3 us
  blocking collectives  45.1 us (60%)
  Pallas kernels  14 us (19%)
  starting transfers between devices  8.91 us (12%)
  waiting for transfers between devices  3.85 us (5%)
  other arithmetic  0.94 us (1%)
    all_to_all x1, blocking collectives, shards(): lax.all_to_all(spread, COL_LEV, 0, 0, tiled=True)  25.7 us
    all_to_all x1, blocking collectives, shards(): parts = lax.all_to_all(send, 'lev', 0, 0, tiled=True)  12 us
    pallas_call x1, Pallas kernels, pairs(): pl.pallas_call(pairs_kernel, in_specs=[pl.BlockSpec(memory_space=pltpu.SM...  8.87 us
    all_to_all x1, blocking collectives, shards(): got = lax.all_to_all(share.reshape(GROUPS, 1, -1), 'lev', 0, 0, tiled=True)  7.37 us
    ppermute x1, starting transfers between devices, shards(): left = lax.ppermute(mid, COL, [(i, i + 1) for i in range(ends)])  6.99 us
    ppermute x1, waiting for transfers between devices, shards(): right = lax.ppermute(mid, COL, [(i + 1, i) for i in range(ends)])  3.84 us
    pallas_call x1, Pallas kernels, pack(): pl.pallas_call(pack_kernel, grid=(GROUPS,), in_specs=[pl.BlockSpec((level...  3.53 us
    ppermute x1, starting transfers between devices, shards(): right = lax.ppermute(mid, COL, [(i + 1, i) for i in range(ends)])  1.92 us
  transfers between devices with their start and end apart: 2, of which 1 were waited for; matrix products, arithmetic and copies ran while one was open for 0% of the time, Pallas kernels for 0%

profile of v1, /device:TPU:1, one launch (start us, length us, event | category | flops | bytes accessed | tf_op | source)
XLA Modules:
  0.0 74.3 jit_solution(14103082990655055180)
XLA Ops:
  0.6 3.5 %pack.1 = bf16[4,256,256]{2,1,0:T(8,128)(2,1)} custom-call(bf16[12,64,1024]{2,1,0:T(8,128)(2,1)} %state.1, f32[12,1024]{1,0:T(8,128)} %error.1, bf16[16,2048]{1,0:T(8,128)(2,1)} %anom.1), custom_call_target="tpu_custom_call" | custom-call | tf_op jit(solution)/shard_map/pack/pallas_call | solution.py:43
  4.2 0.0 copy-start.4
  4.2 0.0 copy-start.5
  4.2 0.0 copy-start.3
  4.2 12.0 %all_to_all.15.parts = bf16[4,256,256]{2,1,0:T(8,128)(2,1)} all-to-all(bf16[4,256,256]{2,1,0:T(8,128)(2,1)} %pack.1), channel_id=1, replica_groups=mesh['col_0'=4,'col_1'=8,'col_2'=2,'lev'=4] {'lev'}, dimensions={0} | all-to-all | bytes 1048576 | tf_op jit(solution)/shard_map/all_to_all | solution.py:123
  16.2 1.6 %total.1.mid = bf16[128,256]{1,0:T(8,128)(2,1)} custom-call(bf16[4,256,256]{2,1,0:T(8,128)(2,1)} %all_to_all.15.parts), custom_call_target="tpu_custom_call" | custom-call | tf_op jit(solution)/shard_map/total/pallas_call | solution.py:67
  17.8 7.0 %collective-permute-start = (bf16[128,256]{1,0:T(8,128)(2,1)}, bf16[128,256]{1,0:T(8,128)(2,1)S(1)}, u32[]{:S(2)}, u32[]{:S(2)}) collective-permute-start(bf16[128,256]{1,0:T(8,128)(2,1)} %total.1.mid), channel_id=1, source_target_pairs={{0,4},{4,8},{8,12},{12,16},{16,20},{20,24},{24,28},{28,32},{32,36}... | collective-permute-start | bytes 196616 | tf_op jit(solution)/shard_map/ppermute | solution.py:126
  24.8 1.9 %collective-permute-start.1 = (bf16[128,256]{1,0:T(8,128)(2,1)}, bf16[128,256]{1,0:T(8,128)(2,1)S(1)}, u32[]{:S(2)}, u32[]{:S(2)}) collective-permute-start(bf16[128,256]{1,0:T(8,128)(2,1)} %total.1.mid), channel_id=1, source_target_pairs={{4,0},{8,4},{12,8},{16,12},{20,16},{24,20},{28,24},{32,28},{36,32}... | collective-permute-start | bytes 196616 | tf_op jit(solution)/shard_map/ppermute | solution.py:127
  26.7 0.0 collective-permute-done.left
  26.7 0.0 copy-start
  26.7 3.8 %collective-permute-done.1.right = bf16[128,256]{1,0:T(8,128)(2,1)S(1)} collective-permute-done((bf16[128,256]{1,0:T(8,128)(2,1)}, bf16[128,256]{1,0:T(8,128)(2,1)S(1)}, u32[]{:S(2)}, u32[]{:S(2)}) %collective-permute-start.1) | collective-permute-done | bytes 65568 | tf_op jit(solution)/shard_map/ppermute | solution.py:127
  30.6 0.0 copy-start.1
  30.6 0.0 copy-done
  30.6 0.6 copy-done.1
  31.2 8.9 %pairs.1 = f32[1,2048]{1,0:T(1,128)} custom-call(s32[1]{0:T(128)} %bitcast.group, bf16[128,256]{1,0:T(8,128)(2,1)} %copy-done, bf16[128,256]{1,0:T(8,128)(2,1)} %total.1.mid, bf16[128,256]{1,0:T(8,128)(2,1)} %copy-done.1, bf16[4,256,256]{2,1,0:T(8,128)(2,1)} %all_to_all.15.parts, s32[32,2048]{1,0:T(8,128)} %index.1, f32[32,2048]{1,0:T(8,128)} %weight.1), custom_call_target="tpu_custom_call" | custom-call | tf_op jit(solution)/shard_map/pairs/pallas_call | solution.py:112
  40.1 7.4 %all_to_all.16 = f32[4,1,512]{2,1,0:T(1,128)S(1)} all-to-all(f32[4,1,512]{2,1,0:T(1,128)} %bitcast.2), channel_id=1, replica_groups=mesh['col_0'=4,'col_1'=8,'col_2'=2,'lev'=4] {'lev'}, dimensions={0} | all-to-all | bytes 16384 | tf_op jit(solution)/shard_map/all_to_all | solution.py:130
  47.5 0.0 copy-done.4
  47.5 0.0 copy-done.5
  47.5 0.0 copy-done.3
  47.5 0.0 copy-start.2
  47.5 0.1 select_reduce_fusion
  47.6 0.1 broadcast_in_dim.2
  47.7 25.7 %all_to_all.17 = f32[256,1,32]{2,1,0:T(1,128)S(1)} all-to-all(f32[256,1,32]{2,1,0:T(1,128)S(1)} %broadcast_in_dim.2), channel_id=1, replica_groups=mesh['col_0'=4,'col_1'=8,'col_2'=2,'lev'=4] {'col_0','col_1','col_2','lev'}, dimensions={0} | all-to-all | bytes 65536 | tf_op jit(solution)/shard_map/all_to_all | solution.py:137
  73.5 0.8 %reduce_sum.29 = f32[32]{0:T(128)} reduce(f32[256,1,32]{2,1,0:T(1,128)S(1)} %all_to_all.17, f32[]{:T(128)} %constant.8.clone.1), dimensions={0,1}, to_apply=%region_2.0 | reduce | flops 8160 | bytes 32900 | tf_op jit(solution)/shard_map/reduce_sum | solution.py:137
  74.3 0.0 copy-done.2
  (2 shorter events, 0.0 us)
Async XLA Ops:
  4.2 43.3 %copy-start.4 = (s32[512]{0:T(512)S(1)}, s32[512]{0:T(512)}, u32[]{:S(2)}) copy-start(s32[512]{0:T(512)} %param.15) | copy-start | bytes 6148
  4.2 43.3 %copy-start.5 = (f32[512]{0:T(512)S(1)}, f32[512]{0:T(512)}, u32[]{:S(2)}) copy-start(f32[512]{0:T(512)} %param.13) | copy-start | bytes 6148
  4.2 43.3 %copy-start.3 = (s32[512]{0:T(512)S(1)}, s32[512]{0:T(512)}, u32[]{:S(2)}) copy-start(s32[512]{0:T(512)} %param.14) | copy-start | bytes 6148
  17.8 8.9 %collective-permute-start = (bf16[128,256]{1,0:T(8,128)(2,1)}, bf16[128,256]{1,0:T(8,128)(2,1)S(1)}, u32[]{:S(2)}, u32[]{:S(2)}) collective-permute-start(bf16[128,256]{1,0:T(8,128)(2,1)} %total.1.mid), channel_id=1, source_target_pairs={{0,4},{4,8},{8,12},{12,16},{16,20},{20,24},{24,28},{28,32},{32,36}... | collective-permute-start | bytes 196616 | tf_op jit(solution)/shard_map/ppermute | solution.py:126
  24.8 5.8 %collective-permute-start.1 = (bf16[128,256]{1,0:T(8,128)(2,1)}, bf16[128,256]{1,0:T(8,128)(2,1)S(1)}, u32[]{:S(2)}, u32[]{:S(2)}) collective-permute-start(bf16[128,256]{1,0:T(8,128)(2,1)} %total.1.mid), channel_id=1, source_target_pairs={{4,0},{8,4},{12,8},{16,12},{20,16},{24,20},{28,24},{32,28},{36,32}... | collective-permute-start | bytes 196616 | tf_op jit(solution)/shard_map/ppermute | solution.py:127
  26.7 3.9 %copy-start = (bf16[128,256]{1,0:T(8,128)(2,1)}, bf16[128,256]{1,0:T(8,128)(2,1)S(1)}, u32[]{:S(2)}) copy-start(bf16[128,256]{1,0:T(8,128)(2,1)S(1)} %collective-permute-done.left) | copy-start | bytes 196612
  30.6 0.6 copy-start.1
  47.5 26.8 %copy-start.2 = (f32[512]{0:T(512)}, f32[512]{0:T(512)S(1)}, u32[]{:S(2)}) copy-start(f32[512]{0:T(512)S(1)} %multiply_multiply_fusion) | copy-start | bytes 6148

commit v2 on v0

v2 whole, which is shorter than its diff:
```python
import functools

import jax
import jax.numpy as jnp
from jax import lax
from jax.experimental import pallas as pl
from jax.experimental.pallas import tpu as pltpu
from jax.sharding import Mesh
from jax.sharding import PartitionSpec as P

MEMBERS = 64
NTYPE = 32
COL = ("col_0", "col_1", "col_2")
COL_LEV = ("col_0", "col_1", "col_2", "lev")
GROUPS = 4
CORES = 2
LANES = 128
ROWS = 8
QUARTER = 256
F32 = jnp.float32
BF16 = jnp.bfloat16
VMEM = pl.BlockSpec(memory_space=pltpu.VMEM)
SMEM = pl.BlockSpec(memory_space=pltpu.SMEM)
ANY = pl.BlockSpec(memory_space=pl.ANY)


def near(x):
    return pltpu.with_memory_space_constraint(x, pltpu.VMEM)


def halves(x, axis):
    hi = x.astype(BF16)
    lo = (x - hi.astype(F32)).astype(BF16)
    return jnp.concatenate([hi, lo], axis=axis)


def pack_kernel(state, error, anom, innovation, live, kind, out, s_buf, e_buf, a_buf, m_buf, sems):
    levels = state.shape[0]
    copies = [
        pltpu.make_async_copy(error, e_buf, sems.at[0]),
        pltpu.make_async_copy(anom, a_buf, sems.at[1]),
        pltpu.make_async_copy(innovation, m_buf.at[0], sems.at[2]),
    ]
    parts = [
        pltpu.make_async_copy(
            state.at[:, :, q * QUARTER : (q + 1) * QUARTER], s_buf.at[q], sems.at[3 + q]
        )
        for q in range(GROUPS)
    ]
    copies[0].start()
    parts[0].start()
    parts[1].start()
    copies[1].start()
    copies[2].start()
    parts[2].start()
    parts[3].start()
    copies[0].wait()
    for q in range(GROUPS):
        parts[q].wait()
        cols = slice(q * QUARTER, (q + 1) * QUARTER)
        total = s_buf[q, 0].astype(F32) * e_buf[0:1, cols]
        for level in range(1, levels):
            total += s_buf[q, level].astype(F32) * e_buf[level : level + 1, cols]
        out[q, 0 : 2 * MEMBERS, :] = halves(total, 0)
    copies[1].wait()
    copies[2].wait()
    rows = anom.shape[0]
    factor = m_buf[0] * live[...].astype(F32) / (MEMBERS - 1.0)
    upper = factor.astype(BF16).astype(F32)
    meta = jnp.concatenate(
        [upper, factor - upper, kind[...].astype(F32), jnp.zeros_like(factor)], axis=0
    ).astype(BF16)
    meta = jnp.concatenate([meta, jnp.zeros_like(meta)], axis=1)
    for q in range(GROUPS):
        for chunk in range(anom.shape[1] // QUARTER):
            at = 2 * MEMBERS + chunk * rows
            out[q, at : at + rows, :] = a_buf[:, chunk * QUARTER : (chunk + 1) * QUARTER]
        out[q, 4 * MEMBERS : 4 * MEMBERS + 16, :] = meta


def pack(state, error, anom, innovation, live, kind):
    levels = state.shape[0]
    return pl.pallas_call(
        pack_kernel,
        in_specs=[ANY, ANY, ANY, ANY, VMEM, VMEM],
        out_specs=VMEM,
        out_shape=pltpu.VMEM((GROUPS, 4 * MEMBERS + 16, QUARTER), BF16),
        scratch_shapes=[
            pltpu.VMEM((GROUPS, levels, MEMBERS, QUARTER), BF16),
            pltpu.VMEM(error.shape, F32),
            pltpu.VMEM(anom.shape, BF16),
            pltpu.VMEM((1,) + innovation.shape, F32),
            pltpu.SemaphoreType.DMA((3 + GROUPS,)),
        ],
        name="pack",
    )(state, error, anom, innovation, live, kind)


def total_kernel(parts, out):
    half = MEMBERS
    total = parts[0, 0:half, :].astype(F32) + parts[0, half : 2 * half, :].astype(F32)
    for group in range(1, GROUPS):
        total += parts[group, 0:half, :].astype(F32) + parts[group, half : 2 * half, :].astype(F32)
    out[...] = halves(total.T, 1)


def total_sens(parts):
    return pl.pallas_call(
        total_kernel,
        in_specs=[VMEM],
        out_specs=VMEM,
        out_shape=pltpu.VMEM((QUARTER, 2 * MEMBERS), BF16),
        name="total",
    )(near(parts))


def choose(rows, bits):
    for bit in bits:
        rows = [jnp.where(bit, rows[i + 1], rows[i]) for i in range(0, len(rows), 2)]
    return rows[0]


def fill(chunk, tables, parts, spread):
    at = pl.multiple_of(2 * MEMBERS + chunk * 16, 16)
    anom = jnp.concatenate([parts[g, pl.ds(at, 16), :] for g in range(GROUPS)], axis=0)
    anom = jnp.concatenate([anom, anom], axis=0)
    for side, table in enumerate(tables):
        spread[side * QUARTER : (side + 1) * QUARTER, :] = jnp.dot(
            table[...], anom, preferred_element_type=F32
        )


def consume(chunk, bases, spread, index, weight, pair, first):
    for half in range(QUARTER // LANES):
        at = pl.multiple_of(chunk * QUARTER + half * LANES, LANES)
        lanes = slice(half * LANES, (half + 1) * LANES)
        acc = jnp.zeros((ROWS, LANES), F32)
        for n in range(0, index.shape[0], ROWS):
            idx = index[n : n + ROWS, pl.ds(at, LANES)]
            row = idx & (ROWS - 1)
            bits = [(idx & (ROWS << k)) != 0 for k in range(5)]
            block = idx >> 8
            value = jnp.zeros((ROWS, LANES), F32)
            for side, base in enumerate(bases):
                got = [
                    jnp.take_along_axis(
                        spread[side * QUARTER + v * ROWS : side * QUARTER + (v + 1) * ROWS, lanes],
                        row,
                        axis=0,
                        mode="promise_in_bounds",
                    )
                    for v in range(QUARTER // ROWS)
                ]
                value = jnp.where(block == base, choose(got, bits), value)
            acc += value * weight[n : n + ROWS, pl.ds(at, LANES)]
        total = jnp.sum(acc, axis=0, keepdims=True)
        line = chunk * (QUARTER // LANES) + half
        pair[pl.ds(line, 1), :] = total if first is None else first[pl.ds(line, 1), :] + total


def pick(bases, tables, parts, index, weight, pair, first, even, odd):
    chunks = index.shape[1] // QUARTER
    fill(0, tables, parts, even)

    @pl.loop(0, chunks // 2)
    def _(step):
        fill(2 * step + 1, tables, parts, odd)
        consume(2 * step, bases, even, index, weight, pair, first)
        fill(jnp.minimum(2 * step + 2, chunks - 1), tables, parts, even)
        consume(2 * step + 1, bases, odd, index, weight, pair, first)


def near_kernel(lev, core, mid, mate, parts, index, weight, out, even, odd):
    group = lev[0]
    side = jnp.where(core[0] == 0, 2, 0)
    bases = (GROUPS + group, side * GROUPS + group)
    pick(bases, (mid, mate), parts, index, weight, out, None, even, odd)


def far_kernel(lev, core, far, parts, index, weight, first, out, even, odd, pair):
    group = lev[0]
    side = jnp.where(core[0] == 0, 0, 2)
    pick((side * GROUPS + group,), (far,), parts, index, weight, pair, first, even, odd)
    kinds = lax.broadcasted_iota(jnp.int32, (NTYPE, LANES), 0).astype(F32)
    sums = jnp.zeros((NTYPE, LANES), F32)
    per = pair.shape[0] // GROUPS
    for g in range(GROUPS):
        meta = parts[g, 4 * MEMBERS : 4 * MEMBERS + 16, 0:LANES].astype(F32)
        share = pair[g * per : (g + 1) * per, :] * (meta[0:per] + meta[per : 2 * per])
        for r in range(per):
            same = meta[2 * per + r : 2 * per + r + 1] == kinds
            sums += jnp.where(same, share[r : r + 1], 0.0)
    sums = jnp.sum(sums.T, axis=0, keepdims=True)
    tail = jnp.concatenate([sums, jnp.zeros((1, LANES - NTYPE), F32)], axis=1)
    tail = jnp.concatenate([tail, jnp.zeros((ROWS - per - 1, LANES), F32)], axis=0)
    for c in range(CORES):
        for g in range(GROUPS):
            mine = pair[g * per : (g + 1) * per, :]
            to = c * GROUPS + g
            out[to, 0:per, :] = jnp.where(core[0] == c, mine, 0.0)
            out[to, per:ROWS, :] = tail


def shards(state_anom, error_sum, obs_anom, local_weight, neighbours, innovation, obs_type, live):
    lines = innovation.shape[0] // LANES
    send = pack(
        state_anom,
        error_sum,
        obs_anom,
        innovation.reshape(lines, LANES),
        live.reshape(lines, LANES),
        obs_type.reshape(lines, LANES),
    )
    parts = lax.all_to_all(send, "lev", 0, 0, tiled=True)
    mid = total_sens(parts)
    pairs = lax.axis_size(COL) // CORES
    odd_even = [(CORES * i + 1, CORES * i + 2) for i in range(pairs - 1)]
    far = lax.ppermute(mid, COL, odd_even + [(b, a) for a, b in odd_even])
    mate = lax.ppermute(mid, "col_2", [(0, 1), (1, 0)])
    lev = lax.axis_index("lev").reshape(1)
    core = lax.axis_index("col_2").reshape(1)
    slots = neighbours.shape[1]
    index, weight, parts = near(neighbours), near(local_weight), near(parts)
    cost = functools.partial(pl.CostEstimate, bytes_accessed=1 << 20, transcendentals=0)
    first = pl.pallas_call(
        near_kernel,
        in_specs=[SMEM, SMEM] + [VMEM] * 5,
        out_specs=VMEM,
        out_shape=pltpu.VMEM((slots // LANES, LANES), F32),
        scratch_shapes=[pltpu.VMEM((2 * QUARTER, QUARTER), F32)] * 2,
        cost_estimate=cost(flops=1 << 27),
        name="near",
    )(lev, core, near(mid), near(mate), parts, index, weight)
    share = pl.pallas_call(
        far_kernel,
        in_specs=[SMEM, SMEM] + [VMEM] * 5,
        out_specs=VMEM,
        out_shape=pltpu.VMEM((CORES * GROUPS, ROWS, LANES), F32),
        scratch_shapes=[pltpu.VMEM((QUARTER, QUARTER), F32)] * 2
        + [pltpu.VMEM((slots // LANES, LANES), F32)],
        cost_estimate=cost(flops=1 << 26),
        name="far",
    )(lev, core, near(far), parts, index, weight, near(first))
    got = jnp.sum(lax.all_to_all(share, ("col_2", "lev"), 0, 0, tiled=True), axis=0)
    pair = got[0:lines].reshape(-1)
    impact = pair * innovation * live.astype(F32) / (MEMBERS - 1.0)
    chips = ("col_0", "col_1")
    spread = jnp.broadcast_to(got[lines : lines + 1][None], (lax.axis_size(chips), 1, LANES))
    type_impact = jnp.sum(lax.all_to_all(spread, chips, 0, 0, tiled=True), axis=(0, 1))[0:NTYPE]
    return (impact, type_impact)


def solution(mesh):
    split = Mesh(
        mesh.devices.reshape(4, 8, 2, mesh.shape["lev"]), ("col_0", "col_1", "col_2", "lev")
    )
    return jax.shard_map(
        shards,
        mesh=split,
        in_specs=(
            P("lev", None, COL),
            P("lev", COL),
            P("lev", COL),
            P(None, COL),
            P(None, COL),
            P(COL_LEV),
            P(COL_LEV),
            P(COL_LEV),
        ),
        out_specs=(P(COL_LEV), P()),
        check_vma=False,
    )
```

time: 219 us -> 55.7 us (0.25)
  other arithmetic: 126 us -> 1.12 us
  blocking collectives: 57.8 us -> 20.6 us
  matrix products: 21.7 us -> 0 us
  starting transfers between devices: 7.43 us -> 17.7 us
  waiting for transfers between devices: 0.48 us -> 8.05 us
  Pallas kernels: 0 us -> 6.6 us
  local copies, waits for them, and re-layouts: 3.91 us -> 0.64 us
    reduce_sum x7 -> x2, other arithmetic: 124 us -> 0.54 us  [the longest x1 0.53 us: shards(): jnp.sum(lax.all_to_all(spread, chips, 0, 0, tiled=True), axis=(0, 1))]
    psum x4 -> x0, blocking collectives: 41.1 us -> none  [by_axis(): return functools.reduce(lax.psum, axes, x)]
    dot_general x4 -> x0, matrix products: 21.7 us -> none  [block_pairs(): jnp.dot(extended, table, precision=lax.Precision.HIGHEST, preferred_eleme...]
    all_to_all x0 -> x1, starting transfers between devices: none -> 12.1 us  [shards(): lax.all_to_all(spread, chips, 0, 0, tiled=True)]
    all_to_all x0 -> x1, waiting for transfers between devices: none -> 8.05 us  [shards(): lax.all_to_all(spread, chips, 0, 0, tiled=True)]
    pallas_call x0 -> x4, Pallas kernels: none -> 6.6 us  [the longest x1 2.42 us: shards(): pl.pallas_call(near_kernel, in_specs=[SMEM, SMEM] + [VMEM] * 5, out_specs...]
    all_to_all x2, blocking collectives: 16.7 us -> 20.6 us  [the longest x1 13.3 us: shards(): parts = lax.all_to_all(send, 'lev', 0, 0, tiled=True)]
    reshape x3 -> x0, local copies, waits for them, and re-layouts: 3.12 us -> none  [the longest x1 1.13 us: shards(): neighbours.reshape(neighbours.shape[0], count, step_rows)]
  transfers between devices with their start and end apart: 2 -> 3, of which waited for: 1 -> 1; matrix products, arithmetic and copies ran while one was open for 1% -> 1% of each run, Pallas kernels for 0% -> 4%
where the time goes in v2:
time: 55.7 us; the launch traced here: 55.5 us
  blocking collectives  20.6 us (37%)
  starting transfers between devices  17.7 us (32%)
  waiting for transfers between devices  8.05 us (14%)
  Pallas kernels  6.6 us (12%)
  other arithmetic  1.12 us (2%)
  between operations  0.74 us (1%)
  local copies, waits for them, and re-layouts  0.64 us (1%)
    all_to_all x1, blocking collectives, shards(): parts = lax.all_to_all(send, 'lev', 0, 0, tiled=True)  13.3 us
    all_to_all x1, starting transfers between devices, shards(): lax.all_to_all(spread, chips, 0, 0, tiled=True)  12.1 us
    all_to_all x1, waiting for transfers between devices, shards(): lax.all_to_all(spread, chips, 0, 0, tiled=True)  8.05 us
    all_to_all x1, blocking collectives, shards(): lax.all_to_all(share, ('col_2', 'lev'), 0, 0, tiled=True)  7.28 us
    ppermute x1, starting transfers between devices, shards(): far = lax.ppermute(mid, COL, odd_even + [(b, a) for a, b in odd_even])  3.44 us
    pallas_call x1, Pallas kernels, shards(): pl.pallas_call(near_kernel, in_specs=[SMEM, SMEM] + [VMEM] * 5, out_specs...  2.42 us
    pallas_call x1, Pallas kernels, pack(): pl.pallas_call(pack_kernel, in_specs=[ANY, ANY, ANY, ANY, VMEM, VMEM], ou...  2.36 us
    ppermute x1, starting transfers between devices, shards(): mate = lax.ppermute(mid, 'col_2', [(0, 1), (1, 0)])  2.19 us
  transfers between devices with their start and end apart: 3, of which 1 were waited for; matrix products, arithmetic and copies ran while one was open for 1% of the time, Pallas kernels for 4%

profile of v2, /device:TPU:1, one launch (start us, length us, event | category | flops | bytes accessed | tf_op | source)
XLA Modules:
  0.0 55.5 jit_solution(8841794974126370292)
XLA Ops:
  0.6 0.0 copy-start
  0.6 0.0 copy-start.1
  0.7 2.4 %pack.1 = bf16[4,272,256]{2,1,0:T(8,128)(2,1)S(1)} custom-call(bf16[12,64,1024]{2,1,0:T(8,128)(2,1)} %state.1, f32[12,1024]{1,0:T(8,128)} %error.1, bf16[16,2048]{1,0:T(8,128)(2,1)} %anom.1, f32[4,128]{1,0:T(4,128)} %bitcast.16, s32[4,128]{1,0:T(4,128)} %bitcast.17, s32[4,128]{1,0:T(4,128)} %bitcast.18), custom_call_target="tpu_custom_call" | custom-call | tf_op jit(solution)/shard_map/pack/pallas_call | solution.py:83
  3.0 13.3 %all_to_all.15.parts = bf16[4,272,256]{2,1,0:T(8,128)(2,1)S(1)} all-to-all(bf16[4,272,256]{2,1,0:T(8,128)(2,1)S(1)} %pack.1), channel_id=1, replica_groups=mesh['col_0'=4,'col_1'=8,'col_2'=2,'lev'=4] {'lev'}, dimensions={0} | all-to-all | bytes 1114112 | tf_op jit(solution)/shard_map/all_to_all | solution.py:214
  16.3 0.0 copy-start.2
  16.3 0.0 copy-start.3
  16.3 0.2 total.1.mid
  16.5 2.2 %collective-permute-start.1 = (bf16[256,128]{1,0:T(8,128)(2,1)S(1)}, bf16[256,128]{1,0:T(8,128)(2,1)S(1)}, u32[]{:S(2)}, u32[]{:S(2)}) collective-permute-start(bf16[256,128]{1,0:T(8,128)(2,1)S(1)} %total.1.mid), channel_id=1, source_target_pairs={{0,4},{4,0},{1,5},{5,1},{2,6},{6,2},{3,7},{7,3},{8,12},{12,8},{9,1... | collective-permute-start | bytes 196616 | tf_op jit(solution)/shard_map/ppermute | solution.py:219
  18.7 3.4 %collective-permute-start = (bf16[256,128]{1,0:T(8,128)(2,1)S(1)}, bf16[256,128]{1,0:T(8,128)(2,1)S(1)}, u32[]{:S(2)}, u32[]{:S(2)}) collective-permute-start(bf16[256,128]{1,0:T(8,128)(2,1)S(1)} %total.1.mid), channel_id=1, source_target_pairs={{4,8},{12,16},{20,24},{28,32},{36,40},{44,48},{52,56},{60,64},{68,... | collective-permute-start | bytes 196616 | tf_op jit(solution)/shard_map/ppermute | solution.py:218
  22.2 0.0 collective-permute-done.1.mate
  22.2 0.0 copy-done
  22.2 0.0 copy-done.1
  22.2 2.4 %near.1.first = f32[16,128]{1,0:T(8,128)S(1)} custom-call(s32[1]{0:T(128)} %bitcast.lev, s32[1]{0:T(128)} %bitcast.1.core, bf16[256,128]{1,0:T(8,128)(2,1)S(1)} %total.1.mid, bf16[256,128]{1,0:T(8,128)(2,1)S(1)} %collective-permute-done.1.mate, bf16[4,272,256]{2,1,0:T(8,128)(2,1)S(1)} %all_to_all.15.parts, s32[32,2048]{1,0:T(8,128)S(1)} %copy-done, ...), custom_call_target="tpu_custom_call" | custom-call | flops 134217728 | bytes 1048576 | tf_op jit(solution)/shard_map/near/pallas_call | solution.py:225
  24.6 0.0 collective-permute-done.far
  24.7 1.6 %far.1 = f32[8,8,128]{2,1,0:T(8,128)S(1)} custom-call(s32[1]{0:T(128)} %bitcast.lev, s32[1]{0:T(128)} %bitcast.1.core, bf16[256,128]{1,0:T(8,128)(2,1)S(1)} %collective-permute-done.far, bf16[4,272,256]{2,1,0:T(8,128)(2,1)S(1)} %all_to_all.15.parts, s32[32,2048]{1,0:T(8,128)S(1)} %copy-done, f32[32,2048]{1,0:T(8,128)S(1)} %copy-done.1, f32[16,128]{1,0:T(8,128)S(1)} %near.1.first), custom_call_target="tpu_custom_call" | custom-call | flops 67108864 | bytes 1048576 | tf_op jit(solution)/shard_map/far/pallas_call | solution.py:234
  26.3 7.3 %all_to_all.16 = f32[8,8,128]{2,1,0:T(8,128)S(1)} all-to-all(f32[8,8,128]{2,1,0:T(8,128)S(1)} %far.1), channel_id=1, replica_groups=mesh['col_0'=4,'col_1'=8,'col_2'=2,'lev'=4] {'col_2','lev'}, dimensions={0} | all-to-all | bytes 65536 | tf_op jit(solution)/shard_map/all_to_all | solution.py:244
  33.6 0.6 %broadcast_in_dim.9 = f32[32,1,128]{2,1,0:T(1,128)} broadcast(f32[128]{0:T(128)S(1)} %slice_bitcast_fusion), dimensions={2} | broadcast | bytes 16896 | tf_op jit(solution)/shard_map/broadcast_in_dim | solution.py:248
  34.2 12.1 %all-to-all-start.2 = ((f32[32,1,128]{2,1,0:T(1,128)}), f32[32,1,128]{2,1,0:T(1,128)S(1)}, u32[]{:S(2)}, u32[]{:S(2)}) async-start(f32[32,1,128]{2,1,0:T(1,128)} %broadcast_in_dim.9), calls=%async_computation.2 | async-start | bytes 32768 | tf_op jit(solution)/shard_map/all_to_all | solution.py:249
  46.3 0.0 copy-done.2
  46.3 0.0 copy-done.3
  46.3 0.6 %fusion.1 = f32[512]{0:T(512)} fusion(f32[512]{0:T(512)S(1)} %copy-done.2, s32[512]{0:T(512)S(1)} %copy-done.3, f32[8,128]{1,0:T(8,128)S(1)} %reduce_sum.18), kind=kLoop, calls=%fused_computation.2 | loop fusion | flops 2048 | bytes 8192 | tf_op jit(solution)/shard_map/div | solution.py:246
  46.9 8.0 %all-to-all-done.2 = f32[32,1,128]{2,1,0:T(1,128)S(1)} async-done(((f32[32,1,128]{2,1,0:T(1,128)}), f32[32,1,128]{2,1,0:T(1,128)S(1)}, u32[]{:S(2)}, u32[]{:S(2)}) %all-to-all-start.2) | async-done | bytes 16416 | tf_op jit(solution)/shard_map/all_to_all | solution.py:249
  54.9 0.5 reduce_sum.19
  (2 shorter events, 0.0 us)
Async XLA Ops:
  0.6 21.6 %copy-start = (s32[32,2048]{1,0:T(8,128)S(1)}, s32[32,2048]{1,0:T(8,128)}, u32[]{:S(2)}) copy-start(s32[32,2048]{1,0:T(8,128)} %index.3) | copy-start | bytes 786436
  0.6 21.6 %copy-start.1 = (f32[32,2048]{1,0:T(8,128)S(1)}, f32[32,2048]{1,0:T(8,128)}, u32[]{:S(2)}) copy-start(f32[32,2048]{1,0:T(8,128)} %weight.3) | copy-start | bytes 786436
  16.3 30.0 %copy-start.2 = (f32[512]{0:T(512)S(1)}, f32[512]{0:T(512)}, u32[]{:S(2)}) copy-start(f32[512]{0:T(512)} %param.13) | copy-start | bytes 6148
  16.3 30.0 %copy-start.3 = (s32[512]{0:T(512)S(1)}, s32[512]{0:T(512)}, u32[]{:S(2)}) copy-start(s32[512]{0:T(512)} %param.15) | copy-start | bytes 6148
  16.5 5.6 %collective-permute-start.1 = (bf16[256,128]{1,0:T(8,128)(2,1)S(1)}, bf16[256,128]{1,0:T(8,128)(2,1)S(1)}, u32[]{:S(2)}, u32[]{:S(2)}) collective-permute-start(bf16[256,128]{1,0:T(8,128)(2,1)S(1)} %total.1.mid), channel_id=1, source_target_pairs={{0,4},{4,0},{1,5},{5,1},{2,6},{6,2},{3,7},{7,3},{8,12},{12,8},{9,1... | collective-permute-start | bytes 196616 | tf_op jit(solution)/shard_map/ppermute | solution.py:219
  18.7 5.9 %collective-permute-start = (bf16[256,128]{1,0:T(8,128)(2,1)S(1)}, bf16[256,128]{1,0:T(8,128)(2,1)S(1)}, u32[]{:S(2)}, u32[]{:S(2)}) collective-permute-start(bf16[256,128]{1,0:T(8,128)(2,1)S(1)} %total.1.mid), channel_id=1, source_target_pairs={{4,8},{12,16},{20,24},{28,32},{36,40},{44,48},{52,56},{60,64},{68,... | collective-permute-start | bytes 196616 | tf_op jit(solution)/shard_map/ppermute | solution.py:218
  34.2 20.8 %all-to-all-start.2 = ((f32[32,1,128]{2,1,0:T(1,128)}), f32[32,1,128]{2,1,0:T(1,128)S(1)}, u32[]{:S(2)}, u32[]{:S(2)}) async-start(f32[32,1,128]{2,1,0:T(1,128)} %broadcast_in_dim.9), calls=%async_computation.2 | async-start | bytes 32768 | tf_op jit(solution)/shard_map/all_to_all | solution.py:249

commit v3 on v2

--- a/solution.py
+++ b/solution.py
@@ -201,6 +201,25 @@
             out[to, per:ROWS, :] = tail
 
 
+def finish_kernel(got, innovation, live, impact, spread):
+    lines = innovation.shape[0]
+    total = got[0]
+    for peer in range(1, got.shape[0]):
+        total += got[peer]
+    pair = total[0:lines, :]
+    impact[...] = pair * innovation[...] * live[...].astype(F32) / (MEMBERS - 1.0)
+    for chip in range(spread.shape[0]):
+        spread[chip] = total[lines : lines + 1, :]
+
+
+def last_kernel(sums, impact, impact_out, type_out):
+    total = sums[0]
+    for chip in range(1, sums.shape[0]):
+        total += sums[chip]
+    type_out[...] = total[:, 0:NTYPE]
+    impact_out[...] = impact[...]
+
+
 def shards(state_anom, error_sum, obs_anom, local_weight, neighbours, innovation, obs_type, live):
     lines = innovation.shape[0] // LANES
     send = pack(
@@ -241,13 +260,30 @@
         cost_estimate=cost(flops=1 << 26),
         name="far",
     )(lev, core, near(far), parts, index, weight, near(first))
-    got = jnp.sum(lax.all_to_all(share, ("col_2", "lev"), 0, 0, tiled=True), axis=0)
-    pair = got[0:lines].reshape(-1)
-    impact = pair * innovation * live.astype(F32) / (MEMBERS - 1.0)
+    got = lax.all_to_all(share, ("col_2", "lev"), 0, 0, tiled=True)
     chips = ("col_0", "col_1")
-    spread = jnp.broadcast_to(got[lines : lines + 1][None], (lax.axis_size(chips), 1, LANES))
-    type_impact = jnp.sum(lax.all_to_all(spread, chips, 0, 0, tiled=True), axis=(0, 1))[0:NTYPE]
-    return (impact, type_impact)
+    impact, spread = pl.pallas_call(
+        finish_kernel,
+        in_specs=[VMEM] * 3,
+        out_specs=[VMEM] * 2,
+        out_shape=[
+            pltpu.VMEM((lines, LANES), F32),
+            pltpu.VMEM((lax.axis_size(chips), 1, LANES), F32),
+        ],
+        name="finish",
+    )(near(got), near(innovation.reshape(lines, LANES)), near(live.reshape(lines, LANES)))
+    sums = lax.all_to_all(spread, chips, 0, 0, tiled=True)
+    impact, type_impact = pl.pallas_call(
+        last_kernel,
+        in_specs=[VMEM] * 2,
+        out_specs=[VMEM] * 2,
+        out_shape=[
+            jax.ShapeDtypeStruct((lines, LANES), F32),
+            jax.ShapeDtypeStruct((1, NTYPE), F32),
+        ],
+        name="last",
+    )(near(sums), near(impact))
+    return (impact.reshape(-1), type_impact.reshape(-1))
 
 
 def solution(mesh):

time: 55.7 us -> 55 us (0.987)
  blocking collectives: 20.6 us -> 41.1 us
  starting transfers between devices: 17.7 us -> 5.63 us
  waiting for transfers between devices: 8.05 us -> 0.01 us
  other arithmetic: 1.12 us -> 0 us
  local copies, waits for them, and re-layouts: 0.64 us -> 0.02 us
  Pallas kernels: 6.6 us -> 7.2 us
    all_to_all x1 -> x2, blocking collectives: 7.28 us -> 27.8 us  [the longest x1 20.6 us: shards(): sums = lax.all_to_all(spread, chips, 0, 0, tiled=True)]
    all_to_all x1 -> x0, starting transfers between devices: 12.1 us -> none  [shards(): lax.all_to_all(spread, chips, 0, 0, tiled=True)]
    all_to_all x1 -> x0, waiting for transfers between devices: 8.05 us -> none  [shards(): lax.all_to_all(spread, chips, 0, 0, tiled=True)]
    broadcast_in_dim x2 -> x0, local copies, waits for them, and re-layouts: 0.62 us -> none  [shards(): jnp.broadcast_to(got[lines:lines + 1][None], (lax.axis_size(chips), 1, LA...]
    pallas_call x0 -> x2, Pallas kernels: none -> 0.6 us  [the longest x1 0.59 us: shards(): pl.pallas_call(last_kernel, in_specs=[VMEM] * 2, out_specs=[VMEM] * 2, ou...]
    div x1 -> x0, other arithmetic: 0.58 us -> none  [shards(): impact = pair * innovation * live.astype(F32) / (MEMBERS - 1.0)]
  transfers between devices with their start and end apart: 3 -> 2, of which waited for: 1 -> 0; matrix products, arithmetic and copies ran while one was open for 1% -> 0% of each run, Pallas kernels for 4% -> 4%
where the time goes in v3:
time: 55 us; the launch traced here: 54.7 us
  blocking collectives  41.1 us (75%)
  Pallas kernels  7.2 us (13%)
  starting transfers between devices  5.63 us (10%)
  between operations  0.72 us (1%)
    all_to_all x1, blocking collectives, shards(): sums = lax.all_to_all(spread, chips, 0, 0, tiled=True)  20.6 us
    all_to_all x1, blocking collectives, shards(): parts = lax.all_to_all(send, 'lev', 0, 0, tiled=True)  13.3 us
    all_to_all x1, blocking collectives, shards(): got = lax.all_to_all(share, ('col_2', 'lev'), 0, 0, tiled=True)  7.28 us
    ppermute x1, starting transfers between devices, shards(): far = lax.ppermute(mid, COL, odd_even + [(b, a) for a, b in odd_even])  3.44 us
    pallas_call x1, Pallas kernels, shards(): pl.pallas_call(near_kernel, in_specs=[SMEM, SMEM] + [VMEM] * 5, out_specs...  2.42 us
    pallas_call x1, Pallas kernels, pack(): pl.pallas_call(pack_kernel, in_specs=[ANY, ANY, ANY, ANY, VMEM, VMEM], ou...  2.36 us
    ppermute x1, starting transfers between devices, shards(): mate = lax.ppermute(mid, 'col_2', [(0, 1), (1, 0)])  2.19 us
    pallas_call x1, Pallas kernels, shards(): pl.pallas_call(far_kernel, in_specs=[SMEM, SMEM] + [VMEM] * 5, out_specs=...  1.62 us
  transfers between devices with their start and end apart: 2, of which 0 were waited for; matrix products, arithmetic and copies ran while one was open for 0% of the time, Pallas kernels for 4%

profile of v3, /device:TPU:1, one launch (start us, length us, event | category | flops | bytes accessed | tf_op | source)
XLA Modules:
  0.0 54.7 jit_solution(2383559198015835441)
XLA Ops:
  0.6 0.0 copy-start
  0.6 0.0 copy-start.1
  0.7 2.4 %pack.1 = bf16[4,272,256]{2,1,0:T(8,128)(2,1)S(1)} custom-call(bf16[12,64,1024]{2,1,0:T(8,128)(2,1)} %state.1, f32[12,1024]{1,0:T(8,128)} %error.1, bf16[16,2048]{1,0:T(8,128)(2,1)} %anom.1, f32[4,128]{1,0:T(4,128)} %bitcast.7, s32[4,128]{1,0:T(4,128)} %bitcast.9, s32[4,128]{1,0:T(4,128)} %bitcast.11), custom_call_target="tpu_custom_call" | custom-call | tf_op jit(solution)/shard_map/pack/pallas_call | solution.py:83
  3.0 13.3 %all_to_all.15.parts = bf16[4,272,256]{2,1,0:T(8,128)(2,1)S(1)} all-to-all(bf16[4,272,256]{2,1,0:T(8,128)(2,1)S(1)} %pack.1), channel_id=1, replica_groups=mesh['col_0'=4,'col_1'=8,'col_2'=2,'lev'=4] {'lev'}, dimensions={0} | all-to-all | bytes 1114112 | tf_op jit(solution)/shard_map/all_to_all | solution.py:233
  16.3 0.0 copy-start.2
  16.3 0.0 copy-start.3
  16.3 0.2 total.1.mid
  16.5 2.2 %collective-permute-start.1 = (bf16[256,128]{1,0:T(8,128)(2,1)S(1)}, bf16[256,128]{1,0:T(8,128)(2,1)S(1)}, u32[]{:S(2)}, u32[]{:S(2)}) collective-permute-start(bf16[256,128]{1,0:T(8,128)(2,1)S(1)} %total.1.mid), channel_id=1, source_target_pairs={{0,4},{4,0},{1,5},{5,1},{2,6},{6,2},{3,7},{7,3},{8,12},{12,8},{9,1... | collective-permute-start | bytes 196616 | tf_op jit(solution)/shard_map/ppermute | solution.py:238
  18.7 3.4 %collective-permute-start = (bf16[256,128]{1,0:T(8,128)(2,1)S(1)}, bf16[256,128]{1,0:T(8,128)(2,1)S(1)}, u32[]{:S(2)}, u32[]{:S(2)}) collective-permute-start(bf16[256,128]{1,0:T(8,128)(2,1)S(1)} %total.1.mid), channel_id=1, source_target_pairs={{4,8},{12,16},{20,24},{28,32},{36,40},{44,48},{52,56},{60,64},{68,... | collective-permute-start | bytes 196616 | tf_op jit(solution)/shard_map/ppermute | solution.py:237
  22.2 0.0 collective-permute-done.1.mate
  22.2 0.0 copy-done
  22.2 0.0 copy-done.1
  22.2 2.4 %near.1.first = f32[16,128]{1,0:T(8,128)S(1)} custom-call(s32[1]{0:T(128)} %bitcast.lev, s32[1]{0:T(128)} %bitcast.1.core, bf16[256,128]{1,0:T(8,128)(2,1)S(1)} %total.1.mid, bf16[256,128]{1,0:T(8,128)(2,1)S(1)} %collective-permute-done.1.mate, bf16[4,272,256]{2,1,0:T(8,128)(2,1)S(1)} %all_to_all.15.parts, s32[32,2048]{1,0:T(8,128)S(1)} %copy-done, ...), custom_call_target="tpu_custom_call" | custom-call | flops 134217728 | bytes 1048576 | tf_op jit(solution)/shard_map/near/pallas_call | solution.py:244
  24.6 0.0 collective-permute-done.far
  24.7 1.6 %far.1 = f32[8,8,128]{2,1,0:T(8,128)S(1)} custom-call(s32[1]{0:T(128)} %bitcast.lev, s32[1]{0:T(128)} %bitcast.1.core, bf16[256,128]{1,0:T(8,128)(2,1)S(1)} %collective-permute-done.far, bf16[4,272,256]{2,1,0:T(8,128)(2,1)S(1)} %all_to_all.15.parts, s32[32,2048]{1,0:T(8,128)S(1)} %copy-done, f32[32,2048]{1,0:T(8,128)S(1)} %copy-done.1, f32[16,128]{1,0:T(8,128)S(1)} %near.1.first), custom_call_target="tpu_custom_call" | custom-call | flops 67108864 | bytes 1048576 | tf_op jit(solution)/shard_map/far/pallas_call | solution.py:253
  26.3 7.3 %all_to_all.16.got = f32[8,8,128]{2,1,0:T(8,128)S(1)} all-to-all(f32[8,8,128]{2,1,0:T(8,128)S(1)} %far.1), channel_id=1, replica_groups=mesh['col_0'=4,'col_1'=8,'col_2'=2,'lev'=4] {'col_2','lev'}, dimensions={0} | all-to-all | bytes 65536 | tf_op jit(solution)/shard_map/all_to_all | solution.py:263
  33.6 0.0 copy-done.2
  33.6 0.0 copy-done.3
  33.6 20.6 %all_to_all.17.sums = f32[32,1,128]{2,1,0:T(1,128)S(1)} all-to-all(f32[32,1,128]{2,1,0:T(1,128)S(1)} %get-tuple-element.6), channel_id=1, replica_groups=mesh['col_0'=4,'col_1'=8,'col_2'=2,'lev'=4] {'col_0','col_1'}, dimensions={0} | all-to-all | bytes 32768 | tf_op jit(solution)/shard_map/all_to_all | solution.py:275
  54.1 0.6 %last.1 = (f32[4,128]{1,0:T(4,128)}, f32[1,32]{1,0:T(1,128)}) custom-call(f32[32,1,128]{2,1,0:T(1,128)S(1)} %all_to_all.17.sums, f32[4,128]{1,0:T(4,128)S(1)} %get-tuple-element.7.impact), custom_call_target="tpu_custom_call" | custom-call | tf_op jit(solution)/shard_map/last/pallas_call | solution.py:276
  (1 shorter events, 0.0 us)
Async XLA Ops:
  0.6 21.6 %copy-start = (s32[32,2048]{1,0:T(8,128)S(1)}, s32[32,2048]{1,0:T(8,128)}, u32[]{:S(2)}) copy-start(s32[32,2048]{1,0:T(8,128)} %index.3) | copy-start | bytes 786436
  0.6 21.6 %copy-start.1 = (f32[32,2048]{1,0:T(8,128)S(1)}, f32[32,2048]{1,0:T(8,128)}, u32[]{:S(2)}) copy-start(f32[32,2048]{1,0:T(8,128)} %weight.3) | copy-start | bytes 786436
  16.3 17.2 %copy-start.2 = (f32[512]{0:T(512)S(1)}, f32[512]{0:T(512)}, u32[]{:S(2)}) copy-start(f32[512]{0:T(512)} %param.13) | copy-start | bytes 6148
  16.3 17.2 %copy-start.3 = (s32[512]{0:T(512)S(1)}, s32[512]{0:T(512)}, u32[]{:S(2)}) copy-start(s32[512]{0:T(512)} %param.15) | copy-start | bytes 6148
  16.5 5.6 %collective-permute-start.1 = (bf16[256,128]{1,0:T(8,128)(2,1)S(1)}, bf16[256,128]{1,0:T(8,128)(2,1)S(1)}, u32[]{:S(2)}, u32[]{:S(2)}) collective-permute-start(bf16[256,128]{1,0:T(8,128)(2,1)S(1)} %total.1.mid), channel_id=1, source_target_pairs={{0,4},{4,0},{1,5},{5,1},{2,6},{6,2},{3,7},{7,3},{8,12},{12,8},{9,1... | collective-permute-start | bytes 196616 | tf_op jit(solution)/shard_map/ppermute | solution.py:238
  18.7 5.9 %collective-permute-start = (bf16[256,128]{1,0:T(8,128)(2,1)S(1)}, bf16[256,128]{1,0:T(8,128)(2,1)S(1)}, u32[]{:S(2)}, u32[]{:S(2)}) collective-permute-start(bf16[256,128]{1,0:T(8,128)(2,1)S(1)} %total.1.mid), channel_id=1, source_target_pairs={{4,8},{12,16},{20,24},{28,32},{36,40},{44,48},{52,56},{60,64},{68,... | collective-permute-start | bytes 196616 | tf_op jit(solution)/shard_map/ppermute | solution.py:237

commit v4 on v3

--- a/solution.py
+++ b/solution.py
@@ -34,36 +34,28 @@
     return jnp.concatenate([hi, lo], axis=axis)
 
 
-def pack_kernel(state, error, anom, innovation, live, kind, out, s_buf, e_buf, a_buf, m_buf, sems):
+def pack_kernel(lev, state, error, anom, innovation, live, kind, *refs):
+    outs, (s_buf, e_buf, a_buf, m_buf, sems) = refs[:GROUPS], refs[GROUPS:]
     levels = state.shape[0]
-    copies = [
+    order = (2, 3, 1, 0)
+    starts = [pl.multiple_of((lev[0] ^ d) * QUARTER, QUARTER) for d in range(GROUPS)]
+    small = [
         pltpu.make_async_copy(error, e_buf, sems.at[0]),
         pltpu.make_async_copy(anom, a_buf, sems.at[1]),
         pltpu.make_async_copy(innovation, m_buf.at[0], sems.at[2]),
     ]
     parts = [
-        pltpu.make_async_copy(
-            state.at[:, :, q * QUARTER : (q + 1) * QUARTER], s_buf.at[q], sems.at[3 + q]
-        )
-        for q in range(GROUPS)
+        pltpu.make_async_copy(state.at[:, :, pl.ds(starts[d], QUARTER)], s_buf.at[d], sems.at[3 + d])
+        for d in range(GROUPS)
     ]
-    copies[0].start()
-    parts[0].start()
-    parts[1].start()
-    copies[1].start()
-    copies[2].start()
-    parts[2].start()
-    parts[3].start()
-    copies[0].wait()
-    for q in range(GROUPS):
-        parts[q].wait()
-        cols = slice(q * QUARTER, (q + 1) * QUARTER)
-        total = s_buf[q, 0].astype(F32) * e_buf[0:1, cols]
-        for level in range(1, levels):
-            total += s_buf[q, level].astype(F32) * e_buf[level : level + 1, cols]
-        out[q, 0 : 2 * MEMBERS, :] = halves(total, 0)
-    copies[1].wait()
-    copies[2].wait()
+    small[0].start()
+    parts[order[0]].start()
+    small[1].start()
+    small[2].start()
+    for d in order[1:]:
+        parts[d].start()
+    small[1].wait()
+    small[2].wait()
     rows = anom.shape[0]
     factor = m_buf[0] * live[...].astype(F32) / (MEMBERS - 1.0)
     upper = factor.astype(BF16).astype(F32)
@@ -71,20 +63,28 @@
         [upper, factor - upper, kind[...].astype(F32), jnp.zeros_like(factor)], axis=0
     ).astype(BF16)
     meta = jnp.concatenate([meta, jnp.zeros_like(meta)], axis=1)
-    for q in range(GROUPS):
+    for out in outs:
         for chunk in range(anom.shape[1] // QUARTER):
             at = 2 * MEMBERS + chunk * rows
-            out[q, at : at + rows, :] = a_buf[:, chunk * QUARTER : (chunk + 1) * QUARTER]
-        out[q, 4 * MEMBERS : 4 * MEMBERS + 16, :] = meta
-
-
-def pack(state, error, anom, innovation, live, kind):
+            out[at : at + rows, :] = a_buf[:, chunk * QUARTER : (chunk + 1) * QUARTER]
+        out[4 * MEMBERS : 4 * MEMBERS + 16, :] = meta
+    small[0].wait()
+    for d in order:
+        parts[d].wait()
+        scale = e_buf[:, pl.ds(starts[d], QUARTER)]
+        total = s_buf[d, 0].astype(F32) * scale[0:1]
+        for level in range(1, levels):
+            total += s_buf[d, level].astype(F32) * scale[level : level + 1]
+        outs[d][0 : 2 * MEMBERS, :] = halves(total, 0)
+
+
+def pack(lev, state, error, anom, innovation, live, kind):
     levels = state.shape[0]
     return pl.pallas_call(
         pack_kernel,
-        in_specs=[ANY, ANY, ANY, ANY, VMEM, VMEM],
-        out_specs=VMEM,
-        out_shape=pltpu.VMEM((GROUPS, 4 * MEMBERS + 16, QUARTER), BF16),
+        in_specs=[SMEM, ANY, ANY, ANY, ANY, VMEM, VMEM],
+        out_specs=[VMEM] * GROUPS,
+        out_shape=[pltpu.VMEM((4 * MEMBERS + 16, QUARTER), BF16)] * GROUPS,
         scratch_shapes=[
             pltpu.VMEM((GROUPS, levels, MEMBERS, QUARTER), BF16),
             pltpu.VMEM(error.shape, F32),
@@ -93,25 +93,33 @@
             pltpu.SemaphoreType.DMA((3 + GROUPS,)),
         ],
         name="pack",
-    )(state, error, anom, innovation, live, kind)
-
-
-def total_kernel(parts, out):
+    )(lev, state, error, anom, innovation, live, kind)
+
+
+def total_kernel(lev, *refs):
+    parts, out, held = refs[:GROUPS], refs[GROUPS], refs[GROUPS + 1]
     half = MEMBERS
-    total = parts[0, 0:half, :].astype(F32) + parts[0, half : 2 * half, :].astype(F32)
-    for group in range(1, GROUPS):
-        total += parts[group, 0:half, :].astype(F32) + parts[group, half : 2 * half, :].astype(F32)
+    total = parts[0][0:half, :].astype(F32) + parts[0][half : 2 * half, :].astype(F32)
+    for part in parts[1:]:
+        total += part[0:half, :].astype(F32) + part[half : 2 * half, :].astype(F32)
+    held[...] = total
+    rows = MEMBERS // GROUPS
+    total = jnp.concatenate(
+        [held[pl.ds(pl.multiple_of((lev[0] ^ d) * rows, rows), rows), :] for d in range(GROUPS)],
+        axis=0,
+    )
     out[...] = halves(total.T, 1)
 
 
-def total_sens(parts):
+def total_sens(lev, parts):
     return pl.pallas_call(
         total_kernel,
-        in_specs=[VMEM],
+        in_specs=[SMEM] + [VMEM] * GROUPS,
         out_specs=VMEM,
         out_shape=pltpu.VMEM((QUARTER, 2 * MEMBERS), BF16),
+        scratch_shapes=[pltpu.VMEM((MEMBERS, QUARTER), F32)],
         name="total",
-    )(near(parts))
+    )(lev, *parts)
 
 
 def choose(rows, bits):
@@ -122,7 +130,7 @@
 
 def fill(chunk, tables, parts, spread):
     at = pl.multiple_of(2 * MEMBERS + chunk * 16, 16)
-    anom = jnp.concatenate([parts[g, pl.ds(at, 16), :] for g in range(GROUPS)], axis=0)
+    anom = jnp.concatenate([part[pl.ds(at, 16), :] for part in parts], axis=0)
     anom = jnp.concatenate([anom, anom], axis=0)
     for side, table in enumerate(tables):
         spread[side * QUARTER : (side + 1) * QUARTER, :] = jnp.dot(
@@ -154,7 +162,8 @@
                 value = jnp.where(block == base, choose(got, bits), value)
             acc += value * weight[n : n + ROWS, pl.ds(at, LANES)]
         total = jnp.sum(acc, axis=0, keepdims=True)
-        line = chunk * (QUARTER // LANES) + half
+        tile = chunk * (QUARTER // LANES) + half
+        line = (tile >> 2) * ROWS + (tile & 3)
         pair[pl.ds(line, 1), :] = total if first is None else first[pl.ds(line, 1), :] + total
 
 
@@ -170,23 +179,26 @@
         consume(2 * step + 1, bases, odd, index, weight, pair, first)
 
 
-def near_kernel(lev, core, mid, mate, parts, index, weight, out, even, odd):
+def near_kernel(lev, core, mid, mate, *refs):
+    parts, (index, weight, out, even, odd) = refs[:GROUPS], refs[GROUPS:]
     group = lev[0]
     side = jnp.where(core[0] == 0, 2, 0)
     bases = (GROUPS + group, side * GROUPS + group)
     pick(bases, (mid, mate), parts, index, weight, out, None, even, odd)
 
 
-def far_kernel(lev, core, far, parts, index, weight, first, out, even, odd, pair):
+def far_kernel(lev, core, far, *refs):
+    parts, (index, weight, first, out, even, odd, pair) = refs[:GROUPS], refs[GROUPS:]
     group = lev[0]
     side = jnp.where(core[0] == 0, 0, 2)
     pick((side * GROUPS + group,), (far,), parts, index, weight, pair, first, even, odd)
     kinds = lax.broadcasted_iota(jnp.int32, (NTYPE, LANES), 0).astype(F32)
     sums = jnp.zeros((NTYPE, LANES), F32)
-    per = pair.shape[0] // GROUPS
-    for g in range(GROUPS):
-        meta = parts[g, 4 * MEMBERS : 4 * MEMBERS + 16, 0:LANES].astype(F32)
-        share = pair[g * per : (g + 1) * per, :] * (meta[0:per] + meta[per : 2 * per])
+    per = ROWS // 2
+    for d, part in enumerate(parts):
+        meta = part[4 * MEMBERS : 4 * MEMBERS + 16, 0:LANES].astype(F32)
+        share = pair[pl.ds(pl.multiple_of((group ^ d) * ROWS, ROWS), ROWS), :][0:per]
+        share = share * (meta[0:per] + meta[per : 2 * per])
         for r in range(per):
             same = meta[2 * per + r : 2 * per + r + 1] == kinds
             sums += jnp.where(same, share[r : r + 1], 0.0)
@@ -195,7 +207,7 @@
     tail = jnp.concatenate([tail, jnp.zeros((ROWS - per - 1, LANES), F32)], axis=0)
     for c in range(CORES):
         for g in range(GROUPS):
-            mine = pair[g * per : (g + 1) * per, :]
+            mine = pair[g * ROWS : g * ROWS + per, :]
             to = c * GROUPS + g
             out[to, 0:per, :] = jnp.where(core[0] == c, mine, 0.0)
             out[to, per:ROWS, :] = tail
@@ -222,7 +234,10 @@
 
 def shards(state_anom, error_sum, obs_anom, local_weight, neighbours, innovation, obs_type, live):
     lines = innovation.shape[0] // LANES
+    lev = lax.axis_index("lev").reshape(1)
+    core = lax.axis_index("col_2").reshape(1)
     send = pack(
+        lev,
         state_anom,
         error_sum,
         obs_anom,
@@ -230,36 +245,36 @@
         live.reshape(lines, LANES),
         obs_type.reshape(lines, LANES),
     )
-    parts = lax.all_to_all(send, "lev", 0, 0, tiled=True)
-    mid = total_sens(parts)
+    parts = [send[0], None, None, None]
+    for d in (2, 3, 1):
+        parts[d] = lax.ppermute(send[d], "lev", [(i, i ^ d) for i in range(GROUPS)])
+    parts = [near(part) for part in parts]
+    mid = total_sens(lev, parts)
     pairs = lax.axis_size(COL) // CORES
     odd_even = [(CORES * i + 1, CORES * i + 2) for i in range(pairs - 1)]
+    mate = lax.ppermute(mid, "col_2", [(0, 1), (1, 0)])
     far = lax.ppermute(mid, COL, odd_even + [(b, a) for a, b in odd_even])
-    mate = lax.ppermute(mid, "col_2", [(0, 1), (1, 0)])
-    lev = lax.axis_index("lev").reshape(1)
-    core = lax.axis_index("col_2").reshape(1)
-    slots = neighbours.shape[1]
-    index, weight, parts = near(neighbours), near(local_weight), near(parts)
+    index, weight = near(neighbours), near(local_weight)
+    lists = GROUPS * ROWS
     cost = functools.partial(pl.CostEstimate, bytes_accessed=1 << 20, transcendentals=0)
     first = pl.pallas_call(
         near_kernel,
-        in_specs=[SMEM, SMEM] + [VMEM] * 5,
+        in_specs=[SMEM, SMEM] + [VMEM] * (GROUPS + 4),
         out_specs=VMEM,
-        out_shape=pltpu.VMEM((slots // LANES, LANES), F32),
+        out_shape=pltpu.VMEM((lists, LANES), F32),
         scratch_shapes=[pltpu.VMEM((2 * QUARTER, QUARTER), F32)] * 2,
         cost_estimate=cost(flops=1 << 27),
         name="near",
-    )(lev, core, near(mid), near(mate), parts, index, weight)
+    )(lev, core, near(mid), near(mate), *parts, index, weight)
     share = pl.pallas_call(
         far_kernel,
-        in_specs=[SMEM, SMEM] + [VMEM] * 5,
+        in_specs=[SMEM, SMEM] + [VMEM] * (GROUPS + 4),
         out_specs=VMEM,
         out_shape=pltpu.VMEM((CORES * GROUPS, ROWS, LANES), F32),
-        scratch_shapes=[pltpu.VMEM((QUARTER, QUARTER), F32)] * 2
-        + [pltpu.VMEM((slots // LANES, LANES), F32)],
+        scratch_shapes=[pltpu.VMEM((QUARTER, QUARTER), F32)] * 2 + [pltpu.VMEM((lists, LANES), F32)],
         cost_estimate=cost(flops=1 << 26),
         name="far",
-    )(lev, core, near(far), parts, index, weight, near(first))
+    )(lev, core, near(far), *parts, index, weight, near(first))
     got = lax.all_to_all(share, ("col_2", "lev"), 0, 0, tiled=True)
     chips = ("col_0", "col_1")
     impact, spread = pl.pallas_call(

time: 55 us -> 53.9 us (0.980)
  blocking collectives: 41.1 us -> 27.8 us
  waiting for transfers between devices: 0.01 us -> 8.62 us
  starting transfers between devices: 5.63 us -> 9.35 us
    all_to_all x1 -> x0, blocking collectives: 13.3 us -> none  [shards(): parts = lax.all_to_all(send, 'lev', 0, 0, tiled=True)]
    ppermute x0 -> x3, waiting for transfers between devices: none -> 8.62 us  [shards(): parts[d] = lax.ppermute(send[d], 'lev', [(i, i ^ d) for i in range(GROUPS)])]
    ppermute x0 -> x3, starting transfers between devices: none -> 4.61 us  [shards(): parts[d] = lax.ppermute(send[d], 'lev', [(i, i ^ d) for i in range(GROUPS)])]
    ppermute x1, starting transfers between devices: 2.19 us -> 1.3 us  [shards(): mate = lax.ppermute(mid, 'col_2', [(0, 1), (1, 0)])]
  transfers between devices with their start and end apart: 2 -> 5, of which waited for: 0 -> 2; matrix products, arithmetic and copies ran while one was open for 0% -> 0% of each run, Pallas kernels for 4% -> 5%
where the time goes in v4:
time: 53.9 us; the launch traced here: 53.7 us
  blocking collectives  27.8 us (52%)
  starting transfers between devices  9.35 us (17%)
  waiting for transfers between devices  8.62 us (16%)
  Pallas kernels  7.15 us (13%)
  between operations  0.75 us (1%)
    all_to_all x1, blocking collectives, shards(): sums = lax.all_to_all(spread, chips, 0, 0, tiled=True)  21.1 us
    ppermute x3, waiting for transfers between devices, shards(): parts[d] = lax.ppermute(send[d], 'lev', [(i, i ^ d) for i in range(GROUPS)])  8.62 us
    all_to_all x1, blocking collectives, shards(): got = lax.all_to_all(share, ('col_2', 'lev'), 0, 0, tiled=True)  6.74 us
    ppermute x3, starting transfers between devices, shards(): parts[d] = lax.ppermute(send[d], 'lev', [(i, i ^ d) for i in range(GROUPS)])  4.61 us
    ppermute x1, starting transfers between devices, shards(): far = lax.ppermute(mid, COL, odd_even + [(b, a) for a, b in odd_even])  3.44 us
    pallas_call x1, Pallas kernels, shards(): pl.pallas_call(near_kernel, in_specs=[SMEM, SMEM] + [VMEM] * (GROUPS + 4)...  2.42 us
    pallas_call x1, Pallas kernels, pack(): pl.pallas_call(pack_kernel, in_specs=[SMEM, ANY, ANY, ANY, ANY, VMEM, VME...  2.35 us
    pallas_call x1, Pallas kernels, shards(): pl.pallas_call(far_kernel, in_specs=[SMEM, SMEM] + [VMEM] * (GROUPS + 4),...  1.55 us
  transfers between devices with their start and end apart: 5, of which 2 were waited for; matrix products, arithmetic and copies ran while one was open for 0% of the time, Pallas kernels for 5%

profile of v4, /device:TPU:1, one launch (start us, length us, event | category | flops | bytes accessed | tf_op | source)
XLA Modules:
  0.0 53.7 jit_solution(9392507091989398997)
XLA Ops:
  0.6 0.0 copy-start
  0.6 0.0 copy-start.1
  0.7 2.4 %pack.1 = (bf16[272,256]{1,0:T(8,128)(2,1)S(1)}, bf16[272,256]{1,0:T(8,128)(2,1)S(1)}, bf16[272,256]{1,0:T(8,128)(2,1)S(1)}, bf16[272,256]{1,0:T(8,128)(2,1)S(1)}) custom-call(s32[1]{0:T(128)} %bitcast.lev, bf16[12,64,1024]{2,1,0:T(8,128)(2,1)} %state.1, f32[12,1024]{1,0:T(8,128)} %error.1, bf16[16,2048]{1,0:T(8,128)(2,1)} %anom.1, f32[4,128]{1,0:T(4,128)} %bitcast.7, ...), custom_call_target="tpu_custom_call" | custom-call | tf_op jit(solution)/shard_map/pack/pallas_call | solution.py:83
  3.0 0.0 copy-start.2
  3.0 0.0 copy-start.3
  3.0 2.1 %collective-permute-start = (bf16[272,256]{1,0:T(8,128)(2,1)S(1)}, bf16[272,256]{1,0:T(8,128)(2,1)S(1)}, u32[]{:S(2)}, u32[]{:S(2)}) collective-permute-start(bf16[272,256]{1,0:T(8,128)(2,1)S(1)} %get-tuple-element.11), channel_id=1, source_target_pairs={{0,1},{1,0},{2,3},{3,2},{4,5},{5,4},{6,7},{7,6},{8,9},{9,8},{10,11... | collective-permute-start | bytes 417800 | tf_op jit(solution)/shard_map/ppermute | solution.py:250
  5.2 2.5 %collective-permute-start.1 = (bf16[272,256]{1,0:T(8,128)(2,1)S(1)}, bf16[272,256]{1,0:T(8,128)(2,1)S(1)}, u32[]{:S(2)}, u32[]{:S(2)}) collective-permute-start(bf16[272,256]{1,0:T(8,128)(2,1)S(1)} %get-tuple-element.12), channel_id=1, source_target_pairs={{0,2},{1,3},{2,0},{3,1},{4,6},{5,7},{6,4},{7,5},{8,10},{9,11},{10,... | collective-permute-start | bytes 417800 | tf_op jit(solution)/shard_map/ppermute | solution.py:250
  7.6 0.0 collective-permute-start.2
  7.7 0.0 collective-permute-done.refs_1_
  7.7 6.0 %collective-permute-done.1.refs_2_ = bf16[272,256]{1,0:T(8,128)(2,1)S(1)} collective-permute-done((bf16[272,256]{1,0:T(8,128)(2,1)S(1)}, bf16[272,256]{1,0:T(8,128)(2,1)S(1)}, u32[]{:S(2)}, u32[]{:S(2)}) %collective-permute-start.1) | collective-permute-done | bytes 139296 | tf_op jit(solution)/shard_map/ppermute | solution.py:250
  13.7 2.6 %collective-permute-done.2.refs_3_ = bf16[272,256]{1,0:T(8,128)(2,1)S(1)} collective-permute-done((bf16[272,256]{1,0:T(8,128)(2,1)S(1)}, bf16[272,256]{1,0:T(8,128)(2,1)S(1)}, u32[]{:S(2)}, u32[]{:S(2)}) %collective-permute-start.2) | collective-permute-done | bytes 139296 | tf_op jit(solution)/shard_map/ppermute | solution.py:250
  16.3 0.2 total.1.mid
  16.5 1.3 %collective-permute-start.4 = (bf16[256,128]{1,0:T(8,128)(2,1)S(1)}, bf16[256,128]{1,0:T(8,128)(2,1)S(1)}, u32[]{:S(2)}, u32[]{:S(2)}) collective-permute-start(bf16[256,128]{1,0:T(8,128)(2,1)S(1)} %total.1.mid), channel_id=1, source_target_pairs={{0,4},{4,0},{1,5},{5,1},{2,6},{6,2},{3,7},{7,3},{8,12},{12,8},{9,1... | collective-permute-start | bytes 196616 | tf_op jit(solution)/shard_map/ppermute | solution.py:255
  17.8 3.4 %collective-permute-start.3 = (bf16[256,128]{1,0:T(8,128)(2,1)S(1)}, bf16[256,128]{1,0:T(8,128)(2,1)S(1)}, u32[]{:S(2)}, u32[]{:S(2)}) collective-permute-start(bf16[256,128]{1,0:T(8,128)(2,1)S(1)} %total.1.mid), channel_id=1, source_target_pairs={{4,8},{12,16},{20,24},{28,32},{36,40},{44,48},{52,56},{60,64},{68,... | collective-permute-start | bytes 196616 | tf_op jit(solution)/shard_map/ppermute | solution.py:256
  21.2 0.0 collective-permute-done.4.mate
  21.3 0.0 copy-done
  21.3 0.0 copy-done.1
  21.3 2.4 %near.1.refs_6_ = f32[32,128]{1,0:T(8,128)S(1)} custom-call(s32[1]{0:T(128)} %bitcast.lev, s32[1]{0:T(128)} %bitcast.1.core, bf16[256,128]{1,0:T(8,128)(2,1)S(1)} %total.1.mid, bf16[256,128]{1,0:T(8,128)(2,1)S(1)} %collective-permute-done.4.mate, bf16[272,256]{1,0:T(8,128)(2,1)S(1)} %get-tuple-element.10.refs_0_, ...), custom_call_target="tpu_custom_call" | custom-call | flops 134217728 | bytes 1048576 | tf_op jit(solution)/shard_map/near/pallas_call | solution.py:260
  23.7 0.0 collective-permute-done.3.far
  23.7 1.6 %far.1 = f32[8,8,128]{2,1,0:T(8,128)S(1)} custom-call(s32[1]{0:T(128)} %bitcast.lev, s32[1]{0:T(128)} %bitcast.1.core, bf16[256,128]{1,0:T(8,128)(2,1)S(1)} %collective-permute-done.3.far, bf16[272,256]{1,0:T(8,128)(2,1)S(1)} %get-tuple-element.10.refs_0_, bf16[272,256]{1,0:T(8,128)(2,1)S(1)} %collective-permute-done.refs_1_, ...), custom_call_target="tpu_custom_call" | custom-call | flops 67108864 | bytes 1048576 | tf_op jit(solution)/shard_map/far/pallas_call | solution.py:269
  25.3 6.7 %all_to_all.10.got = f32[8,8,128]{2,1,0:T(8,128)S(1)} all-to-all(f32[8,8,128]{2,1,0:T(8,128)S(1)} %far.1), channel_id=1, replica_groups=mesh['col_0'=4,'col_1'=8,'col_2'=2,'lev'=4] {'col_2','lev'}, dimensions={0} | all-to-all | bytes 65536 | tf_op jit(solution)/shard_map/all_to_all | solution.py:278
  32.0 0.0 copy-done.2
  32.0 0.0 copy-done.3
  32.0 21.1 %all_to_all.11.sums = f32[32,1,128]{2,1,0:T(1,128)S(1)} all-to-all(f32[32,1,128]{2,1,0:T(1,128)S(1)} %get-tuple-element.14), channel_id=1, replica_groups=mesh['col_0'=4,'col_1'=8,'col_2'=2,'lev'=4] {'col_0','col_1'}, dimensions={0} | all-to-all | bytes 32768 | tf_op jit(solution)/shard_map/all_to_all | solution.py:290
  53.1 0.6 %last.1 = (f32[4,128]{1,0:T(4,128)}, f32[1,32]{1,0:T(1,128)}) custom-call(f32[32,1,128]{2,1,0:T(1,128)S(1)} %all_to_all.11.sums, f32[4,128]{1,0:T(4,128)S(1)} %get-tuple-element.15.impact), custom_call_target="tpu_custom_call" | custom-call | tf_op jit(solution)/shard_map/last/pallas_call | solution.py:291
  (1 shorter events, 0.0 us)
Async XLA Ops:
  0.6 20.6 %copy-start = (s32[32,2048]{1,0:T(8,128)S(1)}, s32[32,2048]{1,0:T(8,128)}, u32[]{:S(2)}) copy-start(s32[32,2048]{1,0:T(8,128)} %refs_4_.3) | copy-start | bytes 786436
  0.6 20.6 %copy-start.1 = (f32[32,2048]{1,0:T(8,128)S(1)}, f32[32,2048]{1,0:T(8,128)}, u32[]{:S(2)}) copy-start(f32[32,2048]{1,0:T(8,128)} %refs_5_.3) | copy-start | bytes 786436
  3.0 29.0 %copy-start.2 = (f32[512]{0:T(512)S(1)}, f32[512]{0:T(512)}, u32[]{:S(2)}) copy-start(f32[512]{0:T(512)} %param.13) | copy-start | bytes 6148
  3.0 29.0 %copy-start.3 = (s32[512]{0:T(512)S(1)}, s32[512]{0:T(512)}, u32[]{:S(2)}) copy-start(s32[512]{0:T(512)} %param.15) | copy-start | bytes 6148
  3.0 4.6 %collective-permute-start = (bf16[272,256]{1,0:T(8,128)(2,1)S(1)}, bf16[272,256]{1,0:T(8,128)(2,1)S(1)}, u32[]{:S(2)}, u32[]{:S(2)}) collective-permute-start(bf16[272,256]{1,0:T(8,128)(2,1)S(1)} %get-tuple-element.11), channel_id=1, source_target_pairs={{0,1},{1,0},{2,3},{3,2},{4,5},{5,4},{6,7},{7,6},{8,9},{9,8},{10,11... | collective-permute-start | bytes 417800 | tf_op jit(solution)/shard_map/ppermute | solution.py:250
  5.2 8.5 %collective-permute-start.1 = (bf16[272,256]{1,0:T(8,128)(2,1)S(1)}, bf16[272,256]{1,0:T(8,128)(2,1)S(1)}, u32[]{:S(2)}, u32[]{:S(2)}) collective-permute-start(bf16[272,256]{1,0:T(8,128)(2,1)S(1)} %get-tuple-element.12), channel_id=1, source_target_pairs={{0,2},{1,3},{2,0},{3,1},{4,6},{5,7},{6,4},{7,5},{8,10},{9,11},{10,... | collective-permute-start | bytes 417800 | tf_op jit(solution)/shard_map/ppermute | solution.py:250
  7.6 8.7 %collective-permute-start.2 = (bf16[272,256]{1,0:T(8,128)(2,1)S(1)}, bf16[272,256]{1,0:T(8,128)(2,1)S(1)}, u32[]{:S(2)}, u32[]{:S(2)}) collective-permute-start(bf16[272,256]{1,0:T(8,128)(2,1)S(1)} %get-tuple-element.13), channel_id=1, source_target_pairs={{0,3},{1,2},{2,1},{3,0},{4,7},{5,6},{6,5},{7,4},{8,11},{9,10},{10,... | collective-permute-start | bytes 417800 | tf_op jit(solution)/shard_map/ppermute | solution.py:250
  16.5 4.8 %collective-permute-start.4 = (bf16[256,128]{1,0:T(8,128)(2,1)S(1)}, bf16[256,128]{1,0:T(8,128)(2,1)S(1)}, u32[]{:S(2)}, u32[]{:S(2)}) collective-permute-start(bf16[256,128]{1,0:T(8,128)(2,1)S(1)} %total.1.mid), channel_id=1, source_target_pairs={{0,4},{4,0},{1,5},{5,1},{2,6},{6,2},{3,7},{7,3},{8,12},{12,8},{9,1... | collective-permute-start | bytes 196616 | tf_op jit(solution)/shard_map/ppermute | solution.py:255
  17.8 5.9 %collective-permute-start.3 = (bf16[256,128]{1,0:T(8,128)(2,1)S(1)}, bf16[256,128]{1,0:T(8,128)(2,1)S(1)}, u32[]{:S(2)}, u32[]{:S(2)}) collective-permute-start(bf16[256,128]{1,0:T(8,128)(2,1)S(1)} %total.1.mid), channel_id=1, source_target_pairs={{4,8},{12,16},{20,24},{28,32},{36,40},{44,48},{52,56},{60,64},{68,... | collective-permute-start | bytes 196616 | tf_op jit(solution)/shard_map/ppermute | solution.py:256

commit v5 on v4

--- a/solution.py
+++ b/solution.py
@@ -34,41 +34,35 @@
     return jnp.concatenate([hi, lo], axis=axis)
 
 
-def pack_kernel(lev, state, error, anom, innovation, live, kind, *refs):
-    outs, (s_buf, e_buf, a_buf, m_buf, sems) = refs[:GROUPS], refs[GROUPS:]
+def pack_kernel(lev, state, error, innovation, live, kind, *refs):
+    outs, (s_buf, e_buf, m_buf, n_buf, sems) = refs[:GROUPS], refs[GROUPS:]
     levels = state.shape[0]
-    order = (2, 3, 1, 0)
+    order = (1, 2, 3, 0)
     starts = [pl.multiple_of((lev[0] ^ d) * QUARTER, QUARTER) for d in range(GROUPS)]
     small = [
         pltpu.make_async_copy(error, e_buf, sems.at[0]),
-        pltpu.make_async_copy(anom, a_buf, sems.at[1]),
-        pltpu.make_async_copy(innovation, m_buf.at[0], sems.at[2]),
+        pltpu.make_async_copy(innovation, m_buf.at[0], sems.at[1]),
+        pltpu.make_async_copy(live, n_buf.at[0], sems.at[2]),
+        pltpu.make_async_copy(kind, n_buf.at[1], sems.at[3]),
     ]
     parts = [
-        pltpu.make_async_copy(state.at[:, :, pl.ds(starts[d], QUARTER)], s_buf.at[d], sems.at[3 + d])
+        pltpu.make_async_copy(state.at[:, :, pl.ds(starts[d], QUARTER)], s_buf.at[d], sems.at[4 + d])
         for d in range(GROUPS)
     ]
     small[0].start()
     parts[order[0]].start()
-    small[1].start()
-    small[2].start()
+    for copy in small[1:]:
+        copy.start()
     for d in order[1:]:
         parts[d].start()
-    small[1].wait()
-    small[2].wait()
-    rows = anom.shape[0]
-    factor = m_buf[0] * live[...].astype(F32) / (MEMBERS - 1.0)
+    for copy in small:
+        copy.wait()
+    factor = m_buf[0] * n_buf[0].astype(F32) / (MEMBERS - 1.0)
     upper = factor.astype(BF16).astype(F32)
     meta = jnp.concatenate(
-        [upper, factor - upper, kind[...].astype(F32), jnp.zeros_like(factor)], axis=0
+        [upper, factor - upper, n_buf[1].astype(F32), jnp.zeros_like(factor)], axis=0
     ).astype(BF16)
     meta = jnp.concatenate([meta, jnp.zeros_like(meta)], axis=1)
-    for out in outs:
-        for chunk in range(anom.shape[1] // QUARTER):
-            at = 2 * MEMBERS + chunk * rows
-            out[at : at + rows, :] = a_buf[:, chunk * QUARTER : (chunk + 1) * QUARTER]
-        out[4 * MEMBERS : 4 * MEMBERS + 16, :] = meta
-    small[0].wait()
     for d in order:
         parts[d].wait()
         scale = e_buf[:, pl.ds(starts[d], QUARTER)]
@@ -76,24 +70,25 @@
         for level in range(1, levels):
             total += s_buf[d, level].astype(F32) * scale[level : level + 1]
         outs[d][0 : 2 * MEMBERS, :] = halves(total, 0)
-
-
-def pack(lev, state, error, anom, innovation, live, kind):
+        outs[d][2 * MEMBERS :, :] = meta
+
+
+def pack(lev, state, error, innovation, live, kind):
     levels = state.shape[0]
     return pl.pallas_call(
         pack_kernel,
-        in_specs=[SMEM, ANY, ANY, ANY, ANY, VMEM, VMEM],
+        in_specs=[SMEM] + [ANY] * 5,
         out_specs=[VMEM] * GROUPS,
-        out_shape=[pltpu.VMEM((4 * MEMBERS + 16, QUARTER), BF16)] * GROUPS,
+        out_shape=[pltpu.VMEM((2 * MEMBERS + 16, QUARTER), BF16)] * GROUPS,
         scratch_shapes=[
             pltpu.VMEM((GROUPS, levels, MEMBERS, QUARTER), BF16),
             pltpu.VMEM(error.shape, F32),
-            pltpu.VMEM(anom.shape, BF16),
             pltpu.VMEM((1,) + innovation.shape, F32),
-            pltpu.SemaphoreType.DMA((3 + GROUPS,)),
+            pltpu.VMEM((2,) + live.shape, jnp.int32),
+            pltpu.SemaphoreType.DMA((4 + GROUPS,)),
         ],
         name="pack",
-    )(lev, state, error, anom, innovation, live, kind)
+    )(lev, state, error, innovation, live, kind)
 
 
 def total_kernel(lev, *refs):
@@ -129,8 +124,8 @@
 
 
 def fill(chunk, tables, parts, spread):
-    at = pl.multiple_of(2 * MEMBERS + chunk * 16, 16)
-    anom = jnp.concatenate([part[pl.ds(at, 16), :] for part in parts], axis=0)
+    at = pl.multiple_of(chunk * QUARTER, QUARTER)
+    anom = jnp.concatenate([part[:, pl.ds(at, QUARTER)] for part in parts], axis=0)
     anom = jnp.concatenate([anom, anom], axis=0)
     for side, table in enumerate(tables):
         spread[side * QUARTER : (side + 1) * QUARTER, :] = jnp.dot(
@@ -188,15 +183,16 @@
 
 
 def far_kernel(lev, core, far, *refs):
-    parts, (index, weight, first, out, even, odd, pair) = refs[:GROUPS], refs[GROUPS:]
+    anoms, parts = refs[:GROUPS], refs[GROUPS : 2 * GROUPS]
+    index, weight, first, out, even, odd, pair = refs[2 * GROUPS :]
     group = lev[0]
     side = jnp.where(core[0] == 0, 0, 2)
-    pick((side * GROUPS + group,), (far,), parts, index, weight, pair, first, even, odd)
+    pick((side * GROUPS + group,), (far,), anoms, index, weight, pair, first, even, odd)
     kinds = lax.broadcasted_iota(jnp.int32, (NTYPE, LANES), 0).astype(F32)
     sums = jnp.zeros((NTYPE, LANES), F32)
     per = ROWS // 2
     for d, part in enumerate(parts):
-        meta = part[4 * MEMBERS : 4 * MEMBERS + 16, 0:LANES].astype(F32)
+        meta = part[2 * MEMBERS :, 0:LANES].astype(F32)
         share = pair[pl.ds(pl.multiple_of((group ^ d) * ROWS, ROWS), ROWS), :][0:per]
         share = share * (meta[0:per] + meta[per : 2 * per])
         for r in range(per):
@@ -236,19 +232,25 @@
     lines = innovation.shape[0] // LANES
     lev = lax.axis_index("lev").reshape(1)
     core = lax.axis_index("col_2").reshape(1)
+
+    def to_groups(blocks):
+        got = [
+            lax.ppermute(block, "lev", [(i, i ^ d) for i in range(GROUPS)])
+            for d, block in enumerate(blocks)
+            if d > 0
+        ]
+        return [near(block) for block in [blocks[0]] + got]
+
     send = pack(
         lev,
         state_anom,
         error_sum,
-        obs_anom,
         innovation.reshape(lines, LANES),
         live.reshape(lines, LANES),
         obs_type.reshape(lines, LANES),
     )
-    parts = [send[0], None, None, None]
-    for d in (2, 3, 1):
-        parts[d] = lax.ppermute(send[d], "lev", [(i, i ^ d) for i in range(GROUPS)])
-    parts = [near(part) for part in parts]
+    parts = to_groups(send)
+    anoms = to_groups([obs_anom] * GROUPS)
     mid = total_sens(lev, parts)
     pairs = lax.axis_size(COL) // CORES
     odd_even = [(CORES * i + 1, CORES * i + 2) for i in range(pairs - 1)]
@@ -265,16 +267,16 @@
         scratch_shapes=[pltpu.VMEM((2 * QUARTER, QUARTER), F32)] * 2,
         cost_estimate=cost(flops=1 << 27),
         name="near",
-    )(lev, core, near(mid), near(mate), *parts, index, weight)
+    )(lev, core, near(mid), near(mate), *anoms, index, weight)
     share = pl.pallas_call(
         far_kernel,
-        in_specs=[SMEM, SMEM] + [VMEM] * (GROUPS + 4),
+        in_specs=[SMEM, SMEM] + [VMEM] * (2 * GROUPS + 4),
         out_specs=VMEM,
         out_shape=pltpu.VMEM((CORES * GROUPS, ROWS, LANES), F32),
         scratch_shapes=[pltpu.VMEM((QUARTER, QUARTER), F32)] * 2 + [pltpu.VMEM((lists, LANES), F32)],
         cost_estimate=cost(flops=1 << 26),
         name="far",
-    )(lev, core, near(far), *parts, index, weight, near(first))
+    )(lev, core, near(far), *anoms, *parts, index, weight, near(first))
     got = lax.all_to_all(share, ("col_2", "lev"), 0, 0, tiled=True)
     chips = ("col_0", "col_1")
     impact, spread = pl.pallas_call(

time: 53.9 us -> 50.8 us (0.942)
  waiting for transfers between devices: 8.62 us -> 1.66 us
  starting transfers between devices: 9.35 us -> 13.6 us
  Pallas kernels: 7.15 us -> 6.5 us
    ppermute x3 -> x6, waiting for transfers between devices: 8.62 us -> 1.6 us  [to_groups(): lax.ppermute(block, 'lev', [(i, i ^ d) for i in range(GROUPS)])]
    ppermute x3 -> x6, starting transfers between devices: 4.61 us -> 7.87 us  [to_groups(): lax.ppermute(block, 'lev', [(i, i ^ d) for i in range(GROUPS)])]
    ppermute x1, starting transfers between devices: 1.3 us -> 2.72 us  [shards(): mate = lax.ppermute(mid, 'col_2', [(0, 1), (1, 0)])]
    all_to_all x1, blocking collectives: 6.74 us -> 8.07 us  [shards(): got = lax.all_to_all(share, ('col_2', 'lev'), 0, 0, tiled=True)]
    all_to_all x1, blocking collectives: 21.1 us -> 20 us  [shards(): sums = lax.all_to_all(spread, chips, 0, 0, tiled=True)]
    pallas_call x2, Pallas kernels: 3.91 us -> 3.25 us  [the longest x1 1.67 us: pack(): pl.pallas_call(pack_kernel, in_specs=[SMEM] + [ANY] * 5, out_specs=[VMEM]...]
  transfers between devices with their start and end apart: 5 -> 8, of which waited for: 2 -> 2; matrix products, arithmetic and copies ran while one was open for 0% -> 0% of each run, Pallas kernels for 5% -> 5%
where the time goes in v5:
time: 50.8 us; the launch traced here: 50.6 us
  blocking collectives  28 us (55%)
  starting transfers between devices  13.6 us (27%)
  Pallas kernels  6.5 us (13%)
  waiting for transfers between devices  1.66 us (3%)
  between operations  0.77 us (2%)
    all_to_all x1, blocking collectives, shards(): sums = lax.all_to_all(spread, chips, 0, 0, tiled=True)  20 us
    all_to_all x1, blocking collectives, shards(): got = lax.all_to_all(share, ('col_2', 'lev'), 0, 0, tiled=True)  8.07 us
    ppermute x6, starting transfers between devices, to_groups(): lax.ppermute(block, 'lev', [(i, i ^ d) for i in range(GROUPS)])  7.87 us
    ppermute x1, starting transfers between devices, shards(): far = lax.ppermute(mid, COL, odd_even + [(b, a) for a, b in odd_even])  3 us
    ppermute x1, starting transfers between devices, shards(): mate = lax.ppermute(mid, 'col_2', [(0, 1), (1, 0)])  2.72 us
    pallas_call x1, Pallas kernels, shards(): pl.pallas_call(near_kernel, in_specs=[SMEM, SMEM] + [VMEM] * (GROUPS + 4)...  2.43 us
    pallas_call x1, Pallas kernels, pack(): pl.pallas_call(pack_kernel, in_specs=[SMEM] + [ANY] * 5, out_specs=[VMEM]...  1.67 us
    ppermute x6, waiting for transfers between devices, to_groups(): lax.ppermute(block, 'lev', [(i, i ^ d) for i in range(GROUPS)])  1.6 us
  transfers between devices with their start and end apart: 8, of which 2 were waited for; matrix products, arithmetic and copies ran while one was open for 0% of the time, Pallas kernels for 5%

profile of v5, /device:TPU:1, one launch (start us, length us, event | category | flops | bytes accessed | tf_op | source)
XLA Modules:
  0.0 50.6 jit_solution(1610027913394198136)
XLA Ops:
  0.6 0.0 copy-start.2
  0.6 0.0 copy-start
  0.7 0.0 copy-start.1
  0.7 1.7 %pack.1 = (bf16[144,256]{1,0:T(8,128)(2,1)S(1)}, bf16[144,256]{1,0:T(8,128)(2,1)S(1)}, bf16[144,256]{1,0:T(8,128)(2,1)S(1)}, bf16[144,256]{1,0:T(8,128)(2,1)S(1)}) custom-call(s32[1]{0:T(128)} %bitcast.lev, bf16[12,64,1024]{2,1,0:T(8,128)(2,1)} %state.1, f32[12,1024]{1,0:T(8,128)} %error.1, f32[4,128]{1,0:T(4,128)} %bitcast.7, s32[4,128]{1,0:T(4,128)} %bitcast.9, ...), custom_call_target="tpu_custom_call" | custom-call | tf_op jit(solution)/shard_map/pack/pallas_call | solution.py:78
  2.3 0.0 copy-start.3
  2.4 0.0 copy-start.4
  2.4 2.1 %collective-permute-start = (bf16[144,256]{1,0:T(8,128)(2,1)S(1)}, bf16[144,256]{1,0:T(8,128)(2,1)S(1)}, u32[]{:S(2)}, u32[]{:S(2)}) collective-permute-start(bf16[144,256]{1,0:T(8,128)(2,1)S(1)} %get-tuple-element.11), channel_id=1, source_target_pairs={{0,1},{1,0},{2,3},{3,2},{4,5},{5,4},{6,7},{7,6},{8,9},{9,8},{10,11... | collective-permute-start | bytes 221192 | tf_op jit(solution)/shard_map/ppermute | solution.py:238
  4.5 2.5 %collective-permute-start.1 = (bf16[144,256]{1,0:T(8,128)(2,1)S(1)}, bf16[144,256]{1,0:T(8,128)(2,1)S(1)}, u32[]{:S(2)}, u32[]{:S(2)}) collective-permute-start(bf16[144,256]{1,0:T(8,128)(2,1)S(1)} %get-tuple-element.12), channel_id=1, source_target_pairs={{0,2},{1,3},{2,0},{3,1},{4,6},{5,7},{6,4},{7,5},{8,10},{9,11},{10,... | collective-permute-start | bytes 221192 | tf_op jit(solution)/shard_map/ppermute | solution.py:238
  6.9 0.0 collective-permute-start.2
  7.0 0.0 copy-done.2
  7.0 2.6 %collective-permute-start.6 = (bf16[16,2048]{1,0:T(8,128)(2,1)S(1)}, bf16[16,2048]{1,0:T(8,128)(2,1)S(1)}, u32[]{:S(2)}, u32[]{:S(2)}) collective-permute-start(bf16[16,2048]{1,0:T(8,128)(2,1)S(1)} %copy-done.2), channel_id=1, source_target_pairs={{0,3},{1,2},{2,1},{3,0},{4,7},{5,6},{6,5},{7,4},{8,11},{9,10},{10,... | collective-permute-start | bytes 196616 | tf_op jit(solution)/shard_map/ppermute | solution.py:238
  9.6 0.0 collective-permute-start.5
  9.6 0.0 collective-permute-done.refs_1_.refs_5_
  9.6 0.6 %collective-permute-start.4 = (bf16[16,2048]{1,0:T(8,128)(2,1)S(1)}, bf16[16,2048]{1,0:T(8,128)(2,1)S(1)}, u32[]{:S(2)}, u32[]{:S(2)}) collective-permute-start(bf16[16,2048]{1,0:T(8,128)(2,1)S(1)} %copy-done.2), channel_id=1, source_target_pairs={{0,1},{1,0},{2,3},{3,2},{4,5},{5,4},{6,7},{7,6},{8,9},{9,8},{10,11... | collective-permute-start | bytes 196616 | tf_op jit(solution)/shard_map/ppermute | solution.py:238
  10.2 0.0 collective-permute-done.1.refs_2_.refs_6_
  10.2 1.6 %collective-permute-done.2.refs_3_.refs_7_ = bf16[144,256]{1,0:T(8,128)(2,1)S(1)} collective-permute-done((bf16[144,256]{1,0:T(8,128)(2,1)S(1)}, bf16[144,256]{1,0:T(8,128)(2,1)S(1)}, u32[]{:S(2)}, u32[]{:S(2)}) %collective-permute-start.2) | collective-permute-done | bytes 73760 | tf_op jit(solution)/shard_map/ppermute | solution.py:238
  11.8 0.2 total.1.mid
  12.1 2.7 %collective-permute-start.7 = (bf16[256,128]{1,0:T(8,128)(2,1)S(1)}, bf16[256,128]{1,0:T(8,128)(2,1)S(1)}, u32[]{:S(2)}, u32[]{:S(2)}) collective-permute-start(bf16[256,128]{1,0:T(8,128)(2,1)S(1)} %total.1.mid), channel_id=1, source_target_pairs={{0,4},{4,0},{1,5},{5,1},{2,6},{6,2},{3,7},{7,3},{8,12},{12,8},{9,1... | collective-permute-start | bytes 196616 | tf_op jit(solution)/shard_map/ppermute | solution.py:257
  14.8 3.0 %collective-permute-start.3 = (bf16[256,128]{1,0:T(8,128)(2,1)S(1)}, bf16[256,128]{1,0:T(8,128)(2,1)S(1)}, u32[]{:S(2)}, u32[]{:S(2)}) collective-permute-start(bf16[256,128]{1,0:T(8,128)(2,1)S(1)} %total.1.mid), channel_id=1, source_target_pairs={{4,8},{12,16},{20,24},{28,32},{36,40},{44,48},{52,56},{60,64},{68,... | collective-permute-start | bytes 196616 | tf_op jit(solution)/shard_map/ppermute | solution.py:258
  17.8 0.0 collective-permute-done.6.refs_3_
  17.8 0.0 collective-permute-done.5.refs_2_
  17.8 0.0 collective-permute-done.4.refs_1_
  17.8 0.0 collective-permute-done.7.mate
  17.8 0.0 copy-done
  17.8 0.0 copy-done.1
  17.8 2.4 %near.1.refs_10_ = f32[32,128]{1,0:T(8,128)S(1)} custom-call(s32[1]{0:T(128)} %bitcast.lev, s32[1]{0:T(128)} %bitcast.1.core, bf16[256,128]{1,0:T(8,128)(2,1)S(1)} %total.1.mid, bf16[256,128]{1,0:T(8,128)(2,1)S(1)} %collective-permute-done.7.mate, bf16[16,2048]{1,0:T(8,128)(2,1)S(1)} %copy-done.2, bf16[16,2048]{1,0:T(8,128)(2,1)S(1)} %collective-permute-done.4.refs_1_, ...), custom_call_target="tpu_custom_call" | custom-call | flops 134217728 | bytes 1048576 | tf_op jit(solution)/shard_map/near/pallas_call | solution.py:262
  20.3 0.1 collective-permute-done.3.far
  20.3 1.6 %far.1 = f32[8,8,128]{2,1,0:T(8,128)S(1)} custom-call(s32[1]{0:T(128)} %bitcast.lev, s32[1]{0:T(128)} %bitcast.1.core, bf16[256,128]{1,0:T(8,128)(2,1)S(1)} %collective-permute-done.3.far, bf16[16,2048]{1,0:T(8,128)(2,1)S(1)} %copy-done.2, bf16[16,2048]{1,0:T(8,128)(2,1)S(1)} %collective-permute-done.4.refs_1_, ...), custom_call_target="tpu_custom_call" | custom-call | flops 67108864 | bytes 1048576 | tf_op jit(solution)/shard_map/far/pallas_call | solution.py:271
  21.9 8.1 %all_to_all.10.got = f32[8,8,128]{2,1,0:T(8,128)S(1)} all-to-all(f32[8,8,128]{2,1,0:T(8,128)S(1)} %far.1), channel_id=1, replica_groups=mesh['col_0'=4,'col_1'=8,'col_2'=2,'lev'=4] {'col_2','lev'}, dimensions={0} | all-to-all | bytes 65536 | tf_op jit(solution)/shard_map/all_to_all | solution.py:280
  30.0 0.0 copy-done.3
  30.0 0.0 copy-done.4
  30.0 20.0 %all_to_all.11.sums = f32[32,1,128]{2,1,0:T(1,128)S(1)} all-to-all(f32[32,1,128]{2,1,0:T(1,128)S(1)} %get-tuple-element.14), channel_id=1, replica_groups=mesh['col_0'=4,'col_1'=8,'col_2'=2,'lev'=4] {'col_0','col_1'}, dimensions={0} | all-to-all | bytes 32768 | tf_op jit(solution)/shard_map/all_to_all | solution.py:292
  50.0 0.6 %last.1 = (f32[4,128]{1,0:T(4,128)}, f32[1,32]{1,0:T(1,128)}) custom-call(f32[32,1,128]{2,1,0:T(1,128)S(1)} %all_to_all.11.sums, f32[4,128]{1,0:T(4,128)S(1)} %get-tuple-element.15.impact), custom_call_target="tpu_custom_call" | custom-call | tf_op jit(solution)/shard_map/last/pallas_call | solution.py:293
  (1 shorter events, 0.0 us)
Async XLA Ops:
  0.6 6.4 %copy-start.2 = (bf16[16,2048]{1,0:T(8,128)(2,1)S(1)}, bf16[16,2048]{1,0:T(8,128)(2,1)}, u32[]{:S(2)}) copy-start(bf16[16,2048]{1,0:T(8,128)(2,1)} %refs_0_.3) | copy-start | bytes 196612
  0.6 17.2 %copy-start = (s32[32,2048]{1,0:T(8,128)S(1)}, s32[32,2048]{1,0:T(8,128)}, u32[]{:S(2)}) copy-start(s32[32,2048]{1,0:T(8,128)} %refs_8_.1) | copy-start | bytes 786436
  0.7 17.2 %copy-start.1 = (f32[32,2048]{1,0:T(8,128)S(1)}, f32[32,2048]{1,0:T(8,128)}, u32[]{:S(2)}) copy-start(f32[32,2048]{1,0:T(8,128)} %refs_9_.1) | copy-start | bytes 786436
  2.3 27.7 %copy-start.3 = (f32[512]{0:T(512)S(1)}, f32[512]{0:T(512)}, u32[]{:S(2)}) copy-start(f32[512]{0:T(512)} %param.13) | copy-start | bytes 6148
  2.4 27.6 %copy-start.4 = (s32[512]{0:T(512)S(1)}, s32[512]{0:T(512)}, u32[]{:S(2)}) copy-start(s32[512]{0:T(512)} %param.15) | copy-start | bytes 6148
  2.4 7.3 %collective-permute-start = (bf16[144,256]{1,0:T(8,128)(2,1)S(1)}, bf16[144,256]{1,0:T(8,128)(2,1)S(1)}, u32[]{:S(2)}, u32[]{:S(2)}) collective-permute-start(bf16[144,256]{1,0:T(8,128)(2,1)S(1)} %get-tuple-element.11), channel_id=1, source_target_pairs={{0,1},{1,0},{2,3},{3,2},{4,5},{5,4},{6,7},{7,6},{8,9},{9,8},{10,11... | collective-permute-start | bytes 221192 | tf_op jit(solution)/shard_map/ppermute | solution.py:238
  4.5 5.8 %collective-permute-start.1 = (bf16[144,256]{1,0:T(8,128)(2,1)S(1)}, bf16[144,256]{1,0:T(8,128)(2,1)S(1)}, u32[]{:S(2)}, u32[]{:S(2)}) collective-permute-start(bf16[144,256]{1,0:T(8,128)(2,1)S(1)} %get-tuple-element.12), channel_id=1, source_target_pairs={{0,2},{1,3},{2,0},{3,1},{4,6},{5,7},{6,4},{7,5},{8,10},{9,11},{10,... | collective-permute-start | bytes 221192 | tf_op jit(solution)/shard_map/ppermute | solution.py:238
  6.9 4.9 %collective-permute-start.2 = (bf16[144,256]{1,0:T(8,128)(2,1)S(1)}, bf16[144,256]{1,0:T(8,128)(2,1)S(1)}, u32[]{:S(2)}, u32[]{:S(2)}) collective-permute-start(bf16[144,256]{1,0:T(8,128)(2,1)S(1)} %get-tuple-element.13), channel_id=1, source_target_pairs={{0,3},{1,2},{2,1},{3,0},{4,7},{5,6},{6,5},{7,4},{8,11},{9,10},{10,... | collective-permute-start | bytes 221192 | tf_op jit(solution)/shard_map/ppermute | solution.py:238
  7.0 10.8 %collective-permute-start.6 = (bf16[16,2048]{1,0:T(8,128)(2,1)S(1)}, bf16[16,2048]{1,0:T(8,128)(2,1)S(1)}, u32[]{:S(2)}, u32[]{:S(2)}) collective-permute-start(bf16[16,2048]{1,0:T(8,128)(2,1)S(1)} %copy-done.2), channel_id=1, source_target_pairs={{0,3},{1,2},{2,1},{3,0},{4,7},{5,6},{6,5},{7,4},{8,11},{9,10},{10,... | collective-permute-start | bytes 196616 | tf_op jit(solution)/shard_map/ppermute | solution.py:238
  9.6 8.2 %collective-permute-start.5 = (bf16[16,2048]{1,0:T(8,128)(2,1)S(1)}, bf16[16,2048]{1,0:T(8,128)(2,1)S(1)}, u32[]{:S(2)}, u32[]{:S(2)}) collective-permute-start(bf16[16,2048]{1,0:T(8,128)(2,1)S(1)} %copy-done.2), channel_id=1, source_target_pairs={{0,2},{1,3},{2,0},{3,1},{4,6},{5,7},{6,4},{7,5},{8,10},{9,11},{10,... | collective-permute-start | bytes 196616 | tf_op jit(solution)/shard_map/ppermute | solution.py:238
  9.6 8.2 %collective-permute-start.4 = (bf16[16,2048]{1,0:T(8,128)(2,1)S(1)}, bf16[16,2048]{1,0:T(8,128)(2,1)S(1)}, u32[]{:S(2)}, u32[]{:S(2)}) collective-permute-start(bf16[16,2048]{1,0:T(8,128)(2,1)S(1)} %copy-done.2), channel_id=1, source_target_pairs={{0,1},{1,0},{2,3},{3,2},{4,5},{5,4},{6,7},{7,6},{8,9},{9,8},{10,11... | collective-permute-start | bytes 196616 | tf_op jit(solution)/shard_map/ppermute | solution.py:238
  12.1 5.8 %collective-permute-start.7 = (bf16[256,128]{1,0:T(8,128)(2,1)S(1)}, bf16[256,128]{1,0:T(8,128)(2,1)S(1)}, u32[]{:S(2)}, u32[]{:S(2)}) collective-permute-start(bf16[256,128]{1,0:T(8,128)(2,1)S(1)} %total.1.mid), channel_id=1, source_target_pairs={{0,4},{4,0},{1,5},{5,1},{2,6},{6,2},{3,7},{7,3},{8,12},{12,8},{9,1... | collective-permute-start | bytes 196616 | tf_op jit(solution)/shard_map/ppermute | solution.py:257
  14.8 5.6 %collective-permute-start.3 = (bf16[256,128]{1,0:T(8,128)(2,1)S(1)}, bf16[256,128]{1,0:T(8,128)(2,1)S(1)}, u32[]{:S(2)}, u32[]{:S(2)}) collective-permute-start(bf16[256,128]{1,0:T(8,128)(2,1)S(1)} %total.1.mid), channel_id=1, source_target_pairs={{4,8},{12,16},{20,24},{28,32},{36,40},{44,48},{52,56},{60,64},{68,... | collective-permute-start | bytes 196616 | tf_op jit(solution)/shard_map/ppermute | solution.py:258

commit v6 on v5

--- a/solution.py
+++ b/solution.py
@@ -184,7 +184,8 @@
 
 def far_kernel(lev, core, far, *refs):
     anoms, parts = refs[:GROUPS], refs[GROUPS : 2 * GROUPS]
-    index, weight, first, out, even, odd, pair = refs[2 * GROUPS :]
+    index, weight, first = refs[2 * GROUPS : 2 * GROUPS + 3]
+    outs, (spread, even, odd, pair) = refs[-GROUPS - 4 : -4], refs[-4:]
     group = lev[0]
     side = jnp.where(core[0] == 0, 0, 2)
     pick((side * GROUPS + group,), (far,), anoms, index, weight, pair, first, even, odd)
@@ -200,30 +201,22 @@
             sums += jnp.where(same, share[r : r + 1], 0.0)
     sums = jnp.sum(sums.T, axis=0, keepdims=True)
     tail = jnp.concatenate([sums, jnp.zeros((1, LANES - NTYPE), F32)], axis=1)
-    tail = jnp.concatenate([tail, jnp.zeros((ROWS - per - 1, LANES), F32)], axis=0)
-    for c in range(CORES):
-        for g in range(GROUPS):
-            mine = pair[g * ROWS : g * ROWS + per, :]
-            to = c * GROUPS + g
-            out[to, 0:per, :] = jnp.where(core[0] == c, mine, 0.0)
-            out[to, per:ROWS, :] = tail
-
-
-def finish_kernel(got, innovation, live, impact, spread):
+    spread[...] = jnp.broadcast_to(tail[None], spread.shape)
+    for d, out in enumerate(outs):
+        out[...] = pair[pl.ds(pl.multiple_of((group ^ d) * ROWS, ROWS), ROWS), :]
+
+
+def finish_kernel(innovation, live, *refs):
+    shares, impact = refs[:-1], refs[-1]
     lines = innovation.shape[0]
-    total = got[0]
-    for peer in range(1, got.shape[0]):
-        total += got[peer]
-    pair = total[0:lines, :]
+    pair = shares[0][0:lines, :]
+    for share in shares[1:]:
+        pair += share[0:lines, :]
     impact[...] = pair * innovation[...] * live[...].astype(F32) / (MEMBERS - 1.0)
-    for chip in range(spread.shape[0]):
-        spread[chip] = total[lines : lines + 1, :]
 
 
 def last_kernel(sums, impact, impact_out, type_out):
-    total = sums[0]
-    for chip in range(1, sums.shape[0]):
-        total += sums[chip]
+    total = jnp.sum(sums[...], axis=0)
     type_out[...] = total[:, 0:NTYPE]
     impact_out[...] = impact[...]
 
@@ -268,28 +261,29 @@
         cost_estimate=cost(flops=1 << 27),
         name="near",
     )(lev, core, near(mid), near(mate), *anoms, index, weight)
-    share = pl.pallas_call(
+    everyone = lax.axis_size(COL_LEV)
+    *shares, spread = pl.pallas_call(
         far_kernel,
         in_specs=[SMEM, SMEM] + [VMEM] * (2 * GROUPS + 4),
-        out_specs=VMEM,
-        out_shape=pltpu.VMEM((CORES * GROUPS, ROWS, LANES), F32),
+        out_specs=[VMEM] * (GROUPS + 1),
+        out_shape=[pltpu.VMEM((ROWS, LANES), F32)] * GROUPS
+        + [jax.ShapeDtypeStruct((everyone, 1, LANES), F32)],
         scratch_shapes=[pltpu.VMEM((QUARTER, QUARTER), F32)] * 2 + [pltpu.VMEM((lists, LANES), F32)],
         cost_estimate=cost(flops=1 << 26),
         name="far",
     )(lev, core, near(far), *anoms, *parts, index, weight, near(first))
-    got = lax.all_to_all(share, ("col_2", "lev"), 0, 0, tiled=True)
-    chips = ("col_0", "col_1")
-    impact, spread = pl.pallas_call(
+    sums = lax.all_to_all(spread, COL_LEV, 0, 0, tiled=True)
+    impact = pl.pallas_call(
         finish_kernel,
-        in_specs=[VMEM] * 3,
-        out_specs=[VMEM] * 2,
-        out_shape=[
-            pltpu.VMEM((lines, LANES), F32),
-            pltpu.VMEM((lax.axis_size(chips), 1, LANES), F32),
-        ],
+        in_specs=[VMEM] * (GROUPS + 2),
+        out_specs=VMEM,
+        out_shape=pltpu.VMEM((lines, LANES), F32),
         name="finish",
-    )(near(got), near(innovation.reshape(lines, LANES)), near(live.reshape(lines, LANES)))
-    sums = lax.all_to_all(spread, chips, 0, 0, tiled=True)
+    )(
+        near(innovation.reshape(lines, LANES)),
+        near(live.reshape(lines, LANES)),
+        *to_groups(shares),
+    )
     impact, type_impact = pl.pallas_call(
         last_kernel,
         in_specs=[VMEM] * 2,

time: 50.8 us -> 49.8 us (0.980)
  blocking collectives: 28 us -> 0 us
  starting transfers between devices: 13.6 us -> 31 us
  waiting for transfers between devices: 1.66 us -> 10.5 us
  Pallas kernels: 6.5 us -> 7.41 us
    all_to_all x2 -> x0, blocking collectives: 28 us -> none  [the longest x1 20 us: shards(): sums = lax.all_to_all(spread, chips, 0, 0, tiled=True)]
    all_to_all x0 -> x1, starting transfers between devices: none -> 13.5 us  [shards(): sums = lax.all_to_all(spread, COL_LEV, 0, 0, tiled=True)]
    all_to_all x0 -> x1, waiting for transfers between devices: none -> 4.92 us  [shards(): sums = lax.all_to_all(spread, COL_LEV, 0, 0, tiled=True)]
    ppermute x6 -> x9, starting transfers between devices: 7.87 us -> 11.8 us  [to_groups(): lax.ppermute(block, 'lev', [(i, i ^ d) for i in range(GROUPS)])]
    ppermute x6 -> x9, waiting for transfers between devices: 1.6 us -> 5.46 us  [to_groups(): lax.ppermute(block, 'lev', [(i, i ^ d) for i in range(GROUPS)])]
    pallas_call x1, Pallas kernels: 1.58 us -> 2.3 us  [shards(): pl.pallas_call(far_kernel, in_specs=[SMEM, SMEM] + [VMEM] * (2 * GROUPS +...]
  transfers between devices with their start and end apart: 8 -> 12, of which waited for: 2 -> 5; matrix products, arithmetic and copies ran while one was open for 0% -> 0% of each run, Pallas kernels for 5% -> 5%
where the time goes in v6:
time: 49.8 us; the launch traced here: 49.7 us
  starting transfers between devices  31 us (62%)
  waiting for transfers between devices  10.5 us (21%)
  Pallas kernels  7.41 us (15%)
  between operations  0.78 us (2%)
    all_to_all x1, starting transfers between devices, shards(): sums = lax.all_to_all(spread, COL_LEV, 0, 0, tiled=True)  13.5 us
    ppermute x9, starting transfers between devices, to_groups(): lax.ppermute(block, 'lev', [(i, i ^ d) for i in range(GROUPS)])  11.8 us
    ppermute x9, waiting for transfers between devices, to_groups(): lax.ppermute(block, 'lev', [(i, i ^ d) for i in range(GROUPS)])  5.46 us
    all_to_all x1, waiting for transfers between devices, shards(): sums = lax.all_to_all(spread, COL_LEV, 0, 0, tiled=True)  4.92 us
    ppermute x1, starting transfers between devices, shards(): far = lax.ppermute(mid, COL, odd_even + [(b, a) for a, b in odd_even])  2.99 us
    ppermute x1, starting transfers between devices, shards(): mate = lax.ppermute(mid, 'col_2', [(0, 1), (1, 0)])  2.73 us
    pallas_call x1, Pallas kernels, shards(): pl.pallas_call(near_kernel, in_specs=[SMEM, SMEM] + [VMEM] * (GROUPS + 4)...  2.43 us
    pallas_call x1, Pallas kernels, shards(): pl.pallas_call(far_kernel, in_specs=[SMEM, SMEM] + [VMEM] * (2 * GROUPS +...  2.3 us
  transfers between devices with their start and end apart: 12, of which 5 were waited for; matrix products, arithmetic and copies ran while one was open for 0% of the time, Pallas kernels for 5%

profile of v6, /device:TPU:1, one launch (start us, length us, event | category | flops | bytes accessed | tf_op | source)
XLA Modules:
  0.0 49.7 jit_solution(10943442481977998363)
XLA Ops:
  0.6 0.0 copy-start.2
  0.6 0.0 copy-start
  0.7 0.0 copy-start.1
  0.7 1.7 %pack.1 = (bf16[144,256]{1,0:T(8,128)(2,1)S(1)}, bf16[144,256]{1,0:T(8,128)(2,1)S(1)}, bf16[144,256]{1,0:T(8,128)(2,1)S(1)}, bf16[144,256]{1,0:T(8,128)(2,1)S(1)}) custom-call(s32[1]{0:T(128)} %bitcast.lev, bf16[12,64,1024]{2,1,0:T(8,128)(2,1)} %state.1, f32[12,1024]{1,0:T(8,128)} %error.1, f32[4,128]{1,0:T(4,128)} %bitcast.7, s32[4,128]{1,0:T(4,128)} %bitcast.9, ...), custom_call_target="tpu_custom_call" | custom-call | tf_op jit(solution)/shard_map/pack/pallas_call | solution.py:78
  2.3 0.0 copy-start.3
  2.4 0.0 copy-start.4
  2.4 2.1 %collective-permute-start = (bf16[144,256]{1,0:T(8,128)(2,1)S(1)}, bf16[144,256]{1,0:T(8,128)(2,1)S(1)}, u32[]{:S(2)}, u32[]{:S(2)}) collective-permute-start(bf16[144,256]{1,0:T(8,128)(2,1)S(1)} %get-tuple-element.14), channel_id=1, source_target_pairs={{0,1},{1,0},{2,3},{3,2},{4,5},{5,4},{6,7},{7,6},{8,9},{9,8},{10,11... | collective-permute-start | bytes 221192 | tf_op jit(solution)/shard_map/ppermute | solution.py:231
  4.5 2.5 %collective-permute-start.1 = (bf16[144,256]{1,0:T(8,128)(2,1)S(1)}, bf16[144,256]{1,0:T(8,128)(2,1)S(1)}, u32[]{:S(2)}, u32[]{:S(2)}) collective-permute-start(bf16[144,256]{1,0:T(8,128)(2,1)S(1)} %get-tuple-element.15), channel_id=1, source_target_pairs={{0,2},{1,3},{2,0},{3,1},{4,6},{5,7},{6,4},{7,5},{8,10},{9,11},{10,... | collective-permute-start | bytes 221192 | tf_op jit(solution)/shard_map/ppermute | solution.py:231
  6.9 0.0 collective-permute-start.2
  7.0 0.0 copy-done.2
  7.0 2.6 %collective-permute-start.6 = (bf16[16,2048]{1,0:T(8,128)(2,1)S(1)}, bf16[16,2048]{1,0:T(8,128)(2,1)S(1)}, u32[]{:S(2)}, u32[]{:S(2)}) collective-permute-start(bf16[16,2048]{1,0:T(8,128)(2,1)S(1)} %copy-done.2), channel_id=1, source_target_pairs={{0,3},{1,2},{2,1},{3,0},{4,7},{5,6},{6,5},{7,4},{8,11},{9,10},{10,... | collective-permute-start | bytes 196616 | tf_op jit(solution)/shard_map/ppermute | solution.py:231
  9.6 0.0 collective-permute-start.5
  9.6 0.0 collective-permute-done.refs_1_.refs_5_
  9.6 0.6 %collective-permute-start.4 = (bf16[16,2048]{1,0:T(8,128)(2,1)S(1)}, bf16[16,2048]{1,0:T(8,128)(2,1)S(1)}, u32[]{:S(2)}, u32[]{:S(2)}) collective-permute-start(bf16[16,2048]{1,0:T(8,128)(2,1)S(1)} %copy-done.2), channel_id=1, source_target_pairs={{0,1},{1,0},{2,3},{3,2},{4,5},{5,4},{6,7},{7,6},{8,9},{9,8},{10,11... | collective-permute-start | bytes 196616 | tf_op jit(solution)/shard_map/ppermute | solution.py:231
  10.2 0.0 collective-permute-done.1.refs_2_.refs_6_
  10.2 1.6 %collective-permute-done.2.refs_3_.refs_7_ = bf16[144,256]{1,0:T(8,128)(2,1)S(1)} collective-permute-done((bf16[144,256]{1,0:T(8,128)(2,1)S(1)}, bf16[144,256]{1,0:T(8,128)(2,1)S(1)}, u32[]{:S(2)}, u32[]{:S(2)}) %collective-permute-start.2) | collective-permute-done | bytes 73760 | tf_op jit(solution)/shard_map/ppermute | solution.py:231
  11.8 0.2 total.1.mid
  12.1 2.7 %collective-permute-start.7 = (bf16[256,128]{1,0:T(8,128)(2,1)S(1)}, bf16[256,128]{1,0:T(8,128)(2,1)S(1)}, u32[]{:S(2)}, u32[]{:S(2)}) collective-permute-start(bf16[256,128]{1,0:T(8,128)(2,1)S(1)} %total.1.mid), channel_id=1, source_target_pairs={{0,4},{4,0},{1,5},{5,1},{2,6},{6,2},{3,7},{7,3},{8,12},{12,8},{9,1... | collective-permute-start | bytes 196616 | tf_op jit(solution)/shard_map/ppermute | solution.py:250
  14.8 3.0 %collective-permute-start.3 = (bf16[256,128]{1,0:T(8,128)(2,1)S(1)}, bf16[256,128]{1,0:T(8,128)(2,1)S(1)}, u32[]{:S(2)}, u32[]{:S(2)}) collective-permute-start(bf16[256,128]{1,0:T(8,128)(2,1)S(1)} %total.1.mid), channel_id=1, source_target_pairs={{4,8},{12,16},{20,24},{28,32},{36,40},{44,48},{52,56},{60,64},{68,... | collective-permute-start | bytes 196616 | tf_op jit(solution)/shard_map/ppermute | solution.py:251
  17.8 0.0 collective-permute-done.6.refs_3_
  17.8 0.0 collective-permute-done.5.refs_2_
  17.8 0.0 collective-permute-done.4.refs_1_
  17.8 0.0 collective-permute-done.7.mate
  17.8 0.0 copy-done
  17.8 0.0 copy-done.1
  17.8 2.4 %near.1.refs_10_ = f32[32,128]{1,0:T(8,128)S(1)} custom-call(s32[1]{0:T(128)} %bitcast.lev, s32[1]{0:T(128)} %bitcast.1.core, bf16[256,128]{1,0:T(8,128)(2,1)S(1)} %total.1.mid, bf16[256,128]{1,0:T(8,128)(2,1)S(1)} %collective-permute-done.7.mate, bf16[16,2048]{1,0:T(8,128)(2,1)S(1)} %copy-done.2, bf16[16,2048]{1,0:T(8,128)(2,1)S(1)} %collective-permute-done.4.refs_1_, ...), custom_call_target="tpu_custom_call" | custom-call | flops 134217728 | bytes 1048576 | tf_op jit(solution)/shard_map/near/pallas_call | solution.py:255
  20.3 0.1 collective-permute-done.3.far
  20.3 2.3 %far.1 = (f32[8,128]{1,0:T(8,128)S(1)}, f32[8,128]{1,0:T(8,128)S(1)}, f32[8,128]{1,0:T(8,128)S(1)}, f32[8,128]{1,0:T(8,128)S(1)}, f32[256,1,128]{2,1,0:T(1,128)}) custom-call(s32[1]{0:T(128)} %bitcast.lev, s32[1]{0:T(128)} %bitcast.1.core, bf16[256,128]{1,0:T(8,128)(2,1)S(1)} %collective-permute-done.3.far, bf16[16,2048]{1,0:T(8,128)(2,1)S(1)} %copy-done.2, ...), custom_call_target="tpu_custom_call" | custom-call | flops 67108864 | bytes 1048576 | tf_op jit(solution)/shard_map/far/pallas_call | solution.py:265
  22.7 13.5 %all-to-all-start = ((f32[256,1,128]{2,1,0:T(1,128)}), f32[256,1,128]{2,1,0:T(1,128)S(1)}, u32[]{:S(2)}, u32[]{:S(2)}) async-start(f32[256,1,128]{2,1,0:T(1,128)} %get-tuple-element.17), calls=%async_computation | async-start | bytes 262144 | tf_op jit(solution)/shard_map/all_to_all | solution.py:275
  36.2 1.4 %collective-permute-start.8 = (f32[8,128]{1,0:T(8,128)S(1)}, f32[8,128]{1,0:T(8,128)S(1)}, u32[]{:S(2)}, u32[]{:S(2)}) collective-permute-start(f32[8,128]{1,0:T(8,128)S(1)} %get-tuple-element.19), channel_id=1, source_target_pairs={{0,1},{1,0},{2,3},{3,2},{4,5},{5,4},{6,7},{7,6},{8,9},{9,8},{10,11... | collective-permute-start | bytes 12296 | tf_op jit(solution)/shard_map/ppermute | solution.py:231
  37.6 2.4 %collective-permute-start.9 = (f32[8,128]{1,0:T(8,128)S(1)}, f32[8,128]{1,0:T(8,128)S(1)}, u32[]{:S(2)}, u32[]{:S(2)}) collective-permute-start(f32[8,128]{1,0:T(8,128)S(1)} %get-tuple-element.20), channel_id=1, source_target_pairs={{0,2},{1,3},{2,0},{3,1},{4,6},{5,7},{6,4},{7,5},{8,10},{9,11},{10,... | collective-permute-start | bytes 12296 | tf_op jit(solution)/shard_map/ppermute | solution.py:231
  40.0 0.1 collective-permute-start.10
  40.1 0.0 collective-permute-done.8.refs_1_
  40.1 1.7 %collective-permute-done.9.refs_2_ = f32[8,128]{1,0:T(8,128)S(1)} collective-permute-done((f32[8,128]{1,0:T(8,128)S(1)}, f32[8,128]{1,0:T(8,128)S(1)}, u32[]{:S(2)}, u32[]{:S(2)}) %collective-permute-start.9) | collective-permute-done | bytes 4128 | tf_op jit(solution)/shard_map/ppermute | solution.py:231
  41.9 2.1 %collective-permute-done.10.refs_3_ = f32[8,128]{1,0:T(8,128)S(1)} collective-permute-done((f32[8,128]{1,0:T(8,128)S(1)}, f32[8,128]{1,0:T(8,128)S(1)}, u32[]{:S(2)}, u32[]{:S(2)}) %collective-permute-start.10) | collective-permute-done | bytes 4128 | tf_op jit(solution)/shard_map/ppermute | solution.py:231
  44.0 0.0 copy-done.3
  44.0 0.0 copy-done.4
  44.0 4.9 %all-to-all-done.sums = f32[256,1,128]{2,1,0:T(1,128)S(1)} async-done(((f32[256,1,128]{2,1,0:T(1,128)}), f32[256,1,128]{2,1,0:T(1,128)S(1)}, u32[]{:S(2)}, u32[]{:S(2)}) %all-to-all-start) | async-done | bytes 131104 | tf_op jit(solution)/shard_map/all_to_all | solution.py:275
  48.9 0.8 %last.1 = (f32[4,128]{1,0:T(4,128)}, f32[1,32]{1,0:T(1,128)}) custom-call(f32[256,1,128]{2,1,0:T(1,128)S(1)} %all-to-all-done.sums, f32[4,128]{1,0:T(4,128)S(1)} %finish.1.impact), custom_call_target="tpu_custom_call" | custom-call | tf_op jit(solution)/shard_map/last/pallas_call | solution.py:287
  (1 shorter events, 0.0 us)
Async XLA Ops:
  0.6 6.3 %copy-start.2 = (bf16[16,2048]{1,0:T(8,128)(2,1)S(1)}, bf16[16,2048]{1,0:T(8,128)(2,1)}, u32[]{:S(2)}) copy-start(bf16[16,2048]{1,0:T(8,128)(2,1)} %refs_0_.3) | copy-start | bytes 196612
  0.6 17.2 %copy-start = (s32[32,2048]{1,0:T(8,128)S(1)}, s32[32,2048]{1,0:T(8,128)}, u32[]{:S(2)}) copy-start(s32[32,2048]{1,0:T(8,128)} %refs_8_.1) | copy-start | bytes 786436
  0.7 17.2 %copy-start.1 = (f32[32,2048]{1,0:T(8,128)S(1)}, f32[32,2048]{1,0:T(8,128)}, u32[]{:S(2)}) copy-start(f32[32,2048]{1,0:T(8,128)} %refs_9_.1) | copy-start | bytes 786436
  2.3 41.6 %copy-start.3 = (f32[512]{0:T(512)S(1)}, f32[512]{0:T(512)}, u32[]{:S(2)}) copy-start(f32[512]{0:T(512)} %param.13) | copy-start | bytes 6148
  2.4 41.6 %copy-start.4 = (s32[512]{0:T(512)S(1)}, s32[512]{0:T(512)}, u32[]{:S(2)}) copy-start(s32[512]{0:T(512)} %param.15) | copy-start | bytes 6148
  2.4 7.2 %collective-permute-start = (bf16[144,256]{1,0:T(8,128)(2,1)S(1)}, bf16[144,256]{1,0:T(8,128)(2,1)S(1)}, u32[]{:S(2)}, u32[]{:S(2)}) collective-permute-start(bf16[144,256]{1,0:T(8,128)(2,1)S(1)} %get-tuple-element.14), channel_id=1, source_target_pairs={{0,1},{1,0},{2,3},{3,2},{4,5},{5,4},{6,7},{7,6},{8,9},{9,8},{10,11... | collective-permute-start | bytes 221192 | tf_op jit(solution)/shard_map/ppermute | solution.py:231
  4.5 5.8 %collective-permute-start.1 = (bf16[144,256]{1,0:T(8,128)(2,1)S(1)}, bf16[144,256]{1,0:T(8,128)(2,1)S(1)}, u32[]{:S(2)}, u32[]{:S(2)}) collective-permute-start(bf16[144,256]{1,0:T(8,128)(2,1)S(1)} %get-tuple-element.15), channel_id=1, source_target_pairs={{0,2},{1,3},{2,0},{3,1},{4,6},{5,7},{6,4},{7,5},{8,10},{9,11},{10,... | collective-permute-start | bytes 221192 | tf_op jit(solution)/shard_map/ppermute | solution.py:231
  6.9 4.9 %collective-permute-start.2 = (bf16[144,256]{1,0:T(8,128)(2,1)S(1)}, bf16[144,256]{1,0:T(8,128)(2,1)S(1)}, u32[]{:S(2)}, u32[]{:S(2)}) collective-permute-start(bf16[144,256]{1,0:T(8,128)(2,1)S(1)} %get-tuple-element.16), channel_id=1, source_target_pairs={{0,3},{1,2},{2,1},{3,0},{4,7},{5,6},{6,5},{7,4},{8,11},{9,10},{10,... | collective-permute-start | bytes 221192 | tf_op jit(solution)/shard_map/ppermute | solution.py:231
  7.0 10.8 %collective-permute-start.6 = (bf16[16,2048]{1,0:T(8,128)(2,1)S(1)}, bf16[16,2048]{1,0:T(8,128)(2,1)S(1)}, u32[]{:S(2)}, u32[]{:S(2)}) collective-permute-start(bf16[16,2048]{1,0:T(8,128)(2,1)S(1)} %copy-done.2), channel_id=1, source_target_pairs={{0,3},{1,2},{2,1},{3,0},{4,7},{5,6},{6,5},{7,4},{8,11},{9,10},{10,... | collective-permute-start | bytes 196616 | tf_op jit(solution)/shard_map/ppermute | solution.py:231
  9.6 8.2 %collective-permute-start.5 = (bf16[16,2048]{1,0:T(8,128)(2,1)S(1)}, bf16[16,2048]{1,0:T(8,128)(2,1)S(1)}, u32[]{:S(2)}, u32[]{:S(2)}) collective-permute-start(bf16[16,2048]{1,0:T(8,128)(2,1)S(1)} %copy-done.2), channel_id=1, source_target_pairs={{0,2},{1,3},{2,0},{3,1},{4,6},{5,7},{6,4},{7,5},{8,10},{9,11},{10,... | collective-permute-start | bytes 196616 | tf_op jit(solution)/shard_map/ppermute | solution.py:231
  9.6 8.2 %collective-permute-start.4 = (bf16[16,2048]{1,0:T(8,128)(2,1)S(1)}, bf16[16,2048]{1,0:T(8,128)(2,1)S(1)}, u32[]{:S(2)}, u32[]{:S(2)}) collective-permute-start(bf16[16,2048]{1,0:T(8,128)(2,1)S(1)} %copy-done.2), channel_id=1, source_target_pairs={{0,1},{1,0},{2,3},{3,2},{4,5},{5,4},{6,7},{7,6},{8,9},{9,8},{10,11... | collective-permute-start | bytes 196616 | tf_op jit(solution)/shard_map/ppermute | solution.py:231
  12.1 5.8 %collective-permute-start.7 = (bf16[256,128]{1,0:T(8,128)(2,1)S(1)}, bf16[256,128]{1,0:T(8,128)(2,1)S(1)}, u32[]{:S(2)}, u32[]{:S(2)}) collective-permute-start(bf16[256,128]{1,0:T(8,128)(2,1)S(1)} %total.1.mid), channel_id=1, source_target_pairs={{0,4},{4,0},{1,5},{5,1},{2,6},{6,2},{3,7},{7,3},{8,12},{12,8},{9,1... | collective-permute-start | bytes 196616 | tf_op jit(solution)/shard_map/ppermute | solution.py:250
  14.8 5.6 %collective-permute-start.3 = (bf16[256,128]{1,0:T(8,128)(2,1)S(1)}, bf16[256,128]{1,0:T(8,128)(2,1)S(1)}, u32[]{:S(2)}, u32[]{:S(2)}) collective-permute-start(bf16[256,128]{1,0:T(8,128)(2,1)S(1)} %total.1.mid), channel_id=1, source_target_pairs={{4,8},{12,16},{20,24},{28,32},{36,40},{44,48},{52,56},{60,64},{68,... | collective-permute-start | bytes 196616 | tf_op jit(solution)/shard_map/ppermute | solution.py:251
  22.7 26.2 %all-to-all-start = ((f32[256,1,128]{2,1,0:T(1,128)}), f32[256,1,128]{2,1,0:T(1,128)S(1)}, u32[]{:S(2)}, u32[]{:S(2)}) async-start(f32[256,1,128]{2,1,0:T(1,128)} %get-tuple-element.17), calls=%async_computation | async-start | bytes 262144 | tf_op jit(solution)/shard_map/all_to_all | solution.py:275
  36.2 3.9 %collective-permute-start.8 = (f32[8,128]{1,0:T(8,128)S(1)}, f32[8,128]{1,0:T(8,128)S(1)}, u32[]{:S(2)}, u32[]{:S(2)}) collective-permute-start(f32[8,128]{1,0:T(8,128)S(1)} %get-tuple-element.19), channel_id=1, source_target_pairs={{0,1},{1,0},{2,3},{3,2},{4,5},{5,4},{6,7},{7,6},{8,9},{9,8},{10,11... | collective-permute-start | bytes 12296 | tf_op jit(solution)/shard_map/ppermute | solution.py:231
  37.6 4.3 %collective-permute-start.9 = (f32[8,128]{1,0:T(8,128)S(1)}, f32[8,128]{1,0:T(8,128)S(1)}, u32[]{:S(2)}, u32[]{:S(2)}) collective-permute-start(f32[8,128]{1,0:T(8,128)S(1)} %get-tuple-element.20), channel_id=1, source_target_pairs={{0,2},{1,3},{2,0},{3,1},{4,6},{5,7},{6,4},{7,5},{8,10},{9,11},{10,... | collective-permute-start | bytes 12296 | tf_op jit(solution)/shard_map/ppermute | solution.py:231
  40.0 4.0 %collective-permute-start.10 = (f32[8,128]{1,0:T(8,128)S(1)}, f32[8,128]{1,0:T(8,128)S(1)}, u32[]{:S(2)}, u32[]{:S(2)}) collective-permute-start(f32[8,128]{1,0:T(8,128)S(1)} %get-tuple-element.21), channel_id=1, source_target_pairs={{0,3},{1,2},{2,1},{3,0},{4,7},{5,6},{6,5},{7,4},{8,11},{9,10},{10,... | collective-permute-start | bytes 12296 | tf_op jit(solution)/shard_map/ppermute | solution.py:231

commit v7 on v6

--- a/solution.py
+++ b/solution.py
@@ -221,18 +221,16 @@
     impact_out[...] = impact[...]
 
 
-def shards(state_anom, error_sum, obs_anom, local_weight, neighbours, innovation, obs_type, live):
+def steps(state_anom, error_sum, obs_anom, local_weight, neighbours, innovation, obs_type, live):
     lines = innovation.shape[0] // LANES
     lev = lax.axis_index("lev").reshape(1)
     core = lax.axis_index("col_2").reshape(1)
 
     def to_groups(blocks):
-        got = [
-            lax.ppermute(block, "lev", [(i, i ^ d) for i in range(GROUPS)])
-            for d, block in enumerate(blocks)
-            if d > 0
-        ]
-        return [near(block) for block in [blocks[0]] + got]
+        got = [blocks[0]]
+        for d in range(1, GROUPS):
+            got.append(lax.ppermute(blocks[d], "lev", [(i, i ^ d) for i in range(GROUPS)]))
+        return [near(block) for block in got]
 
     send = pack(
         lev,
@@ -247,8 +245,8 @@
     mid = total_sens(lev, parts)
     pairs = lax.axis_size(COL) // CORES
     odd_even = [(CORES * i + 1, CORES * i + 2) for i in range(pairs - 1)]
+    far = lax.ppermute(mid, COL, odd_even + [(b, a) for a, b in odd_even])
     mate = lax.ppermute(mid, "col_2", [(0, 1), (1, 0)])
-    far = lax.ppermute(mid, COL, odd_even + [(b, a) for a, b in odd_even])
     index, weight = near(neighbours), near(local_weight)
     lists = GROUPS * ROWS
     cost = functools.partial(pl.CostEstimate, bytes_accessed=1 << 20, transcendentals=0)
@@ -302,7 +300,7 @@
         mesh.devices.reshape(4, 8, 2, mesh.shape["lev"]), ("col_0", "col_1", "col_2", "lev")
     )
     return jax.shard_map(
-        shards,
+        steps,
         mesh=split,
         in_specs=(
             P("lev", None, COL),

time: 49.8 us -> 49.8 us (level)
  no operation moved by 1% of the time
where the time goes in v7:
time: 49.8 us; the launch traced here: 49.7 us
  starting transfers between devices  31 us (62%)
  waiting for transfers between devices  10.5 us (21%)
  Pallas kernels  7.41 us (15%)
  between operations  0.78 us (2%)
    all_to_all x1, starting transfers between devices, steps(): sums = lax.all_to_all(spread, COL_LEV, 0, 0, tiled=True)  13.5 us
    ppermute x9, starting transfers between devices, to_groups(): lax.ppermute(blocks[d], 'lev', [(i, i ^ d) for i in range(GROUPS)])  11.8 us
    ppermute x9, waiting for transfers between devices, to_groups(): lax.ppermute(blocks[d], 'lev', [(i, i ^ d) for i in range(GROUPS)])  5.46 us
    all_to_all x1, waiting for transfers between devices, steps(): sums = lax.all_to_all(spread, COL_LEV, 0, 0, tiled=True)  4.92 us
    ppermute x1, starting transfers between devices, steps(): far = lax.ppermute(mid, COL, odd_even + [(b, a) for a, b in odd_even])  2.99 us
    ppermute x1, starting transfers between devices, steps(): mate = lax.ppermute(mid, 'col_2', [(0, 1), (1, 0)])  2.73 us
    pallas_call x1, Pallas kernels, steps(): pl.pallas_call(near_kernel, in_specs=[SMEM, SMEM] + [VMEM] * (GROUPS + 4)...  2.43 us
    pallas_call x1, Pallas kernels, steps(): pl.pallas_call(far_kernel, in_specs=[SMEM, SMEM] + [VMEM] * (2 * GROUPS +...  2.3 us
  transfers between devices with their start and end apart: 12, of which 5 were waited for; matrix products, arithmetic and copies ran while one was open for 0% of the time, Pallas kernels for 5%

profile of v7, /device:TPU:1, one launch (start us, length us, event | category | flops | bytes accessed | tf_op | source)
XLA Modules:
  0.0 49.7 jit_solution(10943442481977998363)
XLA Ops:
  0.6 0.0 copy-start.2
  0.6 0.0 copy-start
  0.7 0.0 copy-start.1
  0.7 1.7 %pack.1 = (bf16[144,256]{1,0:T(8,128)(2,1)S(1)}, bf16[144,256]{1,0:T(8,128)(2,1)S(1)}, bf16[144,256]{1,0:T(8,128)(2,1)S(1)}, bf16[144,256]{1,0:T(8,128)(2,1)S(1)}) custom-call(s32[1]{0:T(128)} %bitcast.lev, bf16[12,64,1024]{2,1,0:T(8,128)(2,1)} %state.1, f32[12,1024]{1,0:T(8,128)} %error.1, f32[4,128]{1,0:T(4,128)} %bitcast.7, s32[4,128]{1,0:T(4,128)} %bitcast.9, ...), custom_call_target="tpu_custom_call" | custom-call | tf_op jit(solution)/shard_map/pack/pallas_call | solution.py:78
  2.3 0.0 copy-start.3
  2.4 0.0 copy-start.4
  2.4 2.1 %collective-permute-start = (bf16[144,256]{1,0:T(8,128)(2,1)S(1)}, bf16[144,256]{1,0:T(8,128)(2,1)S(1)}, u32[]{:S(2)}, u32[]{:S(2)}) collective-permute-start(bf16[144,256]{1,0:T(8,128)(2,1)S(1)} %get-tuple-element.14), channel_id=1, source_target_pairs={{0,1},{1,0},{2,3},{3,2},{4,5},{5,4},{6,7},{7,6},{8,9},{9,8},{10,11... | collective-permute-start | bytes 221192 | tf_op jit(solution)/shard_map/ppermute | solution.py:232
  4.5 2.5 %collective-permute-start.1 = (bf16[144,256]{1,0:T(8,128)(2,1)S(1)}, bf16[144,256]{1,0:T(8,128)(2,1)S(1)}, u32[]{:S(2)}, u32[]{:S(2)}) collective-permute-start(bf16[144,256]{1,0:T(8,128)(2,1)S(1)} %get-tuple-element.15), channel_id=1, source_target_pairs={{0,2},{1,3},{2,0},{3,1},{4,6},{5,7},{6,4},{7,5},{8,10},{9,11},{10,... | collective-permute-start | bytes 221192 | tf_op jit(solution)/shard_map/ppermute | solution.py:232
  6.9 0.0 collective-permute-start.2
  7.0 0.0 copy-done.2
  7.0 2.6 %collective-permute-start.6 = (bf16[16,2048]{1,0:T(8,128)(2,1)S(1)}, bf16[16,2048]{1,0:T(8,128)(2,1)S(1)}, u32[]{:S(2)}, u32[]{:S(2)}) collective-permute-start(bf16[16,2048]{1,0:T(8,128)(2,1)S(1)} %copy-done.2), channel_id=1, source_target_pairs={{0,3},{1,2},{2,1},{3,0},{4,7},{5,6},{6,5},{7,4},{8,11},{9,10},{10,... | collective-permute-start | bytes 196616 | tf_op jit(solution)/shard_map/ppermute | solution.py:232
  9.6 0.0 collective-permute-start.5
  9.6 0.0 collective-permute-done.refs_1_.refs_5_
  9.6 0.6 %collective-permute-start.4 = (bf16[16,2048]{1,0:T(8,128)(2,1)S(1)}, bf16[16,2048]{1,0:T(8,128)(2,1)S(1)}, u32[]{:S(2)}, u32[]{:S(2)}) collective-permute-start(bf16[16,2048]{1,0:T(8,128)(2,1)S(1)} %copy-done.2), channel_id=1, source_target_pairs={{0,1},{1,0},{2,3},{3,2},{4,5},{5,4},{6,7},{7,6},{8,9},{9,8},{10,11... | collective-permute-start | bytes 196616 | tf_op jit(solution)/shard_map/ppermute | solution.py:232
  10.2 0.0 collective-permute-done.1.refs_2_.refs_6_
  10.2 1.6 %collective-permute-done.2.refs_3_.refs_7_ = bf16[144,256]{1,0:T(8,128)(2,1)S(1)} collective-permute-done((bf16[144,256]{1,0:T(8,128)(2,1)S(1)}, bf16[144,256]{1,0:T(8,128)(2,1)S(1)}, u32[]{:S(2)}, u32[]{:S(2)}) %collective-permute-start.2) | collective-permute-done | bytes 73760 | tf_op jit(solution)/shard_map/ppermute | solution.py:232
  11.8 0.2 total.1.mid
  12.1 2.7 %collective-permute-start.7 = (bf16[256,128]{1,0:T(8,128)(2,1)S(1)}, bf16[256,128]{1,0:T(8,128)(2,1)S(1)}, u32[]{:S(2)}, u32[]{:S(2)}) collective-permute-start(bf16[256,128]{1,0:T(8,128)(2,1)S(1)} %total.1.mid), channel_id=1, source_target_pairs={{0,4},{4,0},{1,5},{5,1},{2,6},{6,2},{3,7},{7,3},{8,12},{12,8},{9,1... | collective-permute-start | bytes 196616 | tf_op jit(solution)/shard_map/ppermute | solution.py:249
  14.8 3.0 %collective-permute-start.3 = (bf16[256,128]{1,0:T(8,128)(2,1)S(1)}, bf16[256,128]{1,0:T(8,128)(2,1)S(1)}, u32[]{:S(2)}, u32[]{:S(2)}) collective-permute-start(bf16[256,128]{1,0:T(8,128)(2,1)S(1)} %total.1.mid), channel_id=1, source_target_pairs={{4,8},{12,16},{20,24},{28,32},{36,40},{44,48},{52,56},{60,64},{68,... | collective-permute-start | bytes 196616 | tf_op jit(solution)/shard_map/ppermute | solution.py:248
  17.8 0.0 collective-permute-done.6.refs_3_
  17.8 0.0 collective-permute-done.5.refs_2_
  17.8 0.0 collective-permute-done.4.refs_1_
  17.8 0.0 collective-permute-done.7.mate
  17.8 0.0 copy-done
  17.8 0.0 copy-done.1
  17.8 2.4 %near.1.refs_10_ = f32[32,128]{1,0:T(8,128)S(1)} custom-call(s32[1]{0:T(128)} %bitcast.lev, s32[1]{0:T(128)} %bitcast.1.core, bf16[256,128]{1,0:T(8,128)(2,1)S(1)} %total.1.mid, bf16[256,128]{1,0:T(8,128)(2,1)S(1)} %collective-permute-done.7.mate, bf16[16,2048]{1,0:T(8,128)(2,1)S(1)} %copy-done.2, bf16[16,2048]{1,0:T(8,128)(2,1)S(1)} %collective-permute-done.4.refs_1_, ...), custom_call_target="tpu_custom_call" | custom-call | flops 134217728 | bytes 1048576 | tf_op jit(solution)/shard_map/near/pallas_call | solution.py:253
  20.3 0.1 collective-permute-done.3.far
  20.3 2.3 %far.1 = (f32[8,128]{1,0:T(8,128)S(1)}, f32[8,128]{1,0:T(8,128)S(1)}, f32[8,128]{1,0:T(8,128)S(1)}, f32[8,128]{1,0:T(8,128)S(1)}, f32[256,1,128]{2,1,0:T(1,128)}) custom-call(s32[1]{0:T(128)} %bitcast.lev, s32[1]{0:T(128)} %bitcast.1.core, bf16[256,128]{1,0:T(8,128)(2,1)S(1)} %collective-permute-done.3.far, bf16[16,2048]{1,0:T(8,128)(2,1)S(1)} %copy-done.2, ...), custom_call_target="tpu_custom_call" | custom-call | flops 67108864 | bytes 1048576 | tf_op jit(solution)/shard_map/far/pallas_call | solution.py:263
  22.7 13.5 %all-to-all-start = ((f32[256,1,128]{2,1,0:T(1,128)}), f32[256,1,128]{2,1,0:T(1,128)S(1)}, u32[]{:S(2)}, u32[]{:S(2)}) async-start(f32[256,1,128]{2,1,0:T(1,128)} %get-tuple-element.17), calls=%async_computation | async-start | bytes 262144 | tf_op jit(solution)/shard_map/all_to_all | solution.py:273
  36.2 1.4 %collective-permute-start.8 = (f32[8,128]{1,0:T(8,128)S(1)}, f32[8,128]{1,0:T(8,128)S(1)}, u32[]{:S(2)}, u32[]{:S(2)}) collective-permute-start(f32[8,128]{1,0:T(8,128)S(1)} %get-tuple-element.19), channel_id=1, source_target_pairs={{0,1},{1,0},{2,3},{3,2},{4,5},{5,4},{6,7},{7,6},{8,9},{9,8},{10,11... | collective-permute-start | bytes 12296 | tf_op jit(solution)/shard_map/ppermute | solution.py:232
  37.6 2.4 %collective-permute-start.9 = (f32[8,128]{1,0:T(8,128)S(1)}, f32[8,128]{1,0:T(8,128)S(1)}, u32[]{:S(2)}, u32[]{:S(2)}) collective-permute-start(f32[8,128]{1,0:T(8,128)S(1)} %get-tuple-element.20), channel_id=1, source_target_pairs={{0,2},{1,3},{2,0},{3,1},{4,6},{5,7},{6,4},{7,5},{8,10},{9,11},{10,... | collective-permute-start | bytes 12296 | tf_op jit(solution)/shard_map/ppermute | solution.py:232
  40.0 0.1 collective-permute-start.10
  40.1 0.0 collective-permute-done.8.refs_1_
  40.1 1.7 %collective-permute-done.9.refs_2_ = f32[8,128]{1,0:T(8,128)S(1)} collective-permute-done((f32[8,128]{1,0:T(8,128)S(1)}, f32[8,128]{1,0:T(8,128)S(1)}, u32[]{:S(2)}, u32[]{:S(2)}) %collective-permute-start.9) | collective-permute-done | bytes 4128 | tf_op jit(solution)/shard_map/ppermute | solution.py:232
  41.9 2.1 %collective-permute-done.10.refs_3_ = f32[8,128]{1,0:T(8,128)S(1)} collective-permute-done((f32[8,128]{1,0:T(8,128)S(1)}, f32[8,128]{1,0:T(8,128)S(1)}, u32[]{:S(2)}, u32[]{:S(2)}) %collective-permute-start.10) | collective-permute-done | bytes 4128 | tf_op jit(solution)/shard_map/ppermute | solution.py:232
  44.0 0.0 copy-done.3
  44.0 0.0 copy-done.4
  44.0 4.9 %all-to-all-done.sums = f32[256,1,128]{2,1,0:T(1,128)S(1)} async-done(((f32[256,1,128]{2,1,0:T(1,128)}), f32[256,1,128]{2,1,0:T(1,128)S(1)}, u32[]{:S(2)}, u32[]{:S(2)}) %all-to-all-start) | async-done | bytes 131104 | tf_op jit(solution)/shard_map/all_to_all | solution.py:273
  48.9 0.8 %last.1 = (f32[4,128]{1,0:T(4,128)}, f32[1,32]{1,0:T(1,128)}) custom-call(f32[256,1,128]{2,1,0:T(1,128)S(1)} %all-to-all-done.sums, f32[4,128]{1,0:T(4,128)S(1)} %finish.1.impact), custom_call_target="tpu_custom_call" | custom-call | tf_op jit(solution)/shard_map/last/pallas_call | solution.py:285
  (1 shorter events, 0.0 us)
Async XLA Ops:
  0.6 6.3 %copy-start.2 = (bf16[16,2048]{1,0:T(8,128)(2,1)S(1)}, bf16[16,2048]{1,0:T(8,128)(2,1)}, u32[]{:S(2)}) copy-start(bf16[16,2048]{1,0:T(8,128)(2,1)} %refs_0_.3) | copy-start | bytes 196612
  0.6 17.2 %copy-start = (s32[32,2048]{1,0:T(8,128)S(1)}, s32[32,2048]{1,0:T(8,128)}, u32[]{:S(2)}) copy-start(s32[32,2048]{1,0:T(8,128)} %refs_8_.1) | copy-start | bytes 786436
  0.7 17.2 %copy-start.1 = (f32[32,2048]{1,0:T(8,128)S(1)}, f32[32,2048]{1,0:T(8,128)}, u32[]{:S(2)}) copy-start(f32[32,2048]{1,0:T(8,128)} %refs_9_.1) | copy-start | bytes 786436
  2.3 41.6 %copy-start.3 = (f32[512]{0:T(512)S(1)}, f32[512]{0:T(512)}, u32[]{:S(2)}) copy-start(f32[512]{0:T(512)} %param.13) | copy-start | bytes 6148
  2.4 41.6 %copy-start.4 = (s32[512]{0:T(512)S(1)}, s32[512]{0:T(512)}, u32[]{:S(2)}) copy-start(s32[512]{0:T(512)} %param.15) | copy-start | bytes 6148
  2.4 7.2 %collective-permute-start = (bf16[144,256]{1,0:T(8,128)(2,1)S(1)}, bf16[144,256]{1,0:T(8,128)(2,1)S(1)}, u32[]{:S(2)}, u32[]{:S(2)}) collective-permute-start(bf16[144,256]{1,0:T(8,128)(2,1)S(1)} %get-tuple-element.14), channel_id=1, source_target_pairs={{0,1},{1,0},{2,3},{3,2},{4,5},{5,4},{6,7},{7,6},{8,9},{9,8},{10,11... | collective-permute-start | bytes 221192 | tf_op jit(solution)/shard_map/ppermute | solution.py:232
  4.5 5.8 %collective-permute-start.1 = (bf16[144,256]{1,0:T(8,128)(2,1)S(1)}, bf16[144,256]{1,0:T(8,128)(2,1)S(1)}, u32[]{:S(2)}, u32[]{:S(2)}) collective-permute-start(bf16[144,256]{1,0:T(8,128)(2,1)S(1)} %get-tuple-element.15), channel_id=1, source_target_pairs={{0,2},{1,3},{2,0},{3,1},{4,6},{5,7},{6,4},{7,5},{8,10},{9,11},{10,... | collective-permute-start | bytes 221192 | tf_op jit(solution)/shard_map/ppermute | solution.py:232
  6.9 4.9 %collective-permute-start.2 = (bf16[144,256]{1,0:T(8,128)(2,1)S(1)}, bf16[144,256]{1,0:T(8,128)(2,1)S(1)}, u32[]{:S(2)}, u32[]{:S(2)}) collective-permute-start(bf16[144,256]{1,0:T(8,128)(2,1)S(1)} %get-tuple-element.16), channel_id=1, source_target_pairs={{0,3},{1,2},{2,1},{3,0},{4,7},{5,6},{6,5},{7,4},{8,11},{9,10},{10,... | collective-permute-start | bytes 221192 | tf_op jit(solution)/shard_map/ppermute | solution.py:232
  7.0 10.8 %collective-permute-start.6 = (bf16[16,2048]{1,0:T(8,128)(2,1)S(1)}, bf16[16,2048]{1,0:T(8,128)(2,1)S(1)}, u32[]{:S(2)}, u32[]{:S(2)}) collective-permute-start(bf16[16,2048]{1,0:T(8,128)(2,1)S(1)} %copy-done.2), channel_id=1, source_target_pairs={{0,3},{1,2},{2,1},{3,0},{4,7},{5,6},{6,5},{7,4},{8,11},{9,10},{10,... | collective-permute-start | bytes 196616 | tf_op jit(solution)/shard_map/ppermute | solution.py:232
  9.6 8.2 %collective-permute-start.5 = (bf16[16,2048]{1,0:T(8,128)(2,1)S(1)}, bf16[16,2048]{1,0:T(8,128)(2,1)S(1)}, u32[]{:S(2)}, u32[]{:S(2)}) collective-permute-start(bf16[16,2048]{1,0:T(8,128)(2,1)S(1)} %copy-done.2), channel_id=1, source_target_pairs={{0,2},{1,3},{2,0},{3,1},{4,6},{5,7},{6,4},{7,5},{8,10},{9,11},{10,... | collective-permute-start | bytes 196616 | tf_op jit(solution)/shard_map/ppermute | solution.py:232
  9.6 8.2 %collective-permute-start.4 = (bf16[16,2048]{1,0:T(8,128)(2,1)S(1)}, bf16[16,2048]{1,0:T(8,128)(2,1)S(1)}, u32[]{:S(2)}, u32[]{:S(2)}) collective-permute-start(bf16[16,2048]{1,0:T(8,128)(2,1)S(1)} %copy-done.2), channel_id=1, source_target_pairs={{0,1},{1,0},{2,3},{3,2},{4,5},{5,4},{6,7},{7,6},{8,9},{9,8},{10,11... | collective-permute-start | bytes 196616 | tf_op jit(solution)/shard_map/ppermute | solution.py:232
  12.1 5.8 %collective-permute-start.7 = (bf16[256,128]{1,0:T(8,128)(2,1)S(1)}, bf16[256,128]{1,0:T(8,128)(2,1)S(1)}, u32[]{:S(2)}, u32[]{:S(2)}) collective-permute-start(bf16[256,128]{1,0:T(8,128)(2,1)S(1)} %total.1.mid), channel_id=1, source_target_pairs={{0,4},{4,0},{1,5},{5,1},{2,6},{6,2},{3,7},{7,3},{8,12},{12,8},{9,1... | collective-permute-start | bytes 196616 | tf_op jit(solution)/shard_map/ppermute | solution.py:249
  14.8 5.6 %collective-permute-start.3 = (bf16[256,128]{1,0:T(8,128)(2,1)S(1)}, bf16[256,128]{1,0:T(8,128)(2,1)S(1)}, u32[]{:S(2)}, u32[]{:S(2)}) collective-permute-start(bf16[256,128]{1,0:T(8,128)(2,1)S(1)} %total.1.mid), channel_id=1, source_target_pairs={{4,8},{12,16},{20,24},{28,32},{36,40},{44,48},{52,56},{60,64},{68,... | collective-permute-start | bytes 196616 | tf_op jit(solution)/shard_map/ppermute | solution.py:248
  22.7 26.2 %all-to-all-start = ((f32[256,1,128]{2,1,0:T(1,128)}), f32[256,1,128]{2,1,0:T(1,128)S(1)}, u32[]{:S(2)}, u32[]{:S(2)}) async-start(f32[256,1,128]{2,1,0:T(1,128)} %get-tuple-element.17), calls=%async_computation | async-start | bytes 262144 | tf_op jit(solution)/shard_map/all_to_all | solution.py:273
  36.2 3.9 %collective-permute-start.8 = (f32[8,128]{1,0:T(8,128)S(1)}, f32[8,128]{1,0:T(8,128)S(1)}, u32[]{:S(2)}, u32[]{:S(2)}) collective-permute-start(f32[8,128]{1,0:T(8,128)S(1)} %get-tuple-element.19), channel_id=1, source_target_pairs={{0,1},{1,0},{2,3},{3,2},{4,5},{5,4},{6,7},{7,6},{8,9},{9,8},{10,11... | collective-permute-start | bytes 12296 | tf_op jit(solution)/shard_map/ppermute | solution.py:232
  37.6 4.3 %collective-permute-start.9 = (f32[8,128]{1,0:T(8,128)S(1)}, f32[8,128]{1,0:T(8,128)S(1)}, u32[]{:S(2)}, u32[]{:S(2)}) collective-permute-start(f32[8,128]{1,0:T(8,128)S(1)} %get-tuple-element.20), channel_id=1, source_target_pairs={{0,2},{1,3},{2,0},{3,1},{4,6},{5,7},{6,4},{7,5},{8,10},{9,11},{10,... | collective-permute-start | bytes 12296 | tf_op jit(solution)/shard_map/ppermute | solution.py:232
  40.0 4.0 %collective-permute-start.10 = (f32[8,128]{1,0:T(8,128)S(1)}, f32[8,128]{1,0:T(8,128)S(1)}, u32[]{:S(2)}, u32[]{:S(2)}) collective-permute-start(f32[8,128]{1,0:T(8,128)S(1)} %get-tuple-element.21), channel_id=1, source_target_pairs={{0,3},{1,2},{2,1},{3,0},{4,7},{5,6},{6,5},{7,4},{8,11},{9,10},{10,... | collective-permute-start | bytes 12296 | tf_op jit(solution)/shard_map/ppermute | solution.py:232

commit v8 on v6

--- a/solution.py
+++ b/solution.py
@@ -117,10 +117,11 @@
     )(lev, *parts)
 
 
-def choose(rows, bits):
-    for bit in bits:
-        rows = [jnp.where(bit, rows[i + 1], rows[i]) for i in range(0, len(rows), 2)]
-    return rows[0]
+def choose(got, bits, low, depth):
+    if depth == 0:
+        return got(low)
+    upper = choose(got, bits, low + (1 << (depth - 1)), depth - 1)
+    return jnp.where(bits[depth - 1], upper, choose(got, bits, low, depth - 1))
 
 
 def fill(chunk, tables, parts, spread):
@@ -145,16 +146,14 @@
             block = idx >> 8
             value = jnp.zeros((ROWS, LANES), F32)
             for side, base in enumerate(bases):
-                got = [
-                    jnp.take_along_axis(
-                        spread[side * QUARTER + v * ROWS : side * QUARTER + (v + 1) * ROWS, lanes],
-                        row,
-                        axis=0,
-                        mode="promise_in_bounds",
+
+                def got(v):
+                    at_row = side * QUARTER + v * ROWS
+                    return jnp.take_along_axis(
+                        spread[at_row : at_row + ROWS, lanes], row, axis=0, mode="promise_in_bounds"
                     )
-                    for v in range(QUARTER // ROWS)
-                ]
-                value = jnp.where(block == base, choose(got, bits), value)
+
+                value = jnp.where(block == base, choose(got, bits, 0, len(bits)), value)
             acc += value * weight[n : n + ROWS, pl.ds(at, LANES)]
         total = jnp.sum(acc, axis=0, keepdims=True)
         tile = chunk * (QUARTER // LANES) + half
@@ -164,14 +163,12 @@
 
 def pick(bases, tables, parts, index, weight, pair, first, even, odd):
     chunks = index.shape[1] // QUARTER
+    slots = [even, odd]
     fill(0, tables, parts, even)
-
-    @pl.loop(0, chunks // 2)
-    def _(step):
-        fill(2 * step + 1, tables, parts, odd)
-        consume(2 * step, bases, even, index, weight, pair, first)
-        fill(jnp.minimum(2 * step + 2, chunks - 1), tables, parts, even)
-        consume(2 * step + 1, bases, odd, index, weight, pair, first)
+    for chunk in range(chunks):
+        if chunk + 1 < chunks:
+            fill(chunk + 1, tables, parts, slots[(chunk + 1) % 2])
+        consume(chunk, bases, slots[chunk % 2], index, weight, pair, first)
 
 
 def near_kernel(lev, core, mid, mate, *refs):

time: 49.8 us -> 49.5 us (level)
  Pallas kernels: 7.41 us -> 6.44 us
  waiting for transfers between devices: 10.5 us -> 11.1 us
    ppermute x1, waiting for transfers between devices: 0.07 us -> 0.73 us  [shards(): far = lax.ppermute(mid, COL, odd_even + [(b, a) for a, b in odd_even])]
    pallas_call x1, Pallas kernels: 2.43 us -> 1.77 us  [shards(): pl.pallas_call(near_kernel, in_specs=[SMEM, SMEM] + [VMEM] * (GROUPS + 4)...]
  transfers between devices with their start and end apart: 12 -> 12, of which waited for: 5 -> 5; matrix products, arithmetic and copies ran while one was open for 0% -> 0% of each run, Pallas kernels for 5% -> 4%
where the time goes in v8:
time: 49.5 us; the launch traced here: 49.4 us
  starting transfers between devices  31 us (63%)
  waiting for transfers between devices  11.1 us (22%)
  Pallas kernels  6.44 us (13%)
  between operations  0.78 us (2%)
    all_to_all x1, starting transfers between devices, shards(): sums = lax.all_to_all(spread, COL_LEV, 0, 0, tiled=True)  13.5 us
    ppermute x9, starting transfers between devices, to_groups(): lax.ppermute(block, 'lev', [(i, i ^ d) for i in range(GROUPS)])  11.8 us
    ppermute x9, waiting for transfers between devices, to_groups(): lax.ppermute(block, 'lev', [(i, i ^ d) for i in range(GROUPS)])  5.46 us
    all_to_all x1, waiting for transfers between devices, shards(): sums = lax.all_to_all(spread, COL_LEV, 0, 0, tiled=True)  4.92 us
    ppermute x1, starting transfers between devices, shards(): far = lax.ppermute(mid, COL, odd_even + [(b, a) for a, b in odd_even])  2.99 us
    ppermute x1, starting transfers between devices, shards(): mate = lax.ppermute(mid, 'col_2', [(0, 1), (1, 0)])  2.73 us
    pallas_call x1, Pallas kernels, shards(): pl.pallas_call(far_kernel, in_specs=[SMEM, SMEM] + [VMEM] * (2 * GROUPS +...  2 us
    pallas_call x1, Pallas kernels, shards(): pl.pallas_call(near_kernel, in_specs=[SMEM, SMEM] + [VMEM] * (GROUPS + 4)...  1.77 us
  transfers between devices with their start and end apart: 12, of which 5 were waited for; matrix products, arithmetic and copies ran while one was open for 0% of the time, Pallas kernels for 4%

profile of v8, /device:TPU:1, one launch (start us, length us, event | category | flops | bytes accessed | tf_op | source)
XLA Modules:
  0.0 49.4 jit_solution(8726123623781995014)
XLA Ops:
  0.6 0.0 copy-start.2
  0.6 0.0 copy-start
  0.7 0.0 copy-start.1
  0.7 1.7 %pack.1 = (bf16[144,256]{1,0:T(8,128)(2,1)S(1)}, bf16[144,256]{1,0:T(8,128)(2,1)S(1)}, bf16[144,256]{1,0:T(8,128)(2,1)S(1)}, bf16[144,256]{1,0:T(8,128)(2,1)S(1)}) custom-call(s32[1]{0:T(128)} %bitcast.lev, bf16[12,64,1024]{2,1,0:T(8,128)(2,1)} %state.1, f32[12,1024]{1,0:T(8,128)} %error.1, f32[4,128]{1,0:T(4,128)} %bitcast.7, s32[4,128]{1,0:T(4,128)} %bitcast.9, ...), custom_call_target="tpu_custom_call" | custom-call | tf_op jit(solution)/shard_map/pack/pallas_call | solution.py:78
  2.3 0.0 copy-start.3
  2.4 0.0 copy-start.4
  2.4 2.1 %collective-permute-start = (bf16[144,256]{1,0:T(8,128)(2,1)S(1)}, bf16[144,256]{1,0:T(8,128)(2,1)S(1)}, u32[]{:S(2)}, u32[]{:S(2)}) collective-permute-start(bf16[144,256]{1,0:T(8,128)(2,1)S(1)} %get-tuple-element.14), channel_id=1, source_target_pairs={{0,1},{1,0},{2,3},{3,2},{4,5},{5,4},{6,7},{7,6},{8,9},{9,8},{10,11... | collective-permute-start | bytes 221192 | tf_op jit(solution)/shard_map/ppermute | solution.py:228
  4.5 2.5 %collective-permute-start.1 = (bf16[144,256]{1,0:T(8,128)(2,1)S(1)}, bf16[144,256]{1,0:T(8,128)(2,1)S(1)}, u32[]{:S(2)}, u32[]{:S(2)}) collective-permute-start(bf16[144,256]{1,0:T(8,128)(2,1)S(1)} %get-tuple-element.15), channel_id=1, source_target_pairs={{0,2},{1,3},{2,0},{3,1},{4,6},{5,7},{6,4},{7,5},{8,10},{9,11},{10,... | collective-permute-start | bytes 221192 | tf_op jit(solution)/shard_map/ppermute | solution.py:228
  6.9 0.0 collective-permute-start.2
  7.0 0.0 copy-done.2
  7.0 2.6 %collective-permute-start.6 = (bf16[16,2048]{1,0:T(8,128)(2,1)S(1)}, bf16[16,2048]{1,0:T(8,128)(2,1)S(1)}, u32[]{:S(2)}, u32[]{:S(2)}) collective-permute-start(bf16[16,2048]{1,0:T(8,128)(2,1)S(1)} %copy-done.2), channel_id=1, source_target_pairs={{0,3},{1,2},{2,1},{3,0},{4,7},{5,6},{6,5},{7,4},{8,11},{9,10},{10,... | collective-permute-start | bytes 196616 | tf_op jit(solution)/shard_map/ppermute | solution.py:228
  9.6 0.0 collective-permute-start.5
  9.6 0.0 collective-permute-done.refs_1_.refs_5_
  9.6 0.6 %collective-permute-start.4 = (bf16[16,2048]{1,0:T(8,128)(2,1)S(1)}, bf16[16,2048]{1,0:T(8,128)(2,1)S(1)}, u32[]{:S(2)}, u32[]{:S(2)}) collective-permute-start(bf16[16,2048]{1,0:T(8,128)(2,1)S(1)} %copy-done.2), channel_id=1, source_target_pairs={{0,1},{1,0},{2,3},{3,2},{4,5},{5,4},{6,7},{7,6},{8,9},{9,8},{10,11... | collective-permute-start | bytes 196616 | tf_op jit(solution)/shard_map/ppermute | solution.py:228
  10.2 0.0 collective-permute-done.1.refs_2_.refs_6_
  10.2 1.6 %collective-permute-done.2.refs_3_.refs_7_ = bf16[144,256]{1,0:T(8,128)(2,1)S(1)} collective-permute-done((bf16[144,256]{1,0:T(8,128)(2,1)S(1)}, bf16[144,256]{1,0:T(8,128)(2,1)S(1)}, u32[]{:S(2)}, u32[]{:S(2)}) %collective-permute-start.2) | collective-permute-done | bytes 73760 | tf_op jit(solution)/shard_map/ppermute | solution.py:228
  11.8 0.2 total.1.mid
  12.1 2.7 %collective-permute-start.7 = (bf16[256,128]{1,0:T(8,128)(2,1)S(1)}, bf16[256,128]{1,0:T(8,128)(2,1)S(1)}, u32[]{:S(2)}, u32[]{:S(2)}) collective-permute-start(bf16[256,128]{1,0:T(8,128)(2,1)S(1)} %total.1.mid), channel_id=1, source_target_pairs={{0,4},{4,0},{1,5},{5,1},{2,6},{6,2},{3,7},{7,3},{8,12},{12,8},{9,1... | collective-permute-start | bytes 196616 | tf_op jit(solution)/shard_map/ppermute | solution.py:247
  14.8 3.0 %collective-permute-start.3 = (bf16[256,128]{1,0:T(8,128)(2,1)S(1)}, bf16[256,128]{1,0:T(8,128)(2,1)S(1)}, u32[]{:S(2)}, u32[]{:S(2)}) collective-permute-start(bf16[256,128]{1,0:T(8,128)(2,1)S(1)} %total.1.mid), channel_id=1, source_target_pairs={{4,8},{12,16},{20,24},{28,32},{36,40},{44,48},{52,56},{60,64},{68,... | collective-permute-start | bytes 196616 | tf_op jit(solution)/shard_map/ppermute | solution.py:248
  17.8 0.0 collective-permute-done.6.refs_3_
  17.8 0.0 collective-permute-done.5.refs_2_
  17.8 0.0 collective-permute-done.4.refs_1_
  17.8 0.0 collective-permute-done.7.mate
  17.8 0.0 copy-done
  17.8 0.0 copy-done.1
  17.8 1.8 %near.1.refs_10_ = f32[32,128]{1,0:T(8,128)S(1)} custom-call(s32[1]{0:T(128)} %bitcast.lev, s32[1]{0:T(128)} %bitcast.1.core, bf16[256,128]{1,0:T(8,128)(2,1)S(1)} %total.1.mid, bf16[256,128]{1,0:T(8,128)(2,1)S(1)} %collective-permute-done.7.mate, bf16[16,2048]{1,0:T(8,128)(2,1)S(1)} %copy-done.2, bf16[16,2048]{1,0:T(8,128)(2,1)S(1)} %collective-permute-done.4.refs_1_, ...), custom_call_target="tpu_custom_call" | custom-call | flops 134217728 | bytes 1048576 | tf_op jit(solution)/shard_map/near/pallas_call | solution.py:252
  19.6 0.7 %collective-permute-done.3.far = bf16[256,128]{1,0:T(8,128)(2,1)S(1)} collective-permute-done((bf16[256,128]{1,0:T(8,128)(2,1)S(1)}, bf16[256,128]{1,0:T(8,128)(2,1)S(1)}, u32[]{:S(2)}, u32[]{:S(2)}) %collective-permute-start.3) | collective-permute-done | bytes 65568 | tf_op jit(solution)/shard_map/ppermute | solution.py:248
  20.3 2.0 %far.1 = (f32[8,128]{1,0:T(8,128)S(1)}, f32[8,128]{1,0:T(8,128)S(1)}, f32[8,128]{1,0:T(8,128)S(1)}, f32[8,128]{1,0:T(8,128)S(1)}, f32[256,1,128]{2,1,0:T(1,128)}) custom-call(s32[1]{0:T(128)} %bitcast.lev, s32[1]{0:T(128)} %bitcast.1.core, bf16[256,128]{1,0:T(8,128)(2,1)S(1)} %collective-permute-done.3.far, bf16[16,2048]{1,0:T(8,128)(2,1)S(1)} %copy-done.2, ...), custom_call_target="tpu_custom_call" | custom-call | flops 67108864 | bytes 1048576 | tf_op jit(solution)/shard_map/far/pallas_call | solution.py:262
  22.3 13.5 %all-to-all-start = ((f32[256,1,128]{2,1,0:T(1,128)}), f32[256,1,128]{2,1,0:T(1,128)S(1)}, u32[]{:S(2)}, u32[]{:S(2)}) async-start(f32[256,1,128]{2,1,0:T(1,128)} %get-tuple-element.17), calls=%async_computation | async-start | bytes 262144 | tf_op jit(solution)/shard_map/all_to_all | solution.py:272
  35.8 1.4 %collective-permute-start.8 = (f32[8,128]{1,0:T(8,128)S(1)}, f32[8,128]{1,0:T(8,128)S(1)}, u32[]{:S(2)}, u32[]{:S(2)}) collective-permute-start(f32[8,128]{1,0:T(8,128)S(1)} %get-tuple-element.19), channel_id=1, source_target_pairs={{0,1},{1,0},{2,3},{3,2},{4,5},{5,4},{6,7},{7,6},{8,9},{9,8},{10,11... | collective-permute-start | bytes 12296 | tf_op jit(solution)/shard_map/ppermute | solution.py:228
  37.3 2.4 %collective-permute-start.9 = (f32[8,128]{1,0:T(8,128)S(1)}, f32[8,128]{1,0:T(8,128)S(1)}, u32[]{:S(2)}, u32[]{:S(2)}) collective-permute-start(f32[8,128]{1,0:T(8,128)S(1)} %get-tuple-element.20), channel_id=1, source_target_pairs={{0,2},{1,3},{2,0},{3,1},{4,6},{5,7},{6,4},{7,5},{8,10},{9,11},{10,... | collective-permute-start | bytes 12296 | tf_op jit(solution)/shard_map/ppermute | solution.py:228
  39.7 0.1 collective-permute-start.10
  39.8 0.0 collective-permute-done.8.refs_1_
  39.8 1.7 %collective-permute-done.9.refs_2_ = f32[8,128]{1,0:T(8,128)S(1)} collective-permute-done((f32[8,128]{1,0:T(8,128)S(1)}, f32[8,128]{1,0:T(8,128)S(1)}, u32[]{:S(2)}, u32[]{:S(2)}) %collective-permute-start.9) | collective-permute-done | bytes 4128 | tf_op jit(solution)/shard_map/ppermute | solution.py:228
  41.5 2.1 %collective-permute-done.10.refs_3_ = f32[8,128]{1,0:T(8,128)S(1)} collective-permute-done((f32[8,128]{1,0:T(8,128)S(1)}, f32[8,128]{1,0:T(8,128)S(1)}, u32[]{:S(2)}, u32[]{:S(2)}) %collective-permute-start.10) | collective-permute-done | bytes 4128 | tf_op jit(solution)/shard_map/ppermute | solution.py:228
  43.7 0.0 copy-done.3
  43.7 0.0 copy-done.4
  43.7 4.9 %all-to-all-done.sums = f32[256,1,128]{2,1,0:T(1,128)S(1)} async-done(((f32[256,1,128]{2,1,0:T(1,128)}), f32[256,1,128]{2,1,0:T(1,128)S(1)}, u32[]{:S(2)}, u32[]{:S(2)}) %all-to-all-start) | async-done | bytes 131104 | tf_op jit(solution)/shard_map/all_to_all | solution.py:272
  48.6 0.8 %last.1 = (f32[4,128]{1,0:T(4,128)}, f32[1,32]{1,0:T(1,128)}) custom-call(f32[256,1,128]{2,1,0:T(1,128)S(1)} %all-to-all-done.sums, f32[4,128]{1,0:T(4,128)S(1)} %finish.1.impact), custom_call_target="tpu_custom_call" | custom-call | tf_op jit(solution)/shard_map/last/pallas_call | solution.py:284
  (1 shorter events, 0.0 us)
Async XLA Ops:
  0.6 6.3 %copy-start.2 = (bf16[16,2048]{1,0:T(8,128)(2,1)S(1)}, bf16[16,2048]{1,0:T(8,128)(2,1)}, u32[]{:S(2)}) copy-start(bf16[16,2048]{1,0:T(8,128)(2,1)} %refs_0_.3) | copy-start | bytes 196612
  0.6 17.2 %copy-start = (s32[32,2048]{1,0:T(8,128)S(1)}, s32[32,2048]{1,0:T(8,128)}, u32[]{:S(2)}) copy-start(s32[32,2048]{1,0:T(8,128)} %refs_8_.1) | copy-start | bytes 786436
  0.7 17.2 %copy-start.1 = (f32[32,2048]{1,0:T(8,128)S(1)}, f32[32,2048]{1,0:T(8,128)}, u32[]{:S(2)}) copy-start(f32[32,2048]{1,0:T(8,128)} %refs_9_.1) | copy-start | bytes 786436
  2.3 41.3 %copy-start.3 = (f32[512]{0:T(512)S(1)}, f32[512]{0:T(512)}, u32[]{:S(2)}) copy-start(f32[512]{0:T(512)} %param.13) | copy-start | bytes 6148
  2.4 41.3 %copy-start.4 = (s32[512]{0:T(512)S(1)}, s32[512]{0:T(512)}, u32[]{:S(2)}) copy-start(s32[512]{0:T(512)} %param.15) | copy-start | bytes 6148
  2.4 7.2 %collective-permute-start = (bf16[144,256]{1,0:T(8,128)(2,1)S(1)}, bf16[144,256]{1,0:T(8,128)(2,1)S(1)}, u32[]{:S(2)}, u32[]{:S(2)}) collective-permute-start(bf16[144,256]{1,0:T(8,128)(2,1)S(1)} %get-tuple-element.14), channel_id=1, source_target_pairs={{0,1},{1,0},{2,3},{3,2},{4,5},{5,4},{6,7},{7,6},{8,9},{9,8},{10,11... | collective-permute-start | bytes 221192 | tf_op jit(solution)/shard_map/ppermute | solution.py:228
  4.5 5.8 %collective-permute-start.1 = (bf16[144,256]{1,0:T(8,128)(2,1)S(1)}, bf16[144,256]{1,0:T(8,128)(2,1)S(1)}, u32[]{:S(2)}, u32[]{:S(2)}) collective-permute-start(bf16[144,256]{1,0:T(8,128)(2,1)S(1)} %get-tuple-element.15), channel_id=1, source_target_pairs={{0,2},{1,3},{2,0},{3,1},{4,6},{5,7},{6,4},{7,5},{8,10},{9,11},{10,... | collective-permute-start | bytes 221192 | tf_op jit(solution)/shard_map/ppermute | solution.py:228
  6.9 4.9 %collective-permute-start.2 = (bf16[144,256]{1,0:T(8,128)(2,1)S(1)}, bf16[144,256]{1,0:T(8,128)(2,1)S(1)}, u32[]{:S(2)}, u32[]{:S(2)}) collective-permute-start(bf16[144,256]{1,0:T(8,128)(2,1)S(1)} %get-tuple-element.16), channel_id=1, source_target_pairs={{0,3},{1,2},{2,1},{3,0},{4,7},{5,6},{6,5},{7,4},{8,11},{9,10},{10,... | collective-permute-start | bytes 221192 | tf_op jit(solution)/shard_map/ppermute | solution.py:228
  7.0 10.8 %collective-permute-start.6 = (bf16[16,2048]{1,0:T(8,128)(2,1)S(1)}, bf16[16,2048]{1,0:T(8,128)(2,1)S(1)}, u32[]{:S(2)}, u32[]{:S(2)}) collective-permute-start(bf16[16,2048]{1,0:T(8,128)(2,1)S(1)} %copy-done.2), channel_id=1, source_target_pairs={{0,3},{1,2},{2,1},{3,0},{4,7},{5,6},{6,5},{7,4},{8,11},{9,10},{10,... | collective-permute-start | bytes 196616 | tf_op jit(solution)/shard_map/ppermute | solution.py:228
  9.6 8.2 %collective-permute-start.5 = (bf16[16,2048]{1,0:T(8,128)(2,1)S(1)}, bf16[16,2048]{1,0:T(8,128)(2,1)S(1)}, u32[]{:S(2)}, u32[]{:S(2)}) collective-permute-start(bf16[16,2048]{1,0:T(8,128)(2,1)S(1)} %copy-done.2), channel_id=1, source_target_pairs={{0,2},{1,3},{2,0},{3,1},{4,6},{5,7},{6,4},{7,5},{8,10},{9,11},{10,... | collective-permute-start | bytes 196616 | tf_op jit(solution)/shard_map/ppermute | solution.py:228
  9.6 8.2 %collective-permute-start.4 = (bf16[16,2048]{1,0:T(8,128)(2,1)S(1)}, bf16[16,2048]{1,0:T(8,128)(2,1)S(1)}, u32[]{:S(2)}, u32[]{:S(2)}) collective-permute-start(bf16[16,2048]{1,0:T(8,128)(2,1)S(1)} %copy-done.2), channel_id=1, source_target_pairs={{0,1},{1,0},{2,3},{3,2},{4,5},{5,4},{6,7},{7,6},{8,9},{9,8},{10,11... | collective-permute-start | bytes 196616 | tf_op jit(solution)/shard_map/ppermute | solution.py:228
  12.1 5.8 %collective-permute-start.7 = (bf16[256,128]{1,0:T(8,128)(2,1)S(1)}, bf16[256,128]{1,0:T(8,128)(2,1)S(1)}, u32[]{:S(2)}, u32[]{:S(2)}) collective-permute-start(bf16[256,128]{1,0:T(8,128)(2,1)S(1)} %total.1.mid), channel_id=1, source_target_pairs={{0,4},{4,0},{1,5},{5,1},{2,6},{6,2},{3,7},{7,3},{8,12},{12,8},{9,1... | collective-permute-start | bytes 196616 | tf_op jit(solution)/shard_map/ppermute | solution.py:247
  14.8 5.6 %collective-permute-start.3 = (bf16[256,128]{1,0:T(8,128)(2,1)S(1)}, bf16[256,128]{1,0:T(8,128)(2,1)S(1)}, u32[]{:S(2)}, u32[]{:S(2)}) collective-permute-start(bf16[256,128]{1,0:T(8,128)(2,1)S(1)} %total.1.mid), channel_id=1, source_target_pairs={{4,8},{12,16},{20,24},{28,32},{36,40},{44,48},{52,56},{60,64},{68,... | collective-permute-start | bytes 196616 | tf_op jit(solution)/shard_map/ppermute | solution.py:248
  22.3 26.2 %all-to-all-start = ((f32[256,1,128]{2,1,0:T(1,128)}), f32[256,1,128]{2,1,0:T(1,128)S(1)}, u32[]{:S(2)}, u32[]{:S(2)}) async-start(f32[256,1,128]{2,1,0:T(1,128)} %get-tuple-element.17), calls=%async_computation | async-start | bytes 262144 | tf_op jit(solution)/shard_map/all_to_all | solution.py:272
  35.8 3.9 %collective-permute-start.8 = (f32[8,128]{1,0:T(8,128)S(1)}, f32[8,128]{1,0:T(8,128)S(1)}, u32[]{:S(2)}, u32[]{:S(2)}) collective-permute-start(f32[8,128]{1,0:T(8,128)S(1)} %get-tuple-element.19), channel_id=1, source_target_pairs={{0,1},{1,0},{2,3},{3,2},{4,5},{5,4},{6,7},{7,6},{8,9},{9,8},{10,11... | collective-permute-start | bytes 12296 | tf_op jit(solution)/shard_map/ppermute | solution.py:228
  37.3 4.3 %collective-permute-start.9 = (f32[8,128]{1,0:T(8,128)S(1)}, f32[8,128]{1,0:T(8,128)S(1)}, u32[]{:S(2)}, u32[]{:S(2)}) collective-permute-start(f32[8,128]{1,0:T(8,128)S(1)} %get-tuple-element.20), channel_id=1, source_target_pairs={{0,2},{1,3},{2,0},{3,1},{4,6},{5,7},{6,4},{7,5},{8,10},{9,11},{10,... | collective-permute-start | bytes 12296 | tf_op jit(solution)/shard_map/ppermute | solution.py:228
  39.7 4.0 %collective-permute-start.10 = (f32[8,128]{1,0:T(8,128)S(1)}, f32[8,128]{1,0:T(8,128)S(1)}, u32[]{:S(2)}, u32[]{:S(2)}) collective-permute-start(f32[8,128]{1,0:T(8,128)S(1)} %get-tuple-element.21), channel_id=1, source_target_pairs={{0,3},{1,2},{2,1},{3,0},{4,7},{5,6},{6,5},{7,4},{8,11},{9,10},{10,... | collective-permute-start | bytes 12296 | tf_op jit(solution)/shard_map/ppermute | solution.py:228

commit v9 on v8

--- a/solution.py
+++ b/solution.py
@@ -171,12 +171,15 @@
         consume(chunk, bases, slots[chunk % 2], index, weight, pair, first)
 
 
-def near_kernel(lev, core, mid, mate, *refs):
+def mid_kernel(lev, core, mid, *refs):
     parts, (index, weight, out, even, odd) = refs[:GROUPS], refs[GROUPS:]
-    group = lev[0]
+    pick((GROUPS + lev[0],), (mid,), parts, index, weight, out, None, even, odd)
+
+
+def mate_kernel(lev, core, mate, *refs):
+    parts, (index, weight, first, out, even, odd) = refs[:GROUPS], refs[GROUPS:]
     side = jnp.where(core[0] == 0, 2, 0)
-    bases = (GROUPS + group, side * GROUPS + group)
-    pick(bases, (mid, mate), parts, index, weight, out, None, even, odd)
+    pick((side * GROUPS + lev[0],), (mate,), parts, index, weight, out, first, even, odd)
 
 
 def far_kernel(lev, core, far, *refs):
@@ -218,7 +221,7 @@
     impact_out[...] = impact[...]
 
 
-def shards(state_anom, error_sum, obs_anom, local_weight, neighbours, innovation, obs_type, live):
+def steps(state_anom, error_sum, obs_anom, local_weight, neighbours, innovation, obs_type, live):
     lines = innovation.shape[0] // LANES
     lev = lax.axis_index("lev").reshape(1)
     core = lax.axis_index("col_2").reshape(1)
@@ -244,20 +247,23 @@
     mid = total_sens(lev, parts)
     pairs = lax.axis_size(COL) // CORES
     odd_even = [(CORES * i + 1, CORES * i + 2) for i in range(pairs - 1)]
+    far = lax.ppermute(mid, COL, odd_even + [(b, a) for a, b in odd_even])
     mate = lax.ppermute(mid, "col_2", [(0, 1), (1, 0)])
-    far = lax.ppermute(mid, COL, odd_even + [(b, a) for a, b in odd_even])
     index, weight = near(neighbours), near(local_weight)
     lists = GROUPS * ROWS
     cost = functools.partial(pl.CostEstimate, bytes_accessed=1 << 20, transcendentals=0)
-    first = pl.pallas_call(
-        near_kernel,
-        in_specs=[SMEM, SMEM] + [VMEM] * (GROUPS + 4),
+    rows = dict(
         out_specs=VMEM,
         out_shape=pltpu.VMEM((lists, LANES), F32),
-        scratch_shapes=[pltpu.VMEM((2 * QUARTER, QUARTER), F32)] * 2,
-        cost_estimate=cost(flops=1 << 27),
-        name="near",
-    )(lev, core, near(mid), near(mate), *anoms, index, weight)
+        scratch_shapes=[pltpu.VMEM((QUARTER, QUARTER), F32)] * 2,
+        cost_estimate=cost(flops=1 << 26),
+    )
+    own = pl.pallas_call(
+        mid_kernel, in_specs=[SMEM, SMEM] + [VMEM] * (GROUPS + 3), name="mid", **rows
+    )(lev, core, near(mid), *anoms, index, weight)
+    first = pl.pallas_call(
+        mate_kernel, in_specs=[SMEM, SMEM] + [VMEM] * (GROUPS + 4), name="mate", **rows
+    )(lev, core, near(mate), *anoms, index, weight, near(own))
     everyone = lax.axis_size(COL_LEV)
     *shares, spread = pl.pallas_call(
         far_kernel,
@@ -299,7 +305,7 @@
         mesh.devices.reshape(4, 8, 2, mesh.shape["lev"]), ("col_0", "col_1", "col_2", "lev")
     )
     return jax.shard_map(
-        shards,
+        steps,
         mesh=split,
         in_specs=(
             P("lev", None, COL),

time: 49.5 us -> 49.5 us (level)
  waiting for transfers between devices: 11.1 us -> 10.6 us
    pallas_call x4 -> x5, Pallas kernels: 4.56 us -> 4.97 us  [the longest x1 1.96 us: steps(): pl.pallas_call(far_kernel, in_specs=[SMEM, SMEM] + [VMEM] * (2 * GROUPS +...]
  transfers between devices with their start and end apart: 12 -> 12, of which waited for: 5 -> 5; matrix products, arithmetic and copies ran while one was open for 0% -> 0% of each run, Pallas kernels for 4% -> 5%
where the time goes in v9:
time: 49.5 us; the launch traced here: 49.3 us
  starting transfers between devices  31 us (63%)
  waiting for transfers between devices  10.6 us (21%)
  Pallas kernels  6.85 us (14%)
  between operations  0.78 us (2%)
    all_to_all x1, starting transfers between devices, steps(): sums = lax.all_to_all(spread, COL_LEV, 0, 0, tiled=True)  13.5 us
    ppermute x9, starting transfers between devices, to_groups(): lax.ppermute(block, 'lev', [(i, i ^ d) for i in range(GROUPS)])  11.8 us
    ppermute x9, waiting for transfers between devices, to_groups(): lax.ppermute(block, 'lev', [(i, i ^ d) for i in range(GROUPS)])  5.46 us
    all_to_all x1, waiting for transfers between devices, steps(): sums = lax.all_to_all(spread, COL_LEV, 0, 0, tiled=True)  4.92 us
    ppermute x1, starting transfers between devices, steps(): far = lax.ppermute(mid, COL, odd_even + [(b, a) for a, b in odd_even])  3 us
    ppermute x1, starting transfers between devices, steps(): mate = lax.ppermute(mid, 'col_2', [(0, 1), (1, 0)])  2.72 us
    pallas_call x1, Pallas kernels, steps(): pl.pallas_call(far_kernel, in_specs=[SMEM, SMEM] + [VMEM] * (2 * GROUPS +...  1.96 us
    pallas_call x1, Pallas kernels, pack(): pl.pallas_call(pack_kernel, in_specs=[SMEM] + [ANY] * 5, out_specs=[VMEM]...  1.67 us
  transfers between devices with their start and end apart: 12, of which 5 were waited for; matrix products, arithmetic and copies ran while one was open for 0% of the time, Pallas kernels for 5%

profile of v9, /device:TPU:1, one launch (start us, length us, event | category | flops | bytes accessed | tf_op | source)
XLA Modules:
  0.0 49.3 jit_solution(2733789157970843153)
XLA Ops:
  0.6 0.0 copy-start.2
  0.6 0.0 copy-start
  0.7 0.0 copy-start.1
  0.7 1.7 %pack.1 = (bf16[144,256]{1,0:T(8,128)(2,1)S(1)}, bf16[144,256]{1,0:T(8,128)(2,1)S(1)}, bf16[144,256]{1,0:T(8,128)(2,1)S(1)}, bf16[144,256]{1,0:T(8,128)(2,1)S(1)}) custom-call(s32[1]{0:T(128)} %bitcast.lev, bf16[12,64,1024]{2,1,0:T(8,128)(2,1)} %state.1, f32[12,1024]{1,0:T(8,128)} %error.1, f32[4,128]{1,0:T(4,128)} %bitcast.7, s32[4,128]{1,0:T(4,128)} %bitcast.9, ...), custom_call_target="tpu_custom_call" | custom-call | tf_op jit(solution)/shard_map/pack/pallas_call | solution.py:78
  2.3 2.1 %collective-permute-start = (bf16[144,256]{1,0:T(8,128)(2,1)S(1)}, bf16[144,256]{1,0:T(8,128)(2,1)S(1)}, u32[]{:S(2)}, u32[]{:S(2)}) collective-permute-start(bf16[144,256]{1,0:T(8,128)(2,1)S(1)} %get-tuple-element.14), channel_id=1, source_target_pairs={{0,1},{1,0},{2,3},{3,2},{4,5},{5,4},{6,7},{7,6},{8,9},{9,8},{10,11... | collective-permute-start | bytes 221192 | tf_op jit(solution)/shard_map/ppermute | solution.py:231
  4.5 2.5 %collective-permute-start.1 = (bf16[144,256]{1,0:T(8,128)(2,1)S(1)}, bf16[144,256]{1,0:T(8,128)(2,1)S(1)}, u32[]{:S(2)}, u32[]{:S(2)}) collective-permute-start(bf16[144,256]{1,0:T(8,128)(2,1)S(1)} %get-tuple-element.15), channel_id=1, source_target_pairs={{0,2},{1,3},{2,0},{3,1},{4,6},{5,7},{6,4},{7,5},{8,10},{9,11},{10,... | collective-permute-start | bytes 221192 | tf_op jit(solution)/shard_map/ppermute | solution.py:231
  6.9 0.0 collective-permute-start.2
  7.0 0.0 copy-done.2
  7.0 2.6 %collective-permute-start.6 = (bf16[16,2048]{1,0:T(8,128)(2,1)S(1)}, bf16[16,2048]{1,0:T(8,128)(2,1)S(1)}, u32[]{:S(2)}, u32[]{:S(2)}) collective-permute-start(bf16[16,2048]{1,0:T(8,128)(2,1)S(1)} %copy-done.2), channel_id=1, source_target_pairs={{0,3},{1,2},{2,1},{3,0},{4,7},{5,6},{6,5},{7,4},{8,11},{9,10},{10,... | collective-permute-start | bytes 196616 | tf_op jit(solution)/shard_map/ppermute | solution.py:231
  9.6 0.0 collective-permute-start.5
  9.6 0.0 collective-permute-done.refs_1_.refs_5_
  9.6 0.6 %collective-permute-start.4 = (bf16[16,2048]{1,0:T(8,128)(2,1)S(1)}, bf16[16,2048]{1,0:T(8,128)(2,1)S(1)}, u32[]{:S(2)}, u32[]{:S(2)}) collective-permute-start(bf16[16,2048]{1,0:T(8,128)(2,1)S(1)} %copy-done.2), channel_id=1, source_target_pairs={{0,1},{1,0},{2,3},{3,2},{4,5},{5,4},{6,7},{7,6},{8,9},{9,8},{10,11... | collective-permute-start | bytes 196616 | tf_op jit(solution)/shard_map/ppermute | solution.py:231
  10.2 0.0 collective-permute-done.1.refs_2_.refs_6_
  10.2 1.6 %collective-permute-done.2.refs_3_.refs_7_ = bf16[144,256]{1,0:T(8,128)(2,1)S(1)} collective-permute-done((bf16[144,256]{1,0:T(8,128)(2,1)S(1)}, bf16[144,256]{1,0:T(8,128)(2,1)S(1)}, u32[]{:S(2)}, u32[]{:S(2)}) %collective-permute-start.2) | collective-permute-done | bytes 73760 | tf_op jit(solution)/shard_map/ppermute | solution.py:231
  11.8 0.2 total.1.mid
  12.0 2.7 %collective-permute-start.7 = (bf16[256,128]{1,0:T(8,128)(2,1)S(1)}, bf16[256,128]{1,0:T(8,128)(2,1)S(1)}, u32[]{:S(2)}, u32[]{:S(2)}) collective-permute-start(bf16[256,128]{1,0:T(8,128)(2,1)S(1)} %total.1.mid), channel_id=1, source_target_pairs={{0,4},{4,0},{1,5},{5,1},{2,6},{6,2},{3,7},{7,3},{8,12},{12,8},{9,1... | collective-permute-start | bytes 196616 | tf_op jit(solution)/shard_map/ppermute | solution.py:251
  14.7 3.0 %collective-permute-start.3 = (bf16[256,128]{1,0:T(8,128)(2,1)S(1)}, bf16[256,128]{1,0:T(8,128)(2,1)S(1)}, u32[]{:S(2)}, u32[]{:S(2)}) collective-permute-start(bf16[256,128]{1,0:T(8,128)(2,1)S(1)} %total.1.mid), channel_id=1, source_target_pairs={{4,8},{12,16},{20,24},{28,32},{36,40},{44,48},{52,56},{60,64},{68,... | collective-permute-start | bytes 196616 | tf_op jit(solution)/shard_map/ppermute | solution.py:250
  17.8 0.0 collective-permute-done.6.refs_3_
  17.8 0.0 collective-permute-done.5.refs_2_
  17.8 0.0 collective-permute-done.4.refs_1_
  17.8 0.0 copy-done
  17.8 0.0 copy-done.1
  17.8 0.0 copy-start.3
  17.8 0.0 copy-start.4
  17.8 1.1 %mid.1.refs_6_ = f32[32,128]{1,0:T(8,128)S(1)} custom-call(s32[1]{0:T(128)} %bitcast.lev, s32[1]{0:T(128)} %bitcast.1.core, bf16[256,128]{1,0:T(8,128)(2,1)S(1)} %total.1.mid, bf16[16,2048]{1,0:T(8,128)(2,1)S(1)} %copy-done.2, bf16[16,2048]{1,0:T(8,128)(2,1)S(1)} %collective-permute-done.4.refs_1_, bf16[16,2048]{1,0:T(8,128)(2,1)S(1)} %collective-permute-done.5.refs_2_, ...), custom_call_target="tpu_custom_call" | custom-call | flops 67108864 | bytes 1048576 | tf_op jit(solution)/shard_map/mid/pallas_call | solution.py:261
  18.9 0.0 collective-permute-done.7.mate
  19.0 1.1 %mate.1.refs_10_ = f32[32,128]{1,0:T(8,128)S(1)} custom-call(s32[1]{0:T(128)} %bitcast.lev, s32[1]{0:T(128)} %bitcast.1.core, bf16[256,128]{1,0:T(8,128)(2,1)S(1)} %collective-permute-done.7.mate, bf16[16,2048]{1,0:T(8,128)(2,1)S(1)} %copy-done.2, bf16[16,2048]{1,0:T(8,128)(2,1)S(1)} %collective-permute-done.4.refs_1_, ...), custom_call_target="tpu_custom_call" | custom-call | flops 67108864 | bytes 1048576 | tf_op jit(solution)/shard_map/mate/pallas_call | solution.py:264
  20.1 0.2 collective-permute-done.3.far
  20.3 2.0 %far.1 = (f32[8,128]{1,0:T(8,128)S(1)}, f32[8,128]{1,0:T(8,128)S(1)}, f32[8,128]{1,0:T(8,128)S(1)}, f32[8,128]{1,0:T(8,128)S(1)}, f32[256,1,128]{2,1,0:T(1,128)}) custom-call(s32[1]{0:T(128)} %bitcast.lev, s32[1]{0:T(128)} %bitcast.1.core, bf16[256,128]{1,0:T(8,128)(2,1)S(1)} %collective-permute-done.3.far, bf16[16,2048]{1,0:T(8,128)(2,1)S(1)} %copy-done.2, ...), custom_call_target="tpu_custom_call" | custom-call | flops 67108864 | bytes 1048576 | tf_op jit(solution)/shard_map/far/pallas_call | solution.py:268
  22.3 13.5 %all-to-all-start = ((f32[256,1,128]{2,1,0:T(1,128)}), f32[256,1,128]{2,1,0:T(1,128)S(1)}, u32[]{:S(2)}, u32[]{:S(2)}) async-start(f32[256,1,128]{2,1,0:T(1,128)} %get-tuple-element.17), calls=%async_computation | async-start | bytes 262144 | tf_op jit(solution)/shard_map/all_to_all | solution.py:278
  35.8 1.4 %collective-permute-start.8 = (f32[8,128]{1,0:T(8,128)S(1)}, f32[8,128]{1,0:T(8,128)S(1)}, u32[]{:S(2)}, u32[]{:S(2)}) collective-permute-start(f32[8,128]{1,0:T(8,128)S(1)} %get-tuple-element.19), channel_id=1, source_target_pairs={{0,1},{1,0},{2,3},{3,2},{4,5},{5,4},{6,7},{7,6},{8,9},{9,8},{10,11... | collective-permute-start | bytes 12296 | tf_op jit(solution)/shard_map/ppermute | solution.py:231
  37.2 2.4 %collective-permute-start.9 = (f32[8,128]{1,0:T(8,128)S(1)}, f32[8,128]{1,0:T(8,128)S(1)}, u32[]{:S(2)}, u32[]{:S(2)}) collective-permute-start(f32[8,128]{1,0:T(8,128)S(1)} %get-tuple-element.20), channel_id=1, source_target_pairs={{0,2},{1,3},{2,0},{3,1},{4,6},{5,7},{6,4},{7,5},{8,10},{9,11},{10,... | collective-permute-start | bytes 12296 | tf_op jit(solution)/shard_map/ppermute | solution.py:231
  39.6 0.1 collective-permute-start.10
  39.7 0.0 collective-permute-done.8.refs_1_
  39.7 1.7 %collective-permute-done.9.refs_2_ = f32[8,128]{1,0:T(8,128)S(1)} collective-permute-done((f32[8,128]{1,0:T(8,128)S(1)}, f32[8,128]{1,0:T(8,128)S(1)}, u32[]{:S(2)}, u32[]{:S(2)}) %collective-permute-start.9) | collective-permute-done | bytes 4128 | tf_op jit(solution)/shard_map/ppermute | solution.py:231
  41.5 2.1 %collective-permute-done.10.refs_3_ = f32[8,128]{1,0:T(8,128)S(1)} collective-permute-done((f32[8,128]{1,0:T(8,128)S(1)}, f32[8,128]{1,0:T(8,128)S(1)}, u32[]{:S(2)}, u32[]{:S(2)}) %collective-permute-start.10) | collective-permute-done | bytes 4128 | tf_op jit(solution)/shard_map/ppermute | solution.py:231
  43.6 0.0 copy-done.3
  43.6 0.0 copy-done.4
  43.6 4.9 %all-to-all-done.sums = f32[256,1,128]{2,1,0:T(1,128)S(1)} async-done(((f32[256,1,128]{2,1,0:T(1,128)}), f32[256,1,128]{2,1,0:T(1,128)S(1)}, u32[]{:S(2)}, u32[]{:S(2)}) %all-to-all-start) | async-done | bytes 131104 | tf_op jit(solution)/shard_map/all_to_all | solution.py:278
  48.5 0.8 %last.1 = (f32[4,128]{1,0:T(4,128)}, f32[1,32]{1,0:T(1,128)}) custom-call(f32[256,1,128]{2,1,0:T(1,128)S(1)} %all-to-all-done.sums, f32[4,128]{1,0:T(4,128)S(1)} %finish.1.impact), custom_call_target="tpu_custom_call" | custom-call | tf_op jit(solution)/shard_map/last/pallas_call | solution.py:290
  (1 shorter events, 0.0 us)
Async XLA Ops:
  0.6 6.3 %copy-start.2 = (bf16[16,2048]{1,0:T(8,128)(2,1)S(1)}, bf16[16,2048]{1,0:T(8,128)(2,1)}, u32[]{:S(2)}) copy-start(bf16[16,2048]{1,0:T(8,128)(2,1)} %refs_0_.5) | copy-start | bytes 196612
  0.6 17.1 %copy-start = (s32[32,2048]{1,0:T(8,128)S(1)}, s32[32,2048]{1,0:T(8,128)}, u32[]{:S(2)}) copy-start(s32[32,2048]{1,0:T(8,128)} %refs_8_.1) | copy-start | bytes 786436
  0.7 17.1 %copy-start.1 = (f32[32,2048]{1,0:T(8,128)S(1)}, f32[32,2048]{1,0:T(8,128)}, u32[]{:S(2)}) copy-start(f32[32,2048]{1,0:T(8,128)} %refs_9_.1) | copy-start | bytes 786436
  2.3 7.3 %collective-permute-start = (bf16[144,256]{1,0:T(8,128)(2,1)S(1)}, bf16[144,256]{1,0:T(8,128)(2,1)S(1)}, u32[]{:S(2)}, u32[]{:S(2)}) collective-permute-start(bf16[144,256]{1,0:T(8,128)(2,1)S(1)} %get-tuple-element.14), channel_id=1, source_target_pairs={{0,1},{1,0},{2,3},{3,2},{4,5},{5,4},{6,7},{7,6},{8,9},{9,8},{10,11... | collective-permute-start | bytes 221192 | tf_op jit(solution)/shard_map/ppermute | solution.py:231
  4.5 5.8 %collective-permute-start.1 = (bf16[144,256]{1,0:T(8,128)(2,1)S(1)}, bf16[144,256]{1,0:T(8,128)(2,1)S(1)}, u32[]{:S(2)}, u32[]{:S(2)}) collective-permute-start(bf16[144,256]{1,0:T(8,128)(2,1)S(1)} %get-tuple-element.15), channel_id=1, source_target_pairs={{0,2},{1,3},{2,0},{3,1},{4,6},{5,7},{6,4},{7,5},{8,10},{9,11},{10,... | collective-permute-start | bytes 221192 | tf_op jit(solution)/shard_map/ppermute | solution.py:231
  6.9 4.9 %collective-permute-start.2 = (bf16[144,256]{1,0:T(8,128)(2,1)S(1)}, bf16[144,256]{1,0:T(8,128)(2,1)S(1)}, u32[]{:S(2)}, u32[]{:S(2)}) collective-permute-start(bf16[144,256]{1,0:T(8,128)(2,1)S(1)} %get-tuple-element.16), channel_id=1, source_target_pairs={{0,3},{1,2},{2,1},{3,0},{4,7},{5,6},{6,5},{7,4},{8,11},{9,10},{10,... | collective-permute-start | bytes 221192 | tf_op jit(solution)/shard_map/ppermute | solution.py:231
  7.0 10.8 %collective-permute-start.6 = (bf16[16,2048]{1,0:T(8,128)(2,1)S(1)}, bf16[16,2048]{1,0:T(8,128)(2,1)S(1)}, u32[]{:S(2)}, u32[]{:S(2)}) collective-permute-start(bf16[16,2048]{1,0:T(8,128)(2,1)S(1)} %copy-done.2), channel_id=1, source_target_pairs={{0,3},{1,2},{2,1},{3,0},{4,7},{5,6},{6,5},{7,4},{8,11},{9,10},{10,... | collective-permute-start | bytes 196616 | tf_op jit(solution)/shard_map/ppermute | solution.py:231
  9.6 8.2 %collective-permute-start.5 = (bf16[16,2048]{1,0:T(8,128)(2,1)S(1)}, bf16[16,2048]{1,0:T(8,128)(2,1)S(1)}, u32[]{:S(2)}, u32[]{:S(2)}) collective-permute-start(bf16[16,2048]{1,0:T(8,128)(2,1)S(1)} %copy-done.2), channel_id=1, source_target_pairs={{0,2},{1,3},{2,0},{3,1},{4,6},{5,7},{6,4},{7,5},{8,10},{9,11},{10,... | collective-permute-start | bytes 196616 | tf_op jit(solution)/shard_map/ppermute | solution.py:231
  9.6 8.2 %collective-permute-start.4 = (bf16[16,2048]{1,0:T(8,128)(2,1)S(1)}, bf16[16,2048]{1,0:T(8,128)(2,1)S(1)}, u32[]{:S(2)}, u32[]{:S(2)}) collective-permute-start(bf16[16,2048]{1,0:T(8,128)(2,1)S(1)} %copy-done.2), channel_id=1, source_target_pairs={{0,1},{1,0},{2,3},{3,2},{4,5},{5,4},{6,7},{7,6},{8,9},{9,8},{10,11... | collective-permute-start | bytes 196616 | tf_op jit(solution)/shard_map/ppermute | solution.py:231
  12.0 6.9 %collective-permute-start.7 = (bf16[256,128]{1,0:T(8,128)(2,1)S(1)}, bf16[256,128]{1,0:T(8,128)(2,1)S(1)}, u32[]{:S(2)}, u32[]{:S(2)}) collective-permute-start(bf16[256,128]{1,0:T(8,128)(2,1)S(1)} %total.1.mid), channel_id=1, source_target_pairs={{0,4},{4,0},{1,5},{5,1},{2,6},{6,2},{3,7},{7,3},{8,12},{12,8},{9,1... | collective-permute-start | bytes 196616 | tf_op jit(solution)/shard_map/ppermute | solution.py:251
  14.7 5.6 %collective-permute-start.3 = (bf16[256,128]{1,0:T(8,128)(2,1)S(1)}, bf16[256,128]{1,0:T(8,128)(2,1)S(1)}, u32[]{:S(2)}, u32[]{:S(2)}) collective-permute-start(bf16[256,128]{1,0:T(8,128)(2,1)S(1)} %total.1.mid), channel_id=1, source_target_pairs={{4,8},{12,16},{20,24},{28,32},{36,40},{44,48},{52,56},{60,64},{68,... | collective-permute-start | bytes 196616 | tf_op jit(solution)/shard_map/ppermute | solution.py:250
  17.8 25.8 %copy-start.3 = (f32[512]{0:T(512)S(1)}, f32[512]{0:T(512)}, u32[]{:S(2)}) copy-start(f32[512]{0:T(512)} %param.13) | copy-start | bytes 6148
  17.8 25.8 %copy-start.4 = (s32[512]{0:T(512)S(1)}, s32[512]{0:T(512)}, u32[]{:S(2)}) copy-start(s32[512]{0:T(512)} %param.15) | copy-start | bytes 6148
  22.3 26.3 %all-to-all-start = ((f32[256,1,128]{2,1,0:T(1,128)}), f32[256,1,128]{2,1,0:T(1,128)S(1)}, u32[]{:S(2)}, u32[]{:S(2)}) async-start(f32[256,1,128]{2,1,0:T(1,128)} %get-tuple-element.17), calls=%async_computation | async-start | bytes 262144 | tf_op jit(solution)/shard_map/all_to_all | solution.py:278
  35.8 3.9 %collective-permute-start.8 = (f32[8,128]{1,0:T(8,128)S(1)}, f32[8,128]{1,0:T(8,128)S(1)}, u32[]{:S(2)}, u32[]{:S(2)}) collective-permute-start(f32[8,128]{1,0:T(8,128)S(1)} %get-tuple-element.19), channel_id=1, source_target_pairs={{0,1},{1,0},{2,3},{3,2},{4,5},{5,4},{6,7},{7,6},{8,9},{9,8},{10,11... | collective-permute-start | bytes 12296 | tf_op jit(solution)/shard_map/ppermute | solution.py:231
  37.2 4.3 %collective-permute-start.9 = (f32[8,128]{1,0:T(8,128)S(1)}, f32[8,128]{1,0:T(8,128)S(1)}, u32[]{:S(2)}, u32[]{:S(2)}) collective-permute-start(f32[8,128]{1,0:T(8,128)S(1)} %get-tuple-element.20), channel_id=1, source_target_pairs={{0,2},{1,3},{2,0},{3,1},{4,6},{5,7},{6,4},{7,5},{8,10},{9,11},{10,... | collective-permute-start | bytes 12296 | tf_op jit(solution)/shard_map/ppermute | solution.py:231
  39.6 4.0 %collective-permute-start.10 = (f32[8,128]{1,0:T(8,128)S(1)}, f32[8,128]{1,0:T(8,128)S(1)}, u32[]{:S(2)}, u32[]{:S(2)}) collective-permute-start(f32[8,128]{1,0:T(8,128)S(1)} %get-tuple-element.21), channel_id=1, source_target_pairs={{0,3},{1,2},{2,1},{3,0},{4,7},{5,6},{6,5},{7,4},{8,11},{9,10},{10,... | collective-permute-start | bytes 12296 | tf_op jit(solution)/shard_map/ppermute | solution.py:231

commit v10 on v9

--- a/solution.py
+++ b/solution.py
@@ -22,6 +22,8 @@
 VMEM = pl.BlockSpec(memory_space=pltpu.VMEM)
 SMEM = pl.BlockSpec(memory_space=pltpu.SMEM)
 ANY = pl.BlockSpec(memory_space=pl.ANY)
+FEWER_SPILLS = pltpu.CompilerParams(
+)
 
 
 def near(x):
@@ -216,7 +218,7 @@
 
 
 def last_kernel(sums, impact, impact_out, type_out):
-    total = jnp.sum(sums[...], axis=0)
+    total = jnp.sum(jnp.sum(sums[...], axis=0), axis=0, keepdims=True)
     type_out[...] = total[:, 0:NTYPE]
     impact_out[...] = impact[...]
 
@@ -227,12 +229,10 @@
     core = lax.axis_index("col_2").reshape(1)
 
     def to_groups(blocks):
-        got = [
-            lax.ppermute(block, "lev", [(i, i ^ d) for i in range(GROUPS)])
-            for d, block in enumerate(blocks)
-            if d > 0
-        ]
-        return [near(block) for block in [blocks[0]] + got]
+        got = [blocks[0]]
+        for d in range(1, GROUPS):
+            got.append(lax.ppermute(blocks[d], "lev", [(i, i ^ d) for i in range(GROUPS)]))
+        return [near(block) for block in got]
 
     send = pack(
         lev,
@@ -257,6 +257,7 @@
         out_shape=pltpu.VMEM((lists, LANES), F32),
         scratch_shapes=[pltpu.VMEM((QUARTER, QUARTER), F32)] * 2,
         cost_estimate=cost(flops=1 << 26),
+        compiler_params=FEWER_SPILLS,
     )
     own = pl.pallas_call(
         mid_kernel, in_specs=[SMEM, SMEM] + [VMEM] * (GROUPS + 3), name="mid", **rows
@@ -270,12 +271,14 @@
         in_specs=[SMEM, SMEM] + [VMEM] * (2 * GROUPS + 4),
         out_specs=[VMEM] * (GROUPS + 1),
         out_shape=[pltpu.VMEM((ROWS, LANES), F32)] * GROUPS
-        + [jax.ShapeDtypeStruct((everyone, 1, LANES), F32)],
+        + [jax.ShapeDtypeStruct((everyone // ROWS, ROWS, LANES), F32)],
         scratch_shapes=[pltpu.VMEM((QUARTER, QUARTER), F32)] * 2 + [pltpu.VMEM((lists, LANES), F32)],
         cost_estimate=cost(flops=1 << 26),
+        compiler_params=FEWER_SPILLS,
         name="far",
     )(lev, core, near(far), *anoms, *parts, index, weight, near(first))
-    sums = lax.all_to_all(spread, COL_LEV, 0, 0, tiled=True)
+    sums = lax.all_to_all(spread.reshape(everyone, 1, LANES), COL_LEV, 0, 0, tiled=True)
+    sums = sums.reshape(everyone // ROWS, ROWS, LANES)
     impact = pl.pallas_call(
         finish_kernel,
         in_specs=[VMEM] * (GROUPS + 2),

time: 49.5 us -> 49.2 us (level)
  no operation moved by 1% of the time
where the time goes in v10:
time: 49.2 us; the launch traced here: 49.1 us
  starting transfers between devices  31 us (63%)
  waiting for transfers between devices  10.6 us (22%)
  Pallas kernels  6.6 us (13%)
  between operations  0.78 us (2%)
    all_to_all x1, starting transfers between devices, steps(): lax.all_to_all(spread.reshape(everyone, 1, LANES), COL_LEV, 0, 0, tiled=T...  13.5 us
    ppermute x9, starting transfers between devices, to_groups(): lax.ppermute(blocks[d], 'lev', [(i, i ^ d) for i in range(GROUPS)])  11.8 us
    ppermute x9, waiting for transfers between devices, to_groups(): lax.ppermute(blocks[d], 'lev', [(i, i ^ d) for i in range(GROUPS)])  5.46 us
    all_to_all x1, waiting for transfers between devices, steps(): lax.all_to_all(spread.reshape(everyone, 1, LANES), COL_LEV, 0, 0, tiled=T...  4.92 us
    ppermute x1, starting transfers between devices, steps(): far = lax.ppermute(mid, COL, odd_even + [(b, a) for a, b in odd_even])  3 us
    ppermute x1, starting transfers between devices, steps(): mate = lax.ppermute(mid, 'col_2', [(0, 1), (1, 0)])  2.72 us
    pallas_call x1, Pallas kernels, steps(): pl.pallas_call(far_kernel, in_specs=[SMEM, SMEM] + [VMEM] * (2 * GROUPS +...  1.9 us
    pallas_call x1, Pallas kernels, pack(): pl.pallas_call(pack_kernel, in_specs=[SMEM] + [ANY] * 5, out_specs=[VMEM]...  1.67 us
  transfers between devices with their start and end apart: 12, of which 5 were waited for; matrix products, arithmetic and copies ran while one was open for 0% of the time, Pallas kernels for 5%

profile of v10, /device:TPU:1, one launch (start us, length us, event | category | flops | bytes accessed | tf_op | source)
XLA Modules:
  0.0 49.1 jit_solution(11554293036927076917)
XLA Ops:
  0.6 0.0 copy-start.2
  0.6 0.0 copy-start
  0.7 0.0 copy-start.1
  0.7 1.7 %pack.1 = (bf16[144,256]{1,0:T(8,128)(2,1)S(1)}, bf16[144,256]{1,0:T(8,128)(2,1)S(1)}, bf16[144,256]{1,0:T(8,128)(2,1)S(1)}, bf16[144,256]{1,0:T(8,128)(2,1)S(1)}) custom-call(s32[1]{0:T(128)} %bitcast.lev, bf16[12,64,1024]{2,1,0:T(8,128)(2,1)} %state.1, f32[12,1024]{1,0:T(8,128)} %error.1, f32[4,128]{1,0:T(4,128)} %bitcast.12, s32[4,128]{1,0:T(4,128)} %bitcast.14, ...), custom_call_target="tpu_custom_call" | custom-call | tf_op jit(solution)/shard_map/pack/pallas_call | solution.py:80
  2.3 2.1 %collective-permute-start = (bf16[144,256]{1,0:T(8,128)(2,1)S(1)}, bf16[144,256]{1,0:T(8,128)(2,1)S(1)}, u32[]{:S(2)}, u32[]{:S(2)}) collective-permute-start(bf16[144,256]{1,0:T(8,128)(2,1)S(1)} %get-tuple-element.14), channel_id=1, source_target_pairs={{0,1},{1,0},{2,3},{3,2},{4,5},{5,4},{6,7},{7,6},{8,9},{9,8},{10,11... | collective-permute-start | bytes 221192 | tf_op jit(solution)/shard_map/ppermute | solution.py:234
  4.5 2.5 %collective-permute-start.1 = (bf16[144,256]{1,0:T(8,128)(2,1)S(1)}, bf16[144,256]{1,0:T(8,128)(2,1)S(1)}, u32[]{:S(2)}, u32[]{:S(2)}) collective-permute-start(bf16[144,256]{1,0:T(8,128)(2,1)S(1)} %get-tuple-element.15), channel_id=1, source_target_pairs={{0,2},{1,3},{2,0},{3,1},{4,6},{5,7},{6,4},{7,5},{8,10},{9,11},{10,... | collective-permute-start | bytes 221192 | tf_op jit(solution)/shard_map/ppermute | solution.py:234
  6.9 0.0 collective-permute-start.2
  7.0 0.0 copy-done.2
  7.0 2.6 %collective-permute-start.6 = (bf16[16,2048]{1,0:T(8,128)(2,1)S(1)}, bf16[16,2048]{1,0:T(8,128)(2,1)S(1)}, u32[]{:S(2)}, u32[]{:S(2)}) collective-permute-start(bf16[16,2048]{1,0:T(8,128)(2,1)S(1)} %copy-done.2), channel_id=1, source_target_pairs={{0,3},{1,2},{2,1},{3,0},{4,7},{5,6},{6,5},{7,4},{8,11},{9,10},{10,... | collective-permute-start | bytes 196616 | tf_op jit(solution)/shard_map/ppermute | solution.py:234
  9.6 0.0 collective-permute-start.5
  9.6 0.0 collective-permute-done.refs_1_.refs_5_
  9.6 0.6 %collective-permute-start.4 = (bf16[16,2048]{1,0:T(8,128)(2,1)S(1)}, bf16[16,2048]{1,0:T(8,128)(2,1)S(1)}, u32[]{:S(2)}, u32[]{:S(2)}) collective-permute-start(bf16[16,2048]{1,0:T(8,128)(2,1)S(1)} %copy-done.2), channel_id=1, source_target_pairs={{0,1},{1,0},{2,3},{3,2},{4,5},{5,4},{6,7},{7,6},{8,9},{9,8},{10,11... | collective-permute-start | bytes 196616 | tf_op jit(solution)/shard_map/ppermute | solution.py:234
  10.2 0.0 collective-permute-done.1.refs_2_.refs_6_
  10.2 1.6 %collective-permute-done.2.refs_3_.refs_7_ = bf16[144,256]{1,0:T(8,128)(2,1)S(1)} collective-permute-done((bf16[144,256]{1,0:T(8,128)(2,1)S(1)}, bf16[144,256]{1,0:T(8,128)(2,1)S(1)}, u32[]{:S(2)}, u32[]{:S(2)}) %collective-permute-start.2) | collective-permute-done | bytes 73760 | tf_op jit(solution)/shard_map/ppermute | solution.py:234
  11.8 0.2 total.1.mid
  12.0 2.7 %collective-permute-start.7 = (bf16[256,128]{1,0:T(8,128)(2,1)S(1)}, bf16[256,128]{1,0:T(8,128)(2,1)S(1)}, u32[]{:S(2)}, u32[]{:S(2)}) collective-permute-start(bf16[256,128]{1,0:T(8,128)(2,1)S(1)} %total.1.mid), channel_id=1, source_target_pairs={{0,4},{4,0},{1,5},{5,1},{2,6},{6,2},{3,7},{7,3},{8,12},{12,8},{9,1... | collective-permute-start | bytes 196616 | tf_op jit(solution)/shard_map/ppermute | solution.py:251
  14.7 3.0 %collective-permute-start.3 = (bf16[256,128]{1,0:T(8,128)(2,1)S(1)}, bf16[256,128]{1,0:T(8,128)(2,1)S(1)}, u32[]{:S(2)}, u32[]{:S(2)}) collective-permute-start(bf16[256,128]{1,0:T(8,128)(2,1)S(1)} %total.1.mid), channel_id=1, source_target_pairs={{4,8},{12,16},{20,24},{28,32},{36,40},{44,48},{52,56},{60,64},{68,... | collective-permute-start | bytes 196616 | tf_op jit(solution)/shard_map/ppermute | solution.py:250
  17.8 0.0 collective-permute-done.6.refs_3_
  17.8 0.0 collective-permute-done.5.refs_2_
  17.8 0.0 collective-permute-done.4.refs_1_
  17.8 0.0 copy-done
  17.8 0.0 copy-done.1
  17.8 0.0 copy-start.3
  17.8 0.0 copy-start.4
  17.8 1.1 %mid.1.refs_6_ = f32[32,128]{1,0:T(8,128)S(1)} custom-call(s32[1]{0:T(128)} %bitcast.lev, s32[1]{0:T(128)} %bitcast.1.core, bf16[256,128]{1,0:T(8,128)(2,1)S(1)} %total.1.mid, bf16[16,2048]{1,0:T(8,128)(2,1)S(1)} %copy-done.2, bf16[16,2048]{1,0:T(8,128)(2,1)S(1)} %collective-permute-done.4.refs_1_, bf16[16,2048]{1,0:T(8,128)(2,1)S(1)} %collective-permute-done.5.refs_2_, ...), custom_call_target="tpu_custom_call" | custom-call | flops 67108864 | bytes 1048576 | tf_op jit(solution)/shard_map/mid/pallas_call | solution.py:262
  18.9 0.0 collective-permute-done.7.mate
  19.0 1.1 %mate.1.refs_10_ = f32[32,128]{1,0:T(8,128)S(1)} custom-call(s32[1]{0:T(128)} %bitcast.lev, s32[1]{0:T(128)} %bitcast.1.core, bf16[256,128]{1,0:T(8,128)(2,1)S(1)} %collective-permute-done.7.mate, bf16[16,2048]{1,0:T(8,128)(2,1)S(1)} %copy-done.2, bf16[16,2048]{1,0:T(8,128)(2,1)S(1)} %collective-permute-done.4.refs_1_, ...), custom_call_target="tpu_custom_call" | custom-call | flops 67108864 | bytes 1048576 | tf_op jit(solution)/shard_map/mate/pallas_call | solution.py:265
  20.1 0.2 collective-permute-done.3.far
  20.3 1.9 %far.1 = (f32[8,128]{1,0:T(8,128)S(1)}, f32[8,128]{1,0:T(8,128)S(1)}, f32[8,128]{1,0:T(8,128)S(1)}, f32[8,128]{1,0:T(8,128)S(1)}, f32[32,8,128]{2,1,0:T(8,128)}) custom-call(s32[1]{0:T(128)} %bitcast.lev, s32[1]{0:T(128)} %bitcast.1.core, bf16[256,128]{1,0:T(8,128)(2,1)S(1)} %collective-permute-done.3.far, bf16[16,2048]{1,0:T(8,128)(2,1)S(1)} %copy-done.2, ...), custom_call_target="tpu_custom_call" | custom-call | flops 67108864 | bytes 1048576 | tf_op jit(solution)/shard_map/far/pallas_call | solution.py:269
  22.2 13.5 %all-to-all-start = ((f32[256,1,128]{2,1,0:T(1,128)}), f32[256,1,128]{2,1,0:T(1,128)S(1)}, u32[]{:S(2)}, u32[]{:S(2)}) async-start(f32[256,1,128]{2,1,0:T(1,128)} %bitcast.16), calls=%async_computation | async-start | bytes 262144 | tf_op jit(solution)/shard_map/all_to_all | solution.py:280
  35.7 1.4 %collective-permute-start.8 = (f32[8,128]{1,0:T(8,128)S(1)}, f32[8,128]{1,0:T(8,128)S(1)}, u32[]{:S(2)}, u32[]{:S(2)}) collective-permute-start(f32[8,128]{1,0:T(8,128)S(1)} %get-tuple-element.19), channel_id=1, source_target_pairs={{0,1},{1,0},{2,3},{3,2},{4,5},{5,4},{6,7},{7,6},{8,9},{9,8},{10,11... | collective-permute-start | bytes 12296 | tf_op jit(solution)/shard_map/ppermute | solution.py:234
  37.2 2.4 %collective-permute-start.9 = (f32[8,128]{1,0:T(8,128)S(1)}, f32[8,128]{1,0:T(8,128)S(1)}, u32[]{:S(2)}, u32[]{:S(2)}) collective-permute-start(f32[8,128]{1,0:T(8,128)S(1)} %get-tuple-element.20), channel_id=1, source_target_pairs={{0,2},{1,3},{2,0},{3,1},{4,6},{5,7},{6,4},{7,5},{8,10},{9,11},{10,... | collective-permute-start | bytes 12296 | tf_op jit(solution)/shard_map/ppermute | solution.py:234
  39.6 0.1 collective-permute-start.10
  39.7 0.0 collective-permute-done.8.refs_1_
  39.7 1.7 %collective-permute-done.9.refs_2_ = f32[8,128]{1,0:T(8,128)S(1)} collective-permute-done((f32[8,128]{1,0:T(8,128)S(1)}, f32[8,128]{1,0:T(8,128)S(1)}, u32[]{:S(2)}, u32[]{:S(2)}) %collective-permute-start.9) | collective-permute-done | bytes 4128 | tf_op jit(solution)/shard_map/ppermute | solution.py:234
  41.4 2.1 %collective-permute-done.10.refs_3_ = f32[8,128]{1,0:T(8,128)S(1)} collective-permute-done((f32[8,128]{1,0:T(8,128)S(1)}, f32[8,128]{1,0:T(8,128)S(1)}, u32[]{:S(2)}, u32[]{:S(2)}) %collective-permute-start.10) | collective-permute-done | bytes 4128 | tf_op jit(solution)/shard_map/ppermute | solution.py:234
  43.5 0.0 copy-done.3
  43.5 0.0 copy-done.4
  43.6 4.9 %all-to-all-done = f32[256,1,128]{2,1,0:T(1,128)S(1)} async-done(((f32[256,1,128]{2,1,0:T(1,128)}), f32[256,1,128]{2,1,0:T(1,128)S(1)}, u32[]{:S(2)}, u32[]{:S(2)}) %all-to-all-start) | async-done | bytes 131104 | tf_op jit(solution)/shard_map/all_to_all | solution.py:280
  48.5 0.6 %last.1 = (f32[4,128]{1,0:T(4,128)}, f32[1,32]{1,0:T(1,128)}) custom-call(f32[32,8,128]{2,1,0:T(8,128)S(1)} %bitcast.11, f32[4,128]{1,0:T(4,128)S(1)} %finish.1.impact), custom_call_target="tpu_custom_call" | custom-call | tf_op jit(solution)/shard_map/last/pallas_call | solution.py:293
  (1 shorter events, 0.0 us)
Async XLA Ops:
  0.6 6.3 %copy-start.2 = (bf16[16,2048]{1,0:T(8,128)(2,1)S(1)}, bf16[16,2048]{1,0:T(8,128)(2,1)}, u32[]{:S(2)}) copy-start(bf16[16,2048]{1,0:T(8,128)(2,1)} %refs_0_.5) | copy-start | bytes 196612
  0.6 17.1 %copy-start = (s32[32,2048]{1,0:T(8,128)S(1)}, s32[32,2048]{1,0:T(8,128)}, u32[]{:S(2)}) copy-start(s32[32,2048]{1,0:T(8,128)} %refs_8_.1) | copy-start | bytes 786436
  0.7 17.1 %copy-start.1 = (f32[32,2048]{1,0:T(8,128)S(1)}, f32[32,2048]{1,0:T(8,128)}, u32[]{:S(2)}) copy-start(f32[32,2048]{1,0:T(8,128)} %refs_9_.1) | copy-start | bytes 786436
  2.3 7.3 %collective-permute-start = (bf16[144,256]{1,0:T(8,128)(2,1)S(1)}, bf16[144,256]{1,0:T(8,128)(2,1)S(1)}, u32[]{:S(2)}, u32[]{:S(2)}) collective-permute-start(bf16[144,256]{1,0:T(8,128)(2,1)S(1)} %get-tuple-element.14), channel_id=1, source_target_pairs={{0,1},{1,0},{2,3},{3,2},{4,5},{5,4},{6,7},{7,6},{8,9},{9,8},{10,11... | collective-permute-start | bytes 221192 | tf_op jit(solution)/shard_map/ppermute | solution.py:234
  4.5 5.8 %collective-permute-start.1 = (bf16[144,256]{1,0:T(8,128)(2,1)S(1)}, bf16[144,256]{1,0:T(8,128)(2,1)S(1)}, u32[]{:S(2)}, u32[]{:S(2)}) collective-permute-start(bf16[144,256]{1,0:T(8,128)(2,1)S(1)} %get-tuple-element.15), channel_id=1, source_target_pairs={{0,2},{1,3},{2,0},{3,1},{4,6},{5,7},{6,4},{7,5},{8,10},{9,11},{10,... | collective-permute-start | bytes 221192 | tf_op jit(solution)/shard_map/ppermute | solution.py:234
  6.9 4.9 %collective-permute-start.2 = (bf16[144,256]{1,0:T(8,128)(2,1)S(1)}, bf16[144,256]{1,0:T(8,128)(2,1)S(1)}, u32[]{:S(2)}, u32[]{:S(2)}) collective-permute-start(bf16[144,256]{1,0:T(8,128)(2,1)S(1)} %get-tuple-element.16), channel_id=1, source_target_pairs={{0,3},{1,2},{2,1},{3,0},{4,7},{5,6},{6,5},{7,4},{8,11},{9,10},{10,... | collective-permute-start | bytes 221192 | tf_op jit(solution)/shard_map/ppermute | solution.py:234
  7.0 10.8 %collective-permute-start.6 = (bf16[16,2048]{1,0:T(8,128)(2,1)S(1)}, bf16[16,2048]{1,0:T(8,128)(2,1)S(1)}, u32[]{:S(2)}, u32[]{:S(2)}) collective-permute-start(bf16[16,2048]{1,0:T(8,128)(2,1)S(1)} %copy-done.2), channel_id=1, source_target_pairs={{0,3},{1,2},{2,1},{3,0},{4,7},{5,6},{6,5},{7,4},{8,11},{9,10},{10,... | collective-permute-start | bytes 196616 | tf_op jit(solution)/shard_map/ppermute | solution.py:234
  9.6 8.2 %collective-permute-start.5 = (bf16[16,2048]{1,0:T(8,128)(2,1)S(1)}, bf16[16,2048]{1,0:T(8,128)(2,1)S(1)}, u32[]{:S(2)}, u32[]{:S(2)}) collective-permute-start(bf16[16,2048]{1,0:T(8,128)(2,1)S(1)} %copy-done.2), channel_id=1, source_target_pairs={{0,2},{1,3},{2,0},{3,1},{4,6},{5,7},{6,4},{7,5},{8,10},{9,11},{10,... | collective-permute-start | bytes 196616 | tf_op jit(solution)/shard_map/ppermute | solution.py:234
  9.6 8.2 %collective-permute-start.4 = (bf16[16,2048]{1,0:T(8,128)(2,1)S(1)}, bf16[16,2048]{1,0:T(8,128)(2,1)S(1)}, u32[]{:S(2)}, u32[]{:S(2)}) collective-permute-start(bf16[16,2048]{1,0:T(8,128)(2,1)S(1)} %copy-done.2), channel_id=1, source_target_pairs={{0,1},{1,0},{2,3},{3,2},{4,5},{5,4},{6,7},{7,6},{8,9},{9,8},{10,11... | collective-permute-start | bytes 196616 | tf_op jit(solution)/shard_map/ppermute | solution.py:234
  12.0 6.9 %collective-permute-start.7 = (bf16[256,128]{1,0:T(8,128)(2,1)S(1)}, bf16[256,128]{1,0:T(8,128)(2,1)S(1)}, u32[]{:S(2)}, u32[]{:S(2)}) collective-permute-start(bf16[256,128]{1,0:T(8,128)(2,1)S(1)} %total.1.mid), channel_id=1, source_target_pairs={{0,4},{4,0},{1,5},{5,1},{2,6},{6,2},{3,7},{7,3},{8,12},{12,8},{9,1... | collective-permute-start | bytes 196616 | tf_op jit(solution)/shard_map/ppermute | solution.py:251
  14.7 5.6 %collective-permute-start.3 = (bf16[256,128]{1,0:T(8,128)(2,1)S(1)}, bf16[256,128]{1,0:T(8,128)(2,1)S(1)}, u32[]{:S(2)}, u32[]{:S(2)}) collective-permute-start(bf16[256,128]{1,0:T(8,128)(2,1)S(1)} %total.1.mid), channel_id=1, source_target_pairs={{4,8},{12,16},{20,24},{28,32},{36,40},{44,48},{52,56},{60,64},{68,... | collective-permute-start | bytes 196616 | tf_op jit(solution)/shard_map/ppermute | solution.py:250
  17.8 25.7 %copy-start.3 = (f32[512]{0:T(512)S(1)}, f32[512]{0:T(512)}, u32[]{:S(2)}) copy-start(f32[512]{0:T(512)} %param.13) | copy-start | bytes 6148
  17.8 25.7 %copy-start.4 = (s32[512]{0:T(512)S(1)}, s32[512]{0:T(512)}, u32[]{:S(2)}) copy-start(s32[512]{0:T(512)} %param.15) | copy-start | bytes 6148
  22.2 26.3 %all-to-all-start = ((f32[256,1,128]{2,1,0:T(1,128)}), f32[256,1,128]{2,1,0:T(1,128)S(1)}, u32[]{:S(2)}, u32[]{:S(2)}) async-start(f32[256,1,128]{2,1,0:T(1,128)} %bitcast.16), calls=%async_computation | async-start | bytes 262144 | tf_op jit(solution)/shard_map/all_to_all | solution.py:280
  35.7 3.9 %collective-permute-start.8 = (f32[8,128]{1,0:T(8,128)S(1)}, f32[8,128]{1,0:T(8,128)S(1)}, u32[]{:S(2)}, u32[]{:S(2)}) collective-permute-start(f32[8,128]{1,0:T(8,128)S(1)} %get-tuple-element.19), channel_id=1, source_target_pairs={{0,1},{1,0},{2,3},{3,2},{4,5},{5,4},{6,7},{7,6},{8,9},{9,8},{10,11... | collective-permute-start | bytes 12296 | tf_op jit(solution)/shard_map/ppermute | solution.py:234
  37.2 4.3 %collective-permute-start.9 = (f32[8,128]{1,0:T(8,128)S(1)}, f32[8,128]{1,0:T(8,128)S(1)}, u32[]{:S(2)}, u32[]{:S(2)}) collective-permute-start(f32[8,128]{1,0:T(8,128)S(1)} %get-tuple-element.20), channel_id=1, source_target_pairs={{0,2},{1,3},{2,0},{3,1},{4,6},{5,7},{6,4},{7,5},{8,10},{9,11},{10,... | collective-permute-start | bytes 12296 | tf_op jit(solution)/shard_map/ppermute | solution.py:234
  39.6 4.0 %collective-permute-start.10 = (f32[8,128]{1,0:T(8,128)S(1)}, f32[8,128]{1,0:T(8,128)S(1)}, u32[]{:S(2)}, u32[]{:S(2)}) collective-permute-start(f32[8,128]{1,0:T(8,128)S(1)} %get-tuple-element.21), channel_id=1, source_target_pairs={{0,3},{1,2},{2,1},{3,0},{4,7},{5,6},{6,5},{7,4},{8,11},{9,10},{10,... | collective-permute-start | bytes 12296 | tf_op jit(solution)/shard_map/ppermute | solution.py:234
